TPU v7x, 16 devices: a whole 2x2x2 slice. The times are simulated.
16 devices in a mesh: dp: 2 (over z), sp: 8 (over y, x, core).
Axes of the slice: x: 2, y: 2, z: 2, core: 2. Of those that a mesh axis runs over, the one named last changes fastest.
Arguments:
- x_in: bfloat16 [16, 1024, 2048], P('dp', 'sp'), parts along dimension 0
- grad_y: bfloat16 [16, 1024, 2048], P('dp', 'sp'), parts along dimension 0
- positions: int32 [16, 1024], P('dp', 'sp'), parts along dimension 0
- g_norm: bfloat16 [2048], replicated
- w_query: bfloat16 [2048, 2048], replicated
- w_key: bfloat16 [2048, 2048], replicated
- w_value: bfloat16 [2048, 2048], replicated
- w_out: bfloat16 [2048, 2048], replicated
- g_query: bfloat16 [2048], replicated
- g_key: bfloat16 [2048], replicated
Outputs:
- output 1: bfloat16 [16, 1024, 2048], P('dp', 'sp'), parts along dimension 0
- output 2: bfloat16 [16, 1024, 2048], P('dp', 'sp'), parts along dimension 0
- output 3: float32 [4096], P(('dp', 'sp')), parts along dimension 0
- output 4: float32 [4096, 2048], P(('dp', 'sp')), parts along dimension 0
- output 5: float32 [4096, 2048], P(('dp', 'sp')), parts along dimension 0
- output 6: float32 [4096, 2048], P(('dp', 'sp')), parts along dimension 0
- output 7: float32 [4096, 2048], P(('dp', 'sp')), parts along dimension 0
- output 8: float32 [4096], P(('dp', 'sp')), parts along dimension 0
- output 9: float32 [4096], P(('dp', 'sp')), parts along dimension 0
There are 2 independent parts. A program takes and returns all parts, laid end to end along the dimension named above; an argument that names none is the same for every part.
All inputs are finite; a program needn't handle non-finite values.
Results may differ from a plain program's by a relative error of at most 0.0114602.
Values are sent between devices in bfloat16 or wider.
A program may use at most 1 GiB of HBM per device.

v0:
```python
import functools
import jax
import jax.numpy as jnp
from jax import lax
from jax.sharding import PartitionSpec as P

HEAD_DIM = 128
QUERY_BLOCK = 128
NORM_EPS = 1e-5
ROPE_BASE = 10000.0
NEG_BIG = -1e30


def rope_tables(positions):
    half_dim = HEAD_DIM // 2
    inv_freq = ROPE_BASE ** (-jnp.arange(half_dim, dtype=jnp.float32) * (2.0 / HEAD_DIM))
    angles = positions.astype(jnp.float32)[..., None] * inv_freq
    return jnp.cos(angles)[:, :, None, :], jnp.sin(angles)[:, :, None, :]


def rope_apply(values, cos_t, sin_t):
    half_dim = values.shape[-1] // 2
    first_half = values[..., :half_dim]
    second_half = values[..., half_dim:]
    return jnp.concatenate([first_half * cos_t - second_half * sin_t, second_half * cos_t + first_half * sin_t], axis=-1)


def rope_revert(grads_in, cos_t, sin_t):
    half_dim = grads_in.shape[-1] // 2
    first_half = grads_in[..., :half_dim]
    second_half = grads_in[..., half_dim:]
    return jnp.concatenate([first_half * cos_t + second_half * sin_t, second_half * cos_t - first_half * sin_t], axis=-1)


def rms_forward(values, gain_vec):
    inv_rms = lax.rsqrt(jnp.mean(values * values, axis=-1, keepdims=True) + NORM_EPS)
    normed = values * inv_rms
    return normed * gain_vec.astype(jnp.float32), normed, inv_rms


def rms_backward(d_out, normed, inv_rms, gain_vec):
    d_normed = d_out * gain_vec.astype(jnp.float32)
    d_in = inv_rms * (d_normed - normed * jnp.mean(d_normed * normed, axis=-1, keepdims=True))
    return d_in, d_out * normed


def project(values, weight):
    return jnp.einsum('bsd,de->bse', values, weight, preferred_element_type=jnp.float32)


def project_back(grads_in, weight):
    return jnp.einsum('bse,de->bsd', grads_in, weight, preferred_element_type=jnp.float32)


def weight_grad(values, grads_in):
    return jnp.einsum('bsd,bse->de', values, grads_in, preferred_element_type=jnp.float32)


def block_front(x_in, positions, g_norm, w_query, w_key, w_value, g_query, g_key):
    n_batch, seq_len, d_model = x_in.shape
    head_shape = (n_batch, seq_len, d_model // HEAD_DIM, HEAD_DIM)
    cos_t, sin_t = rope_tables(positions)
    x_f = x_in.astype(jnp.float32)
    hid_f, x_hat, x_inv = rms_forward(x_f, g_norm)
    hidden = hid_f.astype(jnp.bfloat16)
    q_nrm, q_hat, q_inv = rms_forward(project(hidden, w_query), g_query)
    k_nrm, k_hat, k_inv = rms_forward(project(hidden, w_key), g_key)
    q_rot = rope_apply(q_nrm.reshape(head_shape), cos_t, sin_t).astype(jnp.bfloat16)
    k_rot = rope_apply(k_nrm.reshape(head_shape), cos_t, sin_t).astype(jnp.bfloat16)
    v_val = project(hidden, w_value).astype(jnp.bfloat16).reshape(head_shape)
    saved_fwd = (x_f, x_hat, x_inv, hidden, q_hat, q_inv, k_hat, k_inv, cos_t, sin_t)
    return q_rot, k_rot, v_val, saved_fwd


def block_back(saved_fwd, d_q, d_k, d_v, grad_y, g_norm, w_query, w_key, w_value, g_query, g_key):
    x_f, x_hat, x_inv, hidden, q_hat, q_inv, k_hat, k_inv, cos_t, sin_t = saved_fwd
    flat_shape = hidden.shape
    dq_rot = rope_revert(d_q.astype(jnp.float32), cos_t, sin_t).reshape(flat_shape)
    dk_rot = rope_revert(d_k.astype(jnp.float32), cos_t, sin_t).reshape(flat_shape)
    dq_raw, q_terms = rms_backward(dq_rot, q_hat, q_inv, g_query)
    dk_raw, k_terms = rms_backward(dk_rot, k_hat, k_inv, g_key)
    dq_bf = dq_raw.astype(jnp.bfloat16)
    dk_bf = dk_raw.astype(jnp.bfloat16)
    dv_bf = d_v.reshape(flat_shape)
    d_hidden = project_back(dq_bf, w_query) + project_back(dk_bf, w_key) + project_back(dv_bf, w_value)
    dx_norm, n_terms = rms_backward(d_hidden, x_hat, x_inv, g_norm)
    grad_x = (grad_y.astype(jnp.float32) + dx_norm).astype(jnp.bfloat16)
    return grad_x, (dq_bf, dk_bf, dv_bf), (n_terms, q_terms, k_terms)


def attend_forward(q_all, k_all, v_all, q_offset):
    q_len = q_all.shape[1]
    key_pos = jnp.arange(k_all.shape[1])
    blk_len = min(QUERY_BLOCK, q_len)
    qk_scale = q_all.shape[-1] ** -0.5

    def block_step(blk_idx, loop_state):
        out_buf, lse_buf = loop_state
        q_start = blk_idx * blk_len
        q_blk = lax.dynamic_slice_in_dim(q_all, q_start, blk_len, axis=1)
        scores = jnp.einsum('bqhd,bkhd->bhqk', q_blk, k_all, preferred_element_type=jnp.float32) * qk_scale
        q_pos = q_offset + q_start + jnp.arange(blk_len)
        scores = jnp.where(q_pos[:, None] >= key_pos[None, :], scores, NEG_BIG)
        row_max = jnp.max(scores, axis=-1, keepdims=True)
        exp_scores = jnp.exp(scores - row_max)
        row_sum = jnp.sum(exp_scores, axis=-1, keepdims=True)
        prob_bf = (exp_scores / row_sum).astype(jnp.bfloat16)
        out_blk = jnp.einsum('bhqk,bkhd->bqhd', prob_bf, v_all, preferred_element_type=jnp.float32)
        lse_blk = (row_max + jnp.log(row_sum))[..., 0]
        out_buf = lax.dynamic_update_slice_in_dim(out_buf, out_blk.astype(jnp.bfloat16), q_start, axis=1)
        lse_buf = lax.dynamic_update_slice_in_dim(lse_buf, lse_blk, q_start, axis=2)
        return out_buf, lse_buf

    init_state = (jnp.zeros(q_all.shape, jnp.bfloat16), jnp.zeros((q_all.shape[0], q_all.shape[2], q_len), jnp.float32))
    return lax.fori_loop(0, q_len // blk_len, block_step, init_state)


def attend_backward(q_all, k_all, v_all, lse_all, dout_all, q_offset):
    q_len = q_all.shape[1]
    key_pos = jnp.arange(k_all.shape[1])
    blk_len = min(QUERY_BLOCK, q_len)
    qk_scale = q_all.shape[-1] ** -0.5

    def block_step(blk_idx, loop_state):
        dq_buf, dk_acc, dv_acc = loop_state
        q_start = blk_idx * blk_len
        q_blk = lax.dynamic_slice_in_dim(q_all, q_start, blk_len, axis=1)
        do_blk = lax.dynamic_slice_in_dim(dout_all, q_start, blk_len, axis=1)
        lse_blk = lax.dynamic_slice_in_dim(lse_all, q_start, blk_len, axis=2)
        scores = jnp.einsum('bqhd,bkhd->bhqk', q_blk, k_all, preferred_element_type=jnp.float32) * qk_scale
        q_pos = q_offset + q_start + jnp.arange(blk_len)
        scores = jnp.where(q_pos[:, None] >= key_pos[None, :], scores, NEG_BIG)
        prob_f = jnp.exp(scores - lse_blk[..., None])
        d_prob = jnp.einsum('bqhd,bkhd->bhqk', do_blk, v_all, preferred_element_type=jnp.float32)
        row_dot = jnp.sum(prob_f * d_prob, axis=-1, keepdims=True)
        ds_bf = (prob_f * (d_prob - row_dot) * qk_scale).astype(jnp.bfloat16)
        prob_bf = prob_f.astype(jnp.bfloat16)
        dv_acc = dv_acc + jnp.einsum('bhqk,bqhd->bkhd', prob_bf, do_blk, preferred_element_type=jnp.float32)
        dk_acc = dk_acc + jnp.einsum('bhqk,bqhd->bkhd', ds_bf, q_blk, preferred_element_type=jnp.float32)
        dq_blk = jnp.einsum('bhqk,bkhd->bqhd', ds_bf, k_all, preferred_element_type=jnp.float32)
        dq_buf = lax.dynamic_update_slice_in_dim(dq_buf, dq_blk.astype(jnp.bfloat16), q_start, axis=1)
        return dq_buf, dk_acc, dv_acc

    init_state = (jnp.zeros(q_all.shape, jnp.bfloat16), jnp.zeros(k_all.shape, jnp.float32), jnp.zeros(v_all.shape, jnp.float32))
    return lax.fori_loop(0, q_len // blk_len, block_step, init_state)


def solution(mesh):
    to_heads = functools.partial(lax.all_to_all, axis_name='sp', split_axis=2, concat_axis=1, tiled=True)
    to_tokens = functools.partial(lax.all_to_all, axis_name='sp', split_axis=1, concat_axis=2, tiled=True)

    def sum_rows(partial_sum):
        return lax.psum_scatter(partial_sum, 'sp', scatter_dimension=0, tiled=True)

    def device_step(x_loc, grad_y, positions, g_norm, w_query, w_key, w_value, w_out, g_query, g_key):
        n_batch, loc_len, d_model = x_loc.shape
        q_loc, k_loc, v_loc, saved_fwd = block_front(x_loc, positions, g_norm, w_query, w_key, w_value, g_query, g_key)
        q_all = to_heads(q_loc)
        k_all = to_heads(k_loc)
        v_all = to_heads(v_loc)
        out_all, lse_all = attend_forward(q_all, k_all, v_all, 0)
        attended = to_tokens(out_all).reshape(n_batch, loc_len, d_model)
        y_out = (saved_fwd[0] + project(attended, w_out)).astype(jnp.bfloat16)
        grad_w_out = weight_grad(attended, grad_y)
        d_attn = project_back(grad_y, w_out).astype(jnp.bfloat16).reshape(q_loc.shape)
        dq_all, dk_acc, dv_acc = attend_backward(q_all, k_all, v_all, lse_all, to_heads(d_attn), 0)
        d_q = to_tokens(dq_all)
        d_k = to_tokens(dk_acc.astype(jnp.bfloat16))
        d_v = to_tokens(dv_acc.astype(jnp.bfloat16))
        grad_x, proj_grads, gain_terms = block_back(saved_fwd, d_q, d_k, d_v, grad_y, g_norm, w_query, w_key, w_value, g_query, g_key)
        hidden = saved_fwd[3]
        return (y_out, grad_x, sum_rows(jnp.sum(gain_terms[0], axis=(0, 1))), sum_rows(weight_grad(hidden, proj_grads[0])), sum_rows(weight_grad(hidden, proj_grads[1])), sum_rows(weight_grad(hidden, proj_grads[2])), sum_rows(grad_w_out), sum_rows(jnp.sum(gain_terms[1], axis=(0, 1))), sum_rows(jnp.sum(gain_terms[2], axis=(0, 1))))

    seq_spec = P('dp', 'sp', None)
    mat_rep = P(None, None)
    vec_rep = P(None)
    row_spec = P(('dp', 'sp'), None)
    vec_spec = P(('dp', 'sp'))
    return jax.shard_map(device_step, mesh=mesh, in_specs=(seq_spec, seq_spec, P('dp', 'sp'), vec_rep, mat_rep, mat_rep, mat_rep, mat_rep, vec_rep, vec_rep), out_specs=(seq_spec, seq_spec, vec_spec, row_spec, row_spec, row_spec, row_spec, vec_spec, vec_spec), check_vma=False)
```

profile of v0, /device:TPU:0, one launch (start us, length us, event | category | flops | bytes accessed | tf_op | source)
XLA Modules:
  0.0 1688.2 jit_solution(1331749573165304888)
XLA Ops:
  62.4 17.0 %fusion.124 = (f32[8,128,16,64]{3,2,1,0:T(8,128)}, f32[8,128,16,64]{3,2,1,0:T(8,128)}, f32[8,128,16,64]{3,2,1,0:T(8,128)}, f32[8,128,16,64]{3,2,1,0:T(8,128)}) fusion(f32[8,128,16,128]{3,2,1,0:T(8,128)} %bitcast.169, f32[8,128,16,128]{3,2,1,0:T(8,128)S(1)} %bitcast.166), kind=kLoop, calls=%fused_computation.144 | loop fusion | bytes 33554432 | tf_op jit(solution)/shard_map/slice | solution.py:23
  81.3 31.1 %subtract_convert_fusion = (bf16[8,128,16,64]{3,1,0,2:T(8,128)(2,1)}, bf16[8,128,16,64]{3,1,0,2:T(8,128)(2,1)}, bf16[8,128,16,64]{3,1,0,2:T(8,128)(2,1)}, bf16[8,128,16,64]{3,1,0,2:T(8,128)(2,1)}) fusion(f32[8,128,16,64]{3,2,1,0:T(8,128)} %get-tuple-element.406, f32[8,128,16,64]{3,2,1,0:T(8,128)} %get-tuple-element.405, ...), kind=kLoop, calls=%fused_computation.120 | loop fusion | flops 16777216 | bytes 25690112 | tf_op jit(solution)/shard_map/convert.6
  130.3 43.2 %all-to-all-done.1 = bf16[8,128,16,128]{3,1,0,2:T(8,128)(2,1)} async-done(((bf16[8,128,16,128]{3,1,0,2:T(8,128)(2,1)}), bf16[8,128,16,128]{3,1,0,2:T(8,128)(2,1)}, u32[]{:S(2)}, u32[]{:S(2)}) %all-to-all-start.1) | async-done | bytes 4194336 | tf_op jit(solution)/shard_map/all_to_all | solution.py:159
  193.8 33.3 %all-to-all-done = bf16[8,128,16,128]{3,1,0,2:T(8,128)(2,1)} async-done(((bf16[8,128,16,128]{3,1,0,2:T(8,128)(2,1)}), bf16[8,128,16,128]{3,1,0,2:T(8,128)(2,1)}, u32[]{:S(2)}, u32[]{:S(2)}) %all-to-all-start) | async-done | bytes 4194336 | tf_op jit(solution)/shard_map/all_to_all | solution.py:158
  257.1 23.7 %all-to-all-done.2 = bf16[8,128,16,128]{3,1,0,2:T(8,128)(2,1)} async-done(((bf16[8,128,16,128]{3,1,0,2:T(8,128)(2,1)}), bf16[8,128,16,128]{3,1,0,2:T(8,128)(2,1)}, u32[]{:S(2)}, u32[]{:S(2)}) %all-to-all-start.2) | async-done | bytes 4194336 | tf_op jit(solution)/shard_map/all_to_all | solution.py:160
  294.6 88.8 %while.34 = (s32[]{:T(128)}, bf16[8,1024,2,128]{3,2,0,1:T(2,128)(2,1)}, f32[8,2,1024]{2,1,0:T(2,128)S(1)}, bf16[8,1024,2,128]{3,1,2,0:T(8,128)(2,1)}, bf16[8,102...) while((s32[]{:T(128)}, ...), condition=%wide.region_6.7_spmd.clone, body=%wide.region_3.6_spmd.clone.sunk | while | flops 1099298944 | bytes 53019840 | solution.py:115
  392.2 596.3 %while.35 = (s32[]{:T(128)}, bf16[8,1024,2,128]{3,2,0,1:T(2,128)(2,1)}, f32[8,1024,2,128]{1,3,2,0:T(8,128)}, f32[8,1024,2,128]{1,3,2,0:T(8,128)}, bf16[8,1024,2,...) while((s32[]{:T(128)}, ...), condition=%wide.region_9.10_spmd.clone, body=%wide.region_7.9_spmd.clone.sunk | while | flops 2747668480 | bytes 142787824 | solution.py:145
  405.2 25.4 %bitcast_add_fusion.4 = f32[8,1024,2,128]{1,3,2,0:T(8,128)} fusion(f32[8,1024,2,128]{1,3,2,0:T(8,128)} %get-tuple-element.563, pred[]{:T(512)S(6)} %compare.3, f32[8,2,128,1024]{3,2,1,0:T(8,128)} %fusion.174, f32[8,2,128,1024]{3,2,1,0:T(8,128)} %fusion.175, f32[8,2,128]{2,1,0:T(2,128)S(1)} %constant_dynamic-slice_fusion.2, ...), kind=kOutput, calls=%fused_computation.21.clone.1 | convolution fusion | flops 564136960 | bytes 51134468 | tf_op jit(solution)/shard_map/while/body/eval_jaxpr/bhqk,bqhd->bkhd/dot_general | solution.py:139
  430.6 22.8 %fusion.176 = bf16[8,128,2,128]{3,1,2,0:T(8,128)(2,1)S(1)} fusion(bf16[8,1024,2,128]{3,1,2,0:T(8,128)(2,1)} %get-tuple-element.579, f32[8,2,128,1024]{3,2,1,0:T(8,128)} %fusion.174, f32[8,2,128,1024]{3,2,1,0:T(8,128)} %fusion.175, f32[8,2,128]{2,1,0:T(2,128)S(1)} %constant_dynamic-slice_fusion.2, pred[128,1024]{1,0:T(8,128)(4,1)S(1)} %iota_compare_fusion.5), kind=kOutput, calls=%fused_computation.43.clone.1 | convolution fusion | flops 560204800 | bytes 21635072 | tf_op jit(solution)/shard_map/while/body/eval_jaxpr/bhqk,bkhd->bqhd/dot_general | solution.py:140
  477.5 25.6 %bitcast_add_fusion.4 = f32[8,1024,2,128]{1,3,2,0:T(8,128)} fusion(f32[8,1024,2,128]{1,3,2,0:T(8,128)} %get-tuple-element.563, pred[]{:T(512)S(6)} %compare.3, f32[8,2,128,1024]{3,2,1,0:T(8,128)} %fusion.174, f32[8,2,128,1024]{3,2,1,0:T(8,128)} %fusion.175, f32[8,2,128]{2,1,0:T(2,128)S(1)} %constant_dynamic-slice_fusion.2, ...), kind=kOutput, calls=%fused_computation.21.clone.1 | convolution fusion | flops 564136960 | bytes 51134468 | tf_op jit(solution)/shard_map/while/body/eval_jaxpr/bhqk,bqhd->bkhd/dot_general | solution.py:139
  503.0 22.8 %fusion.176 = bf16[8,128,2,128]{3,1,2,0:T(8,128)(2,1)S(1)} fusion(bf16[8,1024,2,128]{3,1,2,0:T(8,128)(2,1)} %get-tuple-element.579, f32[8,2,128,1024]{3,2,1,0:T(8,128)} %fusion.174, f32[8,2,128,1024]{3,2,1,0:T(8,128)} %fusion.175, f32[8,2,128]{2,1,0:T(2,128)S(1)} %constant_dynamic-slice_fusion.2, pred[128,1024]{1,0:T(8,128)(4,1)S(1)} %iota_compare_fusion.5), kind=kOutput, calls=%fused_computation.43.clone.1 | convolution fusion | flops 560204800 | bytes 21635072 | tf_op jit(solution)/shard_map/while/body/eval_jaxpr/bhqk,bkhd->bqhd/dot_general | solution.py:140
  552.3 25.6 %bitcast_add_fusion.4 = f32[8,1024,2,128]{1,3,2,0:T(8,128)} fusion(f32[8,1024,2,128]{1,3,2,0:T(8,128)} %get-tuple-element.563, pred[]{:T(512)S(6)} %compare.3, f32[8,2,128,1024]{3,2,1,0:T(8,128)} %fusion.174, f32[8,2,128,1024]{3,2,1,0:T(8,128)} %fusion.175, f32[8,2,128]{2,1,0:T(2,128)S(1)} %constant_dynamic-slice_fusion.2, ...), kind=kOutput, calls=%fused_computation.21.clone.1 | convolution fusion | flops 564136960 | bytes 51134468 | tf_op jit(solution)/shard_map/while/body/eval_jaxpr/bhqk,bqhd->bkhd/dot_general | solution.py:139
  577.9 22.8 %fusion.176 = bf16[8,128,2,128]{3,1,2,0:T(8,128)(2,1)S(1)} fusion(bf16[8,1024,2,128]{3,1,2,0:T(8,128)(2,1)} %get-tuple-element.579, f32[8,2,128,1024]{3,2,1,0:T(8,128)} %fusion.174, f32[8,2,128,1024]{3,2,1,0:T(8,128)} %fusion.175, f32[8,2,128]{2,1,0:T(2,128)S(1)} %constant_dynamic-slice_fusion.2, pred[128,1024]{1,0:T(8,128)(4,1)S(1)} %iota_compare_fusion.5), kind=kOutput, calls=%fused_computation.43.clone.1 | convolution fusion | flops 560204800 | bytes 21635072 | tf_op jit(solution)/shard_map/while/body/eval_jaxpr/bhqk,bkhd->bqhd/dot_general | solution.py:140
  627.1 25.6 %bitcast_add_fusion.4 = f32[8,1024,2,128]{1,3,2,0:T(8,128)} fusion(f32[8,1024,2,128]{1,3,2,0:T(8,128)} %get-tuple-element.563, pred[]{:T(512)S(6)} %compare.3, f32[8,2,128,1024]{3,2,1,0:T(8,128)} %fusion.174, f32[8,2,128,1024]{3,2,1,0:T(8,128)} %fusion.175, f32[8,2,128]{2,1,0:T(2,128)S(1)} %constant_dynamic-slice_fusion.2, ...), kind=kOutput, calls=%fused_computation.21.clone.1 | convolution fusion | flops 564136960 | bytes 51134468 | tf_op jit(solution)/shard_map/while/body/eval_jaxpr/bhqk,bqhd->bkhd/dot_general | solution.py:139
  652.7 22.8 %fusion.176 = bf16[8,128,2,128]{3,1,2,0:T(8,128)(2,1)S(1)} fusion(bf16[8,1024,2,128]{3,1,2,0:T(8,128)(2,1)} %get-tuple-element.579, f32[8,2,128,1024]{3,2,1,0:T(8,128)} %fusion.174, f32[8,2,128,1024]{3,2,1,0:T(8,128)} %fusion.175, f32[8,2,128]{2,1,0:T(2,128)S(1)} %constant_dynamic-slice_fusion.2, pred[128,1024]{1,0:T(8,128)(4,1)S(1)} %iota_compare_fusion.5), kind=kOutput, calls=%fused_computation.43.clone.1 | convolution fusion | flops 560204800 | bytes 21635072 | tf_op jit(solution)/shard_map/while/body/eval_jaxpr/bhqk,bkhd->bqhd/dot_general | solution.py:140
  701.9 25.6 %bitcast_add_fusion.4 = f32[8,1024,2,128]{1,3,2,0:T(8,128)} fusion(f32[8,1024,2,128]{1,3,2,0:T(8,128)} %get-tuple-element.563, pred[]{:T(512)S(6)} %compare.3, f32[8,2,128,1024]{3,2,1,0:T(8,128)} %fusion.174, f32[8,2,128,1024]{3,2,1,0:T(8,128)} %fusion.175, f32[8,2,128]{2,1,0:T(2,128)S(1)} %constant_dynamic-slice_fusion.2, ...), kind=kOutput, calls=%fused_computation.21.clone.1 | convolution fusion | flops 564136960 | bytes 51134468 | tf_op jit(solution)/shard_map/while/body/eval_jaxpr/bhqk,bqhd->bkhd/dot_general | solution.py:139
  727.5 22.8 %fusion.176 = bf16[8,128,2,128]{3,1,2,0:T(8,128)(2,1)S(1)} fusion(bf16[8,1024,2,128]{3,1,2,0:T(8,128)(2,1)} %get-tuple-element.579, f32[8,2,128,1024]{3,2,1,0:T(8,128)} %fusion.174, f32[8,2,128,1024]{3,2,1,0:T(8,128)} %fusion.175, f32[8,2,128]{2,1,0:T(2,128)S(1)} %constant_dynamic-slice_fusion.2, pred[128,1024]{1,0:T(8,128)(4,1)S(1)} %iota_compare_fusion.5), kind=kOutput, calls=%fused_computation.43.clone.1 | convolution fusion | flops 560204800 | bytes 21635072 | tf_op jit(solution)/shard_map/while/body/eval_jaxpr/bhqk,bkhd->bqhd/dot_general | solution.py:140
  776.7 25.5 %bitcast_add_fusion.4 = f32[8,1024,2,128]{1,3,2,0:T(8,128)} fusion(f32[8,1024,2,128]{1,3,2,0:T(8,128)} %get-tuple-element.563, pred[]{:T(512)S(6)} %compare.3, f32[8,2,128,1024]{3,2,1,0:T(8,128)} %fusion.174, f32[8,2,128,1024]{3,2,1,0:T(8,128)} %fusion.175, f32[8,2,128]{2,1,0:T(2,128)S(1)} %constant_dynamic-slice_fusion.2, ...), kind=kOutput, calls=%fused_computation.21.clone.1 | convolution fusion | flops 564136960 | bytes 51134468 | tf_op jit(solution)/shard_map/while/body/eval_jaxpr/bhqk,bqhd->bkhd/dot_general | solution.py:139
  802.2 22.8 %fusion.176 = bf16[8,128,2,128]{3,1,2,0:T(8,128)(2,1)S(1)} fusion(bf16[8,1024,2,128]{3,1,2,0:T(8,128)(2,1)} %get-tuple-element.579, f32[8,2,128,1024]{3,2,1,0:T(8,128)} %fusion.174, f32[8,2,128,1024]{3,2,1,0:T(8,128)} %fusion.175, f32[8,2,128]{2,1,0:T(2,128)S(1)} %constant_dynamic-slice_fusion.2, pred[128,1024]{1,0:T(8,128)(4,1)S(1)} %iota_compare_fusion.5), kind=kOutput, calls=%fused_computation.43.clone.1 | convolution fusion | flops 560204800 | bytes 21635072 | tf_op jit(solution)/shard_map/while/body/eval_jaxpr/bhqk,bkhd->bqhd/dot_general | solution.py:140
  851.4 25.6 %bitcast_add_fusion.4 = f32[8,1024,2,128]{1,3,2,0:T(8,128)} fusion(f32[8,1024,2,128]{1,3,2,0:T(8,128)} %get-tuple-element.563, pred[]{:T(512)S(6)} %compare.3, f32[8,2,128,1024]{3,2,1,0:T(8,128)} %fusion.174, f32[8,2,128,1024]{3,2,1,0:T(8,128)} %fusion.175, f32[8,2,128]{2,1,0:T(2,128)S(1)} %constant_dynamic-slice_fusion.2, ...), kind=kOutput, calls=%fused_computation.21.clone.1 | convolution fusion | flops 564136960 | bytes 51134468 | tf_op jit(solution)/shard_map/while/body/eval_jaxpr/bhqk,bqhd->bkhd/dot_general | solution.py:139
  877.0 22.8 %fusion.176 = bf16[8,128,2,128]{3,1,2,0:T(8,128)(2,1)S(1)} fusion(bf16[8,1024,2,128]{3,1,2,0:T(8,128)(2,1)} %get-tuple-element.579, f32[8,2,128,1024]{3,2,1,0:T(8,128)} %fusion.174, f32[8,2,128,1024]{3,2,1,0:T(8,128)} %fusion.175, f32[8,2,128]{2,1,0:T(2,128)S(1)} %constant_dynamic-slice_fusion.2, pred[128,1024]{1,0:T(8,128)(4,1)S(1)} %iota_compare_fusion.5), kind=kOutput, calls=%fused_computation.43.clone.1 | convolution fusion | flops 560204800 | bytes 21635072 | tf_op jit(solution)/shard_map/while/body/eval_jaxpr/bhqk,bkhd->bqhd/dot_general | solution.py:140
  926.3 25.5 %bitcast_add_fusion.4 = f32[8,1024,2,128]{1,3,2,0:T(8,128)} fusion(f32[8,1024,2,128]{1,3,2,0:T(8,128)} %get-tuple-element.563, pred[]{:T(512)S(6)} %compare.3, f32[8,2,128,1024]{3,2,1,0:T(8,128)} %fusion.174, f32[8,2,128,1024]{3,2,1,0:T(8,128)} %fusion.175, f32[8,2,128]{2,1,0:T(2,128)S(1)} %constant_dynamic-slice_fusion.2, ...), kind=kOutput, calls=%fused_computation.21.clone.1 | convolution fusion | flops 564136960 | bytes 51134468 | tf_op jit(solution)/shard_map/while/body/eval_jaxpr/bhqk,bqhd->bkhd/dot_general | solution.py:139
  951.8 22.8 %fusion.176 = bf16[8,128,2,128]{3,1,2,0:T(8,128)(2,1)S(1)} fusion(bf16[8,1024,2,128]{3,1,2,0:T(8,128)(2,1)} %get-tuple-element.579, f32[8,2,128,1024]{3,2,1,0:T(8,128)} %fusion.174, f32[8,2,128,1024]{3,2,1,0:T(8,128)} %fusion.175, f32[8,2,128]{2,1,0:T(2,128)S(1)} %constant_dynamic-slice_fusion.2, pred[128,1024]{1,0:T(8,128)(4,1)S(1)} %iota_compare_fusion.5), kind=kOutput, calls=%fused_computation.43.clone.1 | convolution fusion | flops 560204800 | bytes 21635072 | tf_op jit(solution)/shard_map/while/body/eval_jaxpr/bhqk,bkhd->bqhd/dot_general | solution.py:140
  1001.0 53.6 %all_to_all.120 = bf16[8,1024,2,128]{3,2,0,1:T(2,128)(2,1)} all-to-all(bf16[8,1024,2,128]{3,2,0,1:T(2,128)(2,1)} %copy.50), channel_id=1, replica_groups=mesh['dp'=2,'sp'=8] {'sp'}, dimensions={1} | all-to-all | bytes 8388608 | tf_op jit(solution)/shard_map/all_to_all | solution.py:168
  1065.8 42.4 %all-to-all-done.5 = bf16[8,1024,2,128]{3,2,0,1:T(2,128)(2,1)} async-done(((bf16[8,1024,2,128]{3,2,0,1:T(2,128)(2,1)}), bf16[8,1024,2,128]{3,2,0,1:T(2,128)(2,1)}, u32[]{:S(2)}, u32[]{:S(2)}) %all-to-all-start.5) | async-done | bytes 4194336 | tf_op jit(solution)/shard_map/all_to_all | solution.py:167
  1115.1 19.9 %multiply_add_fusion.1 = (f32[8,128,16,64]{3,1,0,2:T(8,128)S(1)}, f32[8,128,16,64]{3,1,0,2:T(8,128)}, f32[8,128,16,64]{3,1,0,2:T(8,128)}, f32[8,128,16,64]{3,1,0,2:T(8,128)}) fusion(f32[8,128,16,128]{3,1,0,2:T(8,128)} %bitcast.168, f32[8,128,64]{2,1,0:T(8,128)S(1)} %copy-done.10, f32[8,128,64]{2,1,0:T(8,128)S(1)} %copy-done.8, f32[8,128,16,128]{3,1,0,2:T(8,128)} %bitcast.167), kind=kLoop, calls=%fused_computation.118 | loop fusion | flops 12582912 | bytes 34078720 | tf_op jit(solution)/shard_map/add | solution.py:32
  1220.1 74.3 %all_to_all.121 = bf16[8,1024,2,128]{3,2,0,1:T(2,128)(2,1)S(1)} all-to-all(bf16[8,1024,2,128]{3,2,0,1:T(2,128)(2,1)} %copy.53), channel_id=1, replica_groups=mesh['dp'=2,'sp'=8] {'sp'}, dimensions={1} | all-to-all | bytes 8388608 | tf_op jit(solution)/shard_map/all_to_all | solution.py:169
  1323.9 77.3 %all_to_all.122 = bf16[8,1024,2,128]{3,2,0,1:T(2,128)(2,1)S(1)} all-to-all(bf16[8,1024,2,128]{3,2,0,1:T(2,128)(2,1)} %get-tuple-element.305), channel_id=1, replica_groups=mesh['dp'=2,'sp'=8] {'sp'}, dimensions={1} | all-to-all | bytes 8388608 | tf_op jit(solution)/shard_map/all_to_all | solution.py:162
  1460.2 23.5 %fusion.89 = (f32[2048]{0:T(1024)S(1)}, f32[8,128]{1,0:T(8,128)S(1)}, f32[8,128,2048]{2,1,0:T(8,128)}) fusion(bf16[8,128,2048]{2,1,0:T(8,128)(2,1)} %param.14, f32[8,128]{1,0:T(8,128)S(1)} %copy-done.26, f32[2048]{0:T(1024)S(1)} %copy-done.24, f32[8,128,2048]{2,1,0:T(8,128)} %fusion.98, f32[8,128,2048]{2,1,0:T(8,128)} %fusion.102, ...), kind=kOutput, calls=%fused_computation.83 | convolution fusion | flops 8608805888 | bytes 41967616 | tf_op jit(solution)/shard_map/bse,de->bsd/dot_general | solution.py:52
  1483.7 24.2 %all-reduce.3 = (f32[2048]{0:T(1024)S(1)}, f32[2048]{0:T(1024)S(1)}, f32[2048]{0:T(1024)S(1)}) all-reduce(f32[2048]{0:T(1024)S(1)} %get-tuple-element.360, f32[2048]{0:T(1024)S(1)} %copy-done.22, f32[2048]{0:T(1024)S(1)} %get-tuple-element.356), channel_id=2, replica_groups=mesh['dp'=2,'sp'=8] {'sp'}, use_global_device_ids=true, to_apply=%region_14.15.clone | all-reduce | flops 6144 | bytes 49152
  1533.0 33.8 %reduce-scatter.9.cloned.1.call-done = f32[256,2048]{1,0:T(8,128)} async-done(((f32[2048,2048]{1,0:T(8,128)}), f32[256,2048]{1,0:T(8,128)}) %reduce-scatter.9.cloned.1.call-update) | async-done | bytes 2097168 | tf_op jit(solution)/shard_map/reduce_scatter | solution.py:153
  1566.8 114.6 %reduce-scatter.11.cloned.1.call-done = f32[256,2048]{1,0:T(8,128)} async-done(((f32[2048,2048]{1,0:T(8,128)}), f32[256,2048]{1,0:T(8,128)}) %reduce-scatter.11.cloned.1.call-update) | async-done | bytes 2097168 | tf_op jit(solution)/shard_map/reduce_scatter | solution.py:153
  (281 shorter events, 673.0 us)
Async XLA Ops:
  10.3 167.8 %copy-start.25 = (f32[8,128]{1,0:T(8,128)}, f32[8,128]{1,0:T(8,128)S(1)}, u32[]{:S(2)}) copy-start(f32[8,128]{1,0:T(8,128)S(1)} %add_rsqrt_fusion.2) | copy-start | bytes 12292
  11.0 167.1 %copy-start.23 = (f32[2048]{0:T(1024)}, f32[2048]{0:T(1024)S(1)}, u32[]{:S(2)}) copy-start(f32[2048]{0:T(1024)S(1)} %convert_element_type.116) | copy-start | bytes 24580
  11.0 12.8 copy-start.27
  34.9 13.0 copy-start.28
  53.8 8.6 copy-start.29
  81.3 31.2 %copy-start.7 = (f32[8,128,64]{2,1,0:T(8,128)}, f32[8,128,64]{2,1,0:T(8,128)S(1)}, u32[]{:S(2)}) copy-start(f32[8,128,64]{2,1,0:T(8,128)S(1)} %get-tuple-element.413) | copy-start | bytes 786436
  81.3 31.1 %copy-start.9 = (f32[8,128,64]{2,1,0:T(8,128)}, f32[8,128,64]{2,1,0:T(8,128)S(1)}, u32[]{:S(2)}) copy-start(f32[8,128,64]{2,1,0:T(8,128)S(1)} %get-tuple-element.414) | copy-start | bytes 786436
  118.9 54.6 %all-to-all-start.1 = ((bf16[8,128,16,128]{3,1,0,2:T(8,128)(2,1)}), bf16[8,128,16,128]{3,1,0,2:T(8,128)(2,1)}, u32[]{:S(2)}, u32[]{:S(2)}) async-start(bf16[8,128,16,128]{3,1,0,2:T(8,128)(2,1)} %pad_maximum_fusion.1), calls=%async_computation.1 | async-start | bytes 8388608 | tf_op jit(solution)/shard_map/all_to_all | solution.py:159
  173.5 53.7 %all-to-all-start = ((bf16[8,128,16,128]{3,1,0,2:T(8,128)(2,1)}), bf16[8,128,16,128]{3,1,0,2:T(8,128)(2,1)}, u32[]{:S(2)}, u32[]{:S(2)}) async-start(bf16[8,128,16,128]{3,1,0,2:T(8,128)(2,1)} %pad_maximum_fusion), calls=%async_computation | async-start | bytes 8388608 | tf_op jit(solution)/shard_map/all_to_all | solution.py:158
  227.2 53.7 %all-to-all-start.2 = ((bf16[8,128,16,128]{3,1,0,2:T(8,128)(2,1)}), bf16[8,128,16,128]{3,1,0,2:T(8,128)(2,1)}, u32[]{:S(2)}, u32[]{:S(2)}) async-start(bf16[8,128,16,128]{3,1,0,2:T(8,128)(2,1)} %bitcast.176), calls=%async_computation.2 | async-start | bytes 8388608 | tf_op jit(solution)/shard_map/all_to_all | solution.py:160
  280.9 102.5 %all-to-all-start.4 = ((bf16[8,128,16,128]{3,1,0,2:T(8,128)(2,1)}), bf16[8,128,16,128]{3,1,0,2:T(8,128)(2,1)}, u32[]{:S(2)}, u32[]{:S(2)}) async-start(bf16[8,128,16,128]{3,1,0,2:T(8,128)(2,1)} %bitcast.175), calls=%async_computation.4 | async-start | bytes 8388608 | tf_op jit(solution)/shard_map/all_to_all | solution.py:166
  392.6 7.0 copy-start.1
  689.2 7.0 copy-start.1
  1054.6 53.7 %all-to-all-start.5 = ((bf16[8,1024,2,128]{3,2,0,1:T(2,128)(2,1)}), bf16[8,1024,2,128]{3,2,0,1:T(2,128)(2,1)}, u32[]{:S(2)}, u32[]{:S(2)}) async-start(bf16[8,1024,2,128]{3,2,0,1:T(2,128)(2,1)} %get-tuple-element.307), calls=%async_computation.5 | async-start | bytes 8388608 | tf_op jit(solution)/shard_map/all_to_all | solution.py:167
  1059.1 473.9 %reduce-scatter.5.cloned.1.call-start = ((), (), s32[]{:S(2)}) async-start(), calls=%async_computation.12 | async-start | bytes 18874368 | tf_op jit(solution)/shard_map/reduce_scatter | solution.py:153
  1065.8 49.2 %copy-start.8 = (f32[8,128,64]{2,1,0:T(8,128)S(1)}, f32[8,128,64]{2,1,0:T(8,128)}, u32[]{:S(2)}) copy-start(f32[8,128,64]{2,1,0:T(8,128)} %copy-done.7) | copy-start | bytes 786436
  1065.8 49.2 %copy-start.10 = (f32[8,128,64]{2,1,0:T(8,128)S(1)}, f32[8,128,64]{2,1,0:T(8,128)}, u32[]{:S(2)}) copy-start(f32[8,128,64]{2,1,0:T(8,128)} %copy-done.9) | copy-start | bytes 786436
  1108.2 26.7 %slice-start = ((s8[8388608]{0:T(1024)(128)(4,1)}), s8[4194304]{0:T(1024)(128)(4,1)S(1)}, s32[]{:S(2)}) async-start(s8[8388608]{0:T(1024)(128)(4,1)} %bitcast.164), calls=%async_computation.16 | async-start | bytes 8388608
  1115.0 20.0 %slice-start.1 = ((s8[8388608]{0:T(1024)(128)(4,1)}), s8[4194304]{0:T(1024)(128)(4,1)S(1)}, s32[]{:S(2)}) async-start(s8[8388608]{0:T(1024)(128)(4,1)} %bitcast.164), calls=%async_computation.17 | async-start | bytes 8388608
  1115.0 20.0 %copy-start.17 = (f32[2048]{0:T(1024)S(1)}, f32[2048]{0:T(1024)}, u32[]{:S(2)}) copy-start(f32[2048]{0:T(1024)} %copy-done.16) | copy-start | bytes 24580
  1115.0 20.0 %copy-start.21 = (f32[8,128]{1,0:T(8,128)S(1)}, f32[8,128]{1,0:T(8,128)}, u32[]{:S(2)}) copy-start(f32[8,128]{1,0:T(8,128)} %copy-done.20) | copy-start | bytes 12292
  1141.6 8.2 copy-start.4
  1141.6 8.2 copy-start.24
  1141.6 8.2 copy-start.26
  1164.5 368.5 %reduce-scatter.7.cloned.1.call-start = ((), (), s32[]{:S(2)}) async-start(), calls=%async_computation.13 | async-start | bytes 18874368 | tf_op jit(solution)/shard_map/reduce_scatter | solution.py:153
  1178.5 16.4 copy-start.5
  1207.4 359.4 %reduce-scatter.9.cloned.1.call-start = ((), (), s32[]{:S(2)}) async-start(), calls=%async_computation.14 | async-start | bytes 18874368 | tf_op jit(solution)/shard_map/reduce_scatter | solution.py:153
  1323.9 357.5 %reduce-scatter.11.cloned.1.call-start = ((), (), s32[]{:S(2)}) async-start(), calls=%async_computation.15 | async-start | bytes 18874368 | tf_op jit(solution)/shard_map/reduce_scatter | solution.py:153
  1431.6 15.0 copy-start.13
  1460.2 23.5 %copy-start.22 = (f32[2048]{0:T(1024)S(1)}, f32[2048]{0:T(1024)}, u32[]{:S(2)}) copy-start(f32[2048]{0:T(1024)} %get-tuple-element.358) | copy-start | bytes 24580
  1509.8 9.8 copy-start.6
  1509.8 10.5 copy-start.12
  (24 other events, 132.6 us)
Sparse Core Ops, SparseCore 0:
  1164.6 148.5 reduce-scatter.4
  1317.3 134.2 reduce-scatter.6
  1455.7 111.0 reduce-scatter.8
  1570.8 110.5 reduce-scatter.10
where the time goes:
time: 1700 us; the launch traced here: 1690 us
  matrix products  816 us (48%)
  waiting for transfers between devices  291 us (17%)
  blocking collectives  229 us (13%)
  local copies, waits for them, and re-layouts  160 us (9%)
  other arithmetic  151 us (9%)
  starting transfers between devices  24.1 us (1%)
    dot_general x8, matrix products, block_step(): jnp.einsum('bhqk,bqhd->bkhd', ds_bf, q_blk, preferred_element_type=jnp.fl...  204 us
    dot_general x8, matrix products, block_step(): jnp.einsum('bhqk,bkhd->bqhd', ds_bf, k_all, preferred_element_type=jnp.fl...  183 us
    reduce_scatter x4, waiting for transfers between devices, sum_rows(): return lax.psum_scatter(partial_sum, 'sp', scatter_dimension=0, tiled=True)  148 us
    dot_general x8, matrix products, block_step(): jnp.einsum('bhqk,bqhd->bkhd', prob_bf, do_blk, preferred_element_type=jnp...  96.5 us
    dot_general x16, matrix products, block_step(): jnp.einsum('bqhd,bkhd->bhqk', q_blk, k_all, preferred_element_type=jnp.fl...  89.2 us
    all_to_all x1, blocking collectives, device_step(): attended = to_tokens(out_all).reshape(n_batch, loc_len, d_model)  77.3 us
    all_to_all x1, blocking collectives, device_step(): d_v = to_tokens(dv_acc.astype(jnp.bfloat16))  74.3 us
    dot_general x4, matrix products, project_back(): jnp.einsum('bse,de->bsd', grads_in, weight, preferred_element_type=jnp.fl...  64.6 us
  transfers between devices with their start and end apart: 9, of which 6 were waited for; matrix products, arithmetic and copies ran while one was open for 20% of the time, Pallas kernels for 0%

commit v1 on v0

v1 whole, which is shorter than its diff:
```python
import functools
import jax
import jax.numpy as jnp
from jax import lax
from jax.experimental import pallas as pl
from jax.experimental.pallas import tpu as pltpu
from jax.sharding import PartitionSpec as P

HEAD_DIM = 128
NORM_EPS = 1e-5
ROPE_BASE = 10000.0
NEG_BIG = -1e30
Q_BLK = 256
LOG2E = 1.4426950408889634


def mm(lhs, rhs):
    return lax.dot_general(lhs, rhs, (((1,), (0,)), ((), ())), preferred_element_type=jnp.float32)


def mm_nt(lhs, rhs):
    return lax.dot_general(lhs, rhs, (((1,), (1,)), ((), ())), preferred_element_type=jnp.float32)


def mm_tn(lhs, rhs):
    return lax.dot_general(lhs, rhs, (((0,), (0,)), ((), ())), preferred_element_type=jnp.float32)


def rope_tables(positions):
    half_dim = HEAD_DIM // 2
    inv_freq = ROPE_BASE ** (-jnp.arange(half_dim, dtype=jnp.float32) * (2.0 / HEAD_DIM))
    angles = positions.astype(jnp.float32)[..., None] * inv_freq
    cos_h, sin_h = jnp.cos(angles), jnp.sin(angles)
    return jnp.concatenate([cos_h, cos_h], axis=-1), jnp.concatenate([-sin_h, sin_h], axis=-1)


def rotate(values, cos_t, sin_t):
    return values * cos_t + pltpu.roll(values, HEAD_DIM // 2, 1) * sin_t


ANY_SPEC = pl.BlockSpec(memory_space=pltpu.HBM)
N_BLK = 256
MIB = 1024 * 1024
VMEM_MIB = 63


def bf_shape(*dims):
    return jax.ShapeDtypeStruct(dims, jnp.bfloat16)


def f32_shape(*dims):
    return jax.ShapeDtypeStruct(dims, jnp.float32)


def cost(flops, bytes_moved, exps=0):
    return pl.CostEstimate(flops=flops, bytes_accessed=bytes_moved, transcendentals=exps)


def limit(mib):
    return pltpu.CompilerParams(vmem_limit_bytes=max(mib, VMEM_MIB) * MIB)


def fixed(*dims):
    return pl.BlockSpec(dims, lambda i: (0,) * len(dims), pipeline_mode=pl.Buffered(1))


def qkv_kernel(x_ref, gain_ref, wq_ref, wk_ref, wv_ref, hid_ref, q_ref, k_ref, v_ref, qinv_ref, kinv_ref, qsum, ksum):
    step = pl.program_id(0)
    rows, width = x_ref.shape

    @pl.when(step == 0)
    def _():
        @pl.loop(0, rows // 128)
        def _(blk):
            span = pl.ds(pl.multiple_of(blk * 128, 128), 128)
            x_f = x_ref[span, :].astype(jnp.float32)
            inv_rms = lax.rsqrt(jnp.mean(x_f * x_f, axis=-1, keepdims=True) + NORM_EPS)
            hid_ref[span, :] = (x_f * inv_rms * gain_ref[...].astype(jnp.float32)).astype(jnp.bfloat16)

        qsum[...] = jnp.zeros_like(qsum)
        ksum[...] = jnp.zeros_like(ksum)

    for w_ref, out_ref, acc in ((wq_ref, q_ref, qsum), (wk_ref, k_ref, ksum)):
        raw = mm(hid_ref[...], w_ref[...])
        out_ref[...] = raw
        for part in range(N_BLK // 128):
            piece = raw[:, part * 128:(part + 1) * 128]
            acc[...] += piece * piece
    v_ref[...] = mm(hid_ref[...], wv_ref[...]).astype(jnp.bfloat16)

    @pl.when(step == pl.num_programs(0) - 1)
    def _():
        for acc, inv_ref in ((qsum, qinv_ref), (ksum, kinv_ref)):
            inv_ref[...] = lax.rsqrt(jnp.sum(acc[...], axis=-1, keepdims=True) * (1.0 / width) + NORM_EPS)


def qkv_call(x_seq, gain, w_query, w_key, w_value):
    rows, width = x_seq.shape
    w_col = pl.BlockSpec((width, N_BLK), lambda i: (0, i))
    o_col = pl.BlockSpec((rows, N_BLK), lambda i: (0, i))
    return pl.pallas_call(
        qkv_kernel, grid=(width // N_BLK,),
        in_specs=[fixed(rows, width), fixed(1, width), w_col, w_col, w_col],
        out_specs=[pl.BlockSpec((rows, width), lambda i: (0, 0)), o_col, o_col, o_col] + [pl.BlockSpec((rows, 1), lambda i: (0, 0))] * 2,
        out_shape=[bf_shape(rows, width), f32_shape(rows, width), f32_shape(rows, width), bf_shape(rows, width), f32_shape(rows, 1), f32_shape(rows, 1)],
        scratch_shapes=[pltpu.VMEM((rows, 128), jnp.float32)] * 2,
        cost_estimate=cost(6 * rows * width * width, 6 * width * width + 14 * rows * width),
        compiler_params=limit(48), name="qkv",
    )(x_seq, gain.reshape(1, width), w_query, w_key, w_value)


def rope_heads(q1_ref, k1_ref, qinv_ref, kinv_ref, gq_ref, gk_ref, cos_ref, sin_ref, q_s, k_s):
    cos_t, sin_t = cos_ref[...], sin_ref[...]
    q_s[...] = rotate(q1_ref[...] * qinv_ref[...] * gq_ref[...].astype(jnp.float32), cos_t, sin_t).astype(jnp.bfloat16)
    k_s[...] = rotate(k1_ref[...] * kinv_ref[...] * gk_ref[...].astype(jnp.float32), cos_t, sin_t).astype(jnp.bfloat16)


def masked_scores(keys, q_blk, q_lo):
    scores = mm_nt(keys, q_blk)
    edge = scores[q_lo:, :]
    key_pos = lax.broadcasted_iota(jnp.int32, edge.shape, 0)
    q_pos = lax.broadcasted_iota(jnp.int32, edge.shape, 1)
    edge = jnp.where(q_pos >= key_pos, edge, NEG_BIG)
    return edge if q_lo == 0 else jnp.concatenate([scores[:q_lo, :], edge], axis=0)


def attn_fwd_kernel(q1_ref, k1_ref, v_ref, qinv_ref, kinv_ref, gq_ref, gk_ref, cos_ref, sin_ref, a_ref, q_s, k_s, lse_ref):
    seq = q1_ref.shape[0]
    rope_heads(q1_ref, k1_ref, qinv_ref, kinv_ref, gq_ref, gk_ref, cos_ref, sin_ref, q_s, k_s)
    to_log2 = HEAD_DIM ** -0.5 * LOG2E
    v_t = v_ref[...].T
    for blk in range(seq // Q_BLK):
        q_lo, k_len = blk * Q_BLK, (blk + 1) * Q_BLK
        scores = masked_scores(k_s[:k_len, :], q_s[q_lo:k_len, :], q_lo)
        top = jnp.max(scores, axis=0, keepdims=True)
        prob = jnp.exp2((scores - top) * to_log2)
        total = jnp.sum(prob, axis=0, keepdims=True)
        out_t = mm(v_t[:, :k_len], prob.astype(jnp.bfloat16)) * (1.0 / total)
        a_ref[q_lo:k_len, :] = out_t.T.astype(jnp.bfloat16)
        lse_ref[0, :, q_lo:k_len] = top * to_log2 + jnp.log2(total)


def attn_bwd_kernel(q_ref, k_ref, v_ref, do_ref, lse_ref, dep_ref, dq_ref, dk_ref, dv_ref, dk_s, dv_s):
    seq = q_ref.shape[0]
    scale = HEAD_DIM ** -0.5
    k_t = k_ref[...].T
    n_blk = seq // Q_BLK
    for blk in reversed(range(n_blk)):
        q_lo, k_len = blk * Q_BLK, (blk + 1) * Q_BLK
        q_blk = q_ref[q_lo:k_len, :]
        do_blk = do_ref[q_lo:k_len, :]
        scores = masked_scores(k_ref[:k_len, :], q_blk, q_lo)
        prob = jnp.exp2(scores * (scale * LOG2E) - lse_ref[0, :, q_lo:k_len])
        d_prob = mm_nt(v_ref[:k_len, :], do_blk)
        row_dot = jnp.sum(prob * d_prob, axis=0, keepdims=True)
        ds_bf = (prob * ((d_prob - row_dot) * scale)).astype(jnp.bfloat16)
        dq_t = mm(k_t[:, :k_len], ds_bf)
        dq_ref[q_lo:k_len, :] = dq_t.T.astype(jnp.bfloat16)
        dv_part = mm(prob.astype(jnp.bfloat16), do_blk)
        dk_part = mm(ds_bf, q_blk)
        if blk == n_blk - 1:
            dv_s[...] = dv_part
            dk_s[...] = dk_part
        else:
            dv_s[:k_len, :] += dv_part
            dk_s[:k_len, :] += dk_part
    dv_ref[...] = dv_s[...].astype(jnp.bfloat16)
    dk_ref[...] = dk_s[...].astype(jnp.bfloat16)


def attn_specs(seq):
    head = pl.BlockSpec((seq, HEAD_DIM), lambda h: (0, h))
    lse = pl.BlockSpec((1, 1, seq), lambda h: (h, 0, 0))
    return head, lse


def attn_fwd_call(q_raw, k_raw, v_val, q_inv, k_inv, g_query, g_key, cos_t, sin_t):
    seq, width = q_raw.shape
    n_heads = width // HEAD_DIM
    head, lse = attn_specs(seq)
    gain = pl.BlockSpec((1, HEAD_DIM), lambda h: (0, h))
    return pl.pallas_call(
        attn_fwd_kernel, grid=(n_heads,),
        in_specs=[head, head, head, fixed(seq, 1), fixed(seq, 1), gain, gain, fixed(seq, HEAD_DIM), fixed(seq, HEAD_DIM)],
        out_specs=[head, head, head, lse],
        out_shape=[bf_shape(seq, width)] * 3 + [f32_shape(n_heads, 1, seq)],
        cost_estimate=cost(4 * seq * seq * width, 16 * seq * width, seq * seq * n_heads // 2),
        compiler_params=limit(40), name="attention_fwd",
    )(q_raw, k_raw, v_val, q_inv, k_inv, g_query.reshape(1, width), g_key.reshape(1, width), cos_t, sin_t)


def attn_bwd_call(q_bf, k_bf, v_val, d_attn, lse_all, dep):
    seq, width = q_bf.shape
    n_heads = width // HEAD_DIM
    head, lse = attn_specs(seq)
    return pl.pallas_call(
        attn_bwd_kernel, grid=(n_heads,),
        in_specs=[head, head, head, head, lse, ANY_SPEC],
        out_specs=[head] * 3, out_shape=[bf_shape(seq, width)] * 3,
        scratch_shapes=[pltpu.VMEM((seq, HEAD_DIM), jnp.float32)] * 2,
        cost_estimate=cost(10 * seq * seq * width, 14 * seq * width, seq * seq * n_heads // 2),
        compiler_params=limit(40), name="attention_bwd",
    )(q_bf, k_bf, v_val, d_attn, lse_all, dep)


def out_kernel(a_ref, w_ref, x_ref, dep_ref, y_ref):
    y_ref[...] = (x_ref[...].astype(jnp.float32) + mm(a_ref[...], w_ref[...])).astype(jnp.bfloat16)


def out_call(attended, w_out, x_seq, dep):
    rows, width = x_seq.shape
    o_col = pl.BlockSpec((rows, N_BLK), lambda i: (0, i))
    return pl.pallas_call(
        out_kernel, grid=(width // N_BLK,),
        in_specs=[fixed(rows, width), pl.BlockSpec((width, N_BLK), lambda i: (0, i)), o_col, ANY_SPEC],
        out_specs=o_col, out_shape=bf_shape(rows, width),
        cost_estimate=cost(2 * rows * width * width, 2 * width * width + 6 * rows * width),
        compiler_params=limit(32), name="project_out",
    )(attended, w_out, x_seq, dep)


def head_grad_kernel(gy_ref, w_ref, dep_ref, out_ref):
    out_ref[...] = mm_nt(gy_ref[...], w_ref[...]).astype(jnp.bfloat16)


def head_grad_call(gy_seq, w_out, dep):
    rows, width = gy_seq.shape
    return pl.pallas_call(
        head_grad_kernel, grid=(width // N_BLK,),
        in_specs=[fixed(rows, width), pl.BlockSpec((N_BLK, width), lambda i: (i, 0)), ANY_SPEC],
        out_specs=pl.BlockSpec((rows, N_BLK), lambda i: (0, i)), out_shape=bf_shape(rows, width),
        cost_estimate=cost(2 * rows * width * width, 2 * width * width + 4 * rows * width),
        compiler_params=limit(32), name="head_grad",
    )(gy_seq, w_out, dep)


def copy_kernel(in_ref, dep_ref, out_ref):
    out_ref[...] = in_ref[...]


def copy_call(values, dep):
    blk = pl.BlockSpec((1,) + values.shape[1:], lambda i: (i, 0, 0))
    return pl.pallas_call(
        copy_kernel, grid=(values.shape[0],), in_specs=[blk, ANY_SPEC], out_specs=blk,
        out_shape=jax.ShapeDtypeStruct(values.shape, values.dtype),
        cost_estimate=cost(0, 4 * values.size), compiler_params=limit(16), name="store_rows",
    )(values, dep)


def hid_grad_kernel(dq_ref, dk_ref, dv_ref, wq_ref, wk_ref, wv_ref, dep_ref, out_ref):
    out_ref[...] = mm_nt(dq_ref[...], wq_ref[...]) + mm_nt(dk_ref[...], wk_ref[...]) + mm_nt(dv_ref[...], wv_ref[...])


def hid_grad_call(dq_raw, dk_raw, dv_bf, w_query, w_key, w_value, dep):
    rows, width = dq_raw.shape
    w_row = pl.BlockSpec((N_BLK, width), lambda i: (i, 0))
    return pl.pallas_call(
        hid_grad_kernel, grid=(width // N_BLK,),
        in_specs=[fixed(rows, width)] * 3 + [w_row] * 3 + [ANY_SPEC],
        out_specs=pl.BlockSpec((rows, N_BLK), lambda i: (0, i)), out_shape=f32_shape(rows, width),
        cost_estimate=cost(6 * rows * width * width, 6 * width * width + 10 * rows * width),
        compiler_params=limit(40), name="hidden_grad",
    )(dq_raw, dk_raw, dv_bf, w_query, w_key, w_value, dep)


def x_grad_kernel(dh_ref, x_ref, gy_ref, gain_ref, gx_ref, gsum_ref):
    x_f = x_ref[...].astype(jnp.float32)
    inv_rms = lax.rsqrt(jnp.mean(x_f * x_f, axis=-1, keepdims=True) + NORM_EPS)
    hat = x_f * inv_rms
    d_hid = dh_ref[...]

    @pl.when(pl.program_id(0) == 0)
    def _():
        gsum_ref[...] = jnp.zeros_like(gsum_ref)

    gsum_ref[...] += jnp.sum(d_hid * hat, axis=0, keepdims=True)
    d_nrm = d_hid * gain_ref[...].astype(jnp.float32)
    d_x = inv_rms * (d_nrm - hat * jnp.mean(d_nrm * hat, axis=-1, keepdims=True))
    gx_ref[...] = (gy_ref[...].astype(jnp.float32) + d_x).astype(jnp.bfloat16)


def x_grad_call(d_hid, x_seq, gy_seq, gain):
    rows, width = x_seq.shape
    row_blk = pl.BlockSpec((128, width), lambda i: (i, 0))
    vec = pl.BlockSpec((1, width), lambda i: (0, 0))
    return pl.pallas_call(
        x_grad_kernel, grid=(rows // 128,),
        in_specs=[row_blk, row_blk, row_blk, vec], out_specs=[row_blk, vec],
        out_shape=[bf_shape(rows, width), f32_shape(1, width)],
        cost_estimate=cost(12 * rows * width, 10 * rows * width), compiler_params=limit(16), name="input_grad",
    )(d_hid, x_seq, gy_seq, gain.reshape(1, width))


def weight_kernel(idx_ref, la_ref, lb_ref, ra_ref, rb_ref, dep_ref, xl_ref, yr_ref, kl_ref, kr_ref):
    step = pl.program_id(0)
    y_bit, x_bit = step // 2, lax.rem(step, 2)
    half = kl_ref.shape[-1]
    for lo, (near, far, pick, slot) in ((0, (kl_ref, xl_ref, x_bit, y_bit)), (half, (kr_ref, yr_ref, y_bit, x_bit))):
        part = mm_tn(la_ref[...], ra_ref[:, lo:lo + half]) + mm_tn(lb_ref[...], rb_ref[:, lo:lo + half])

        @pl.when(pick == 0)
        def _():
            near[pl.ds(slot, 1)] = part[None]

        @pl.when(pick == 1)
        def _():
            far[pl.ds(slot, 1)] = part[None]


def weight_call(idx, left_mine, left_peer, right_mine, right_peer, dep):
    rows, width = left_mine.shape
    blk = width // 8
    left = pl.BlockSpec((rows, blk), lambda i, idx_ref: (0, idx_ref[i]))
    right = pl.BlockSpec((rows, width), lambda i, idx_ref: (0, 0), pipeline_mode=pl.Buffered(1))
    out = pl.BlockSpec((2, blk, width // 2), lambda i, idx_ref: (0, 0, 0))
    return pl.pallas_call(
        weight_kernel,
        grid_spec=pltpu.PrefetchScalarGridSpec(
            num_scalar_prefetch=1, grid=(4,),
            in_specs=[left, left, right, right, ANY_SPEC], out_specs=[out] * 4),
        out_shape=[f32_shape(2, blk, width // 2)] * 4,
        cost_estimate=cost(4 * rows * width * width // 2, 12 * rows * width + 2 * width * width),
        compiler_params=limit(48), name="weight_grad",
    )(idx, left_mine, left_peer, right_mine, right_peer, dep)


def merge_kernel(kl_ref, rl_ref, kr_ref, rr_ref, dep_ref, stay_l, away_l, stay_r, away_r):
    stay_l[...] = kl_ref[0] + rl_ref[0]
    away_l[...] = kl_ref[1] + rl_ref[1]
    stay_r[...] = kr_ref[0] + rr_ref[0]
    away_r[...] = kr_ref[1] + rr_ref[1]


def merge_call(keep_l, recv_l, keep_r, recv_r, dep):
    _, rows, cols = keep_l.shape
    inp = pl.BlockSpec((2, 64, cols), lambda i: (0, i, 0))
    out = pl.BlockSpec((64, cols), lambda i: (i, 0))
    return pl.pallas_call(
        merge_kernel, grid=(rows // 64,), in_specs=[inp] * 4 + [ANY_SPEC], out_specs=[out] * 4,
        out_shape=[f32_shape(rows, cols)] * 4,
        cost_estimate=cost(4 * rows * cols, 48 * rows * cols), compiler_params=limit(16), name="merge",
    )(keep_l, recv_l, keep_r, recv_r, dep)


def final_kernel(sl_ref, rl_ref, sr_ref, rr_ref, dep_ref, out_ref):
    half = sl_ref.shape[-1]
    out_ref[:, :half] = sl_ref[...] + rl_ref[...]
    out_ref[:, half:] = sr_ref[...] + rr_ref[...]


def final_call(stay_l, recv_l, stay_r, recv_r, dep):
    rows, cols = stay_l.shape
    inp = pl.BlockSpec((64, cols), lambda i: (i, 0))
    return pl.pallas_call(
        final_kernel, grid=(rows // 64,), in_specs=[inp] * 4 + [ANY_SPEC],
        out_specs=pl.BlockSpec((64, 2 * cols), lambda i: (i, 0)), out_shape=f32_shape(rows, 2 * cols),
        cost_estimate=cost(2 * rows * cols, 24 * rows * cols), compiler_params=limit(16), name="final_add",
    )(stay_l, recv_l, stay_r, recv_r, dep)


def unnorm_kernel(dq_ref, raw_ref, inv_ref, gain_ref, cos_ref, sin_ref, dep_ref, out_ref, gsum_ref, dn_s, hat_s):
    blk, width = raw_ref.shape
    cos_t, sin_t = cos_ref[...], -sin_ref[...]
    inv_rms = inv_ref[...]

    @pl.when(pl.program_id(0) == 0)
    def _():
        gsum_ref[...] = jnp.zeros_like(gsum_ref)

    acc = jnp.zeros((blk, HEAD_DIM), jnp.float32)
    for head in range(width // HEAD_DIM):
        cols = slice(head * HEAD_DIM, (head + 1) * HEAD_DIM)
        d_out = rotate(dq_ref[:, cols].astype(jnp.float32), cos_t, sin_t)
        hat = raw_ref[:, cols] * inv_rms
        gsum_ref[:, cols] += jnp.sum(d_out * hat, axis=0, keepdims=True)
        d_nrm = d_out * gain_ref[:, cols].astype(jnp.float32)
        acc += d_nrm * hat
        dn_s[:, cols] = d_nrm
        hat_s[:, cols] = hat
    mean = jnp.sum(acc, axis=-1, keepdims=True) * (1.0 / width)
    out_ref[...] = (inv_rms * (dn_s[...] - hat_s[...] * mean)).astype(jnp.bfloat16)


def unnorm_call(d_rot, raw, inv_rms, gain, cos_t, sin_t, dep):
    rows, width = raw.shape
    blk = 128
    row_blk = pl.BlockSpec((blk, width), lambda i: (i, 0))
    vec = pl.BlockSpec((1, width), lambda i: (0, 0))
    tab = pl.BlockSpec((blk, HEAD_DIM), lambda i: (i, 0))
    return pl.pallas_call(
        unnorm_kernel, grid=(rows // blk,),
        in_specs=[row_blk, row_blk, pl.BlockSpec((blk, 1), lambda i: (i, 0)), vec, tab, tab, ANY_SPEC],
        out_specs=[row_blk, vec],
        out_shape=[jax.ShapeDtypeStruct((rows, width), jnp.bfloat16), jax.ShapeDtypeStruct((1, width), jnp.float32)],
        scratch_shapes=[pltpu.VMEM((blk, width), jnp.float32)] * 2,
        cost_estimate=pl.CostEstimate(flops=rows * width * 12, bytes_accessed=rows * width * 8, transcendentals=0),
        compiler_params=limit(16), name="unnorm",
    )(d_rot, raw, inv_rms, gain.reshape(1, width), cos_t, sin_t, dep)


def solution(mesh):
    n_sp = mesh.shape['sp']
    swap = functools.partial(lax.all_to_all, axis_name='sp', split_axis=0, concat_axis=0, tiled=True)

    def flip(values, bit):
        return lax.ppermute(values, 'sp', [(dev, dev ^ bit) for dev in range(n_sp)])

    def block_step(x_loc, grad_y, positions, g_norm, w_query, w_key, w_value, w_out, g_query, g_key):
        n_batch, loc_len, width = x_loc.shape
        seq = n_sp * loc_len
        rows = width // n_sp
        me = lax.axis_index('sp')
        idx = me ^ jnp.array([0, 2, 4, 6], jnp.int32)

        def first_hop(parts):
            far_l, far_r, near_l, near_r = parts
            return near_l, flip(far_l, 2), near_r, flip(far_r, 4)

        def second_hop(parts):
            stay_l, away_l, stay_r, away_r = parts
            return stay_l, flip(away_l, 4), stay_r, flip(away_r, 2)

        cos_t, sin_t = rope_tables(swap(positions).reshape(seq))
        x_seq = swap(x_loc).reshape(seq, width)
        gy_seq = swap(grad_y).reshape(seq, width)
        hidden, q_raw, k_raw, v_val, q_inv, k_inv = qkv_call(x_seq, g_norm, w_query, w_key, w_value)
        attended, q_bf, k_bf, lse_all = attn_fwd_call(q_raw, k_raw, v_val, q_inv, k_inv, g_query, g_key, cos_t, sin_t)
        a_peer = flip(attended, 1)
        gy_peer = flip(gy_seq, 1)
        hid_peer = flip(hidden, 1)
        y_seq = out_call(attended, w_out, x_seq, attended)
        y_swap = swap(y_seq.reshape(n_batch, loc_len, width))
        part_o = weight_call(idx, attended, a_peer, gy_seq, gy_peer, y_seq)
        hop_o = first_hop(part_o)
        d_attn = head_grad_call(gy_seq, w_out, part_o[2])
        dq_bf, dk_bf, dv_bf = attn_bwd_call(q_bf, k_bf, v_val, d_attn, lse_all, y_seq)
        dv_peer = flip(dv_bf, 1)
        mrg_o = merge_call(*hop_o, dv_bf)
        fin_o = second_hop(mrg_o)
        part_v = weight_call(idx, hidden, hid_peer, dv_bf, dv_peer, mrg_o[0])
        hop_v = first_hop(part_v)
        dq_raw, gq_sum = unnorm_call(dq_bf, q_raw, q_inv, g_query, cos_t, sin_t, part_v[2])
        dq_peer = flip(dq_raw, 1)
        dk_raw, gk_sum = unnorm_call(dk_bf, k_raw, k_inv, g_key, cos_t, sin_t, dq_raw)
        dk_peer = flip(dk_raw, 1)
        part_q = weight_call(idx, hidden, hid_peer, dq_raw, dq_peer, dk_raw)
        hop_q = first_hop(part_q)
        part_k = weight_call(idx, hidden, hid_peer, dk_raw, dk_peer, part_q[2])
        hop_k = first_hop(part_k)
        d_hid = hid_grad_call(dq_raw, dk_raw, dv_bf, w_query, w_key, w_value, part_k[2])
        gx_seq, gn_sum = x_grad_call(d_hid, x_seq, gy_seq, g_norm)
        gx_swap = swap(gx_seq.reshape(n_batch, loc_len, width))
        gains = jnp.concatenate([gn_sum, gq_sum, gk_sum], axis=0)
        cut = [lax.dynamic_slice_in_dim(gains, (me ^ off) * rows, rows, axis=1) for off in range(n_sp)]
        gain_rows = sum((flip(cut[off], off) for off in range(1, n_sp)), cut[0])
        mrg_v = merge_call(*hop_v, gx_seq)
        fin_v = second_hop(mrg_v)
        mrg_q = merge_call(*hop_q, mrg_v[0])
        fin_q = second_hop(mrg_q)
        y_out = copy_call(y_swap, mrg_q[0])
        mrg_k = merge_call(*hop_k, y_out)
        fin_k = second_hop(mrg_k)
        grad_wo = final_call(*fin_o, mrg_k[0])
        grad_x = copy_call(gx_swap, grad_wo)
        grad_wv = final_call(*fin_v, grad_x)
        grad_wq = final_call(*fin_q, grad_wv)
        grad_wk = final_call(*fin_k, grad_wq)
        return (y_out, grad_x, gain_rows[0], grad_wq, grad_wk, grad_wv, grad_wo, gain_rows[1], gain_rows[2])

    seq_spec = P('dp', 'sp', None)
    mat_rep = P(None, None)
    vec_rep = P(None)
    row_spec = P(('dp', 'sp'), None)
    vec_spec = P(('dp', 'sp'))
    return jax.shard_map(block_step, mesh=mesh, in_specs=(seq_spec, seq_spec, P('dp', 'sp'), vec_rep, mat_rep, mat_rep, mat_rep, mat_rep, vec_rep, vec_rep), out_specs=(seq_spec, seq_spec, vec_spec, row_spec, row_spec, row_spec, row_spec, vec_spec, vec_spec), check_vma=False)
```

time: 1700 us -> 706 us (0.42)
  matrix products: 816 us -> 0 us
  Pallas kernels: 0 us -> 348 us
  blocking collectives: 229 us -> 63.6 us
  local copies, waits for them, and re-layouts: 160 us -> 2.42 us
  other arithmetic: 151 us -> 3.78 us
  waiting for transfers between devices: 291 us -> 245 us
    dot_general x68 -> x0, matrix products: 816 us -> none  [the longest x8 204 us: block_step(): jnp.einsum('bhqk,bqhd->bkhd', ds_bf, q_blk, preferred_element_type=jnp.fl...]
    pallas_call x0 -> x23, Pallas kernels: none -> 348 us  [the longest x4 74.3 us: weight_call(): pl.pallas_call(weight_kernel, grid_spec=pltpu.PrefetchScalarGridSpec(num_...]
    ppermute x0 -> x29, waiting for transfers between devices: none -> 245 us  [flip(): return lax.ppermute(values, 'sp', [(dev, dev ^ bit) for dev in range(n_sp)])]
    reduce_scatter x4 -> x0, waiting for transfers between devices: 148 us -> none  [sum_rows(): return lax.psum_scatter(partial_sum, 'sp', scatter_dimension=0, tiled=True)]
    all_to_all x5 -> x3, waiting for transfers between devices: 143 us -> 0.01 us  [the longest x1 0.01 us: block_step(): y_swap = swap(y_seq.reshape(n_batch, loc_len, width))]
    all_to_all x3 -> x2, blocking collectives: 205 us -> 63.6 us  [the longest x1 53.5 us: block_step(): x_seq = swap(x_loc).reshape(seq, width)]
    reduce_sum x11 -> x0, other arithmetic: 41.4 us -> none  [the longest x8 18.5 us: block_step(): row_sum = jnp.sum(exp_scores, axis=-1, keepdims=True)]
    convert_element_type x6 -> x0, other arithmetic: 33.1 us -> none  [the longest x1 14.4 us: block_back(): dk_bf = dk_raw.astype(jnp.bfloat16)]
  transfers between devices with their start and end apart: 9 -> 32, of which waited for: 6 -> 9; matrix products, arithmetic and copies ran while one was open for 20% -> 1% of each run, Pallas kernels for 0% -> 45%
where the time goes in v1:
time: 706 us; the launch traced here: 704 us
  Pallas kernels  348 us (49%)
  waiting for transfers between devices  245 us (35%)
  blocking collectives  63.6 us (9%)
  starting transfers between devices  40.5 us (6%)
    ppermute x29, waiting for transfers between devices, flip(): return lax.ppermute(values, 'sp', [(dev, dev ^ bit) for dev in range(n_sp)])  245 us
    pallas_call x4, Pallas kernels, weight_call(): pl.pallas_call(weight_kernel, grid_spec=pltpu.PrefetchScalarGridSpec(num_...  74.3 us
    all_to_all x1, blocking collectives, block_step(): x_seq = swap(x_loc).reshape(seq, width)  53.5 us
    pallas_call x1, Pallas kernels, attn_bwd_call(): pl.pallas_call(attn_bwd_kernel, grid=(n_heads,), in_specs=[head, head, he...  47.9 us
    pallas_call x1, Pallas kernels, attn_fwd_call(): pl.pallas_call(attn_fwd_kernel, grid=(n_heads,), in_specs=[head, head, he...  38.2 us
    pallas_call x1, Pallas kernels, qkv_call(): pl.pallas_call(qkv_kernel, grid=(width // N_BLK,), in_specs=[fixed(rows,...  36.6 us
    pallas_call x1, Pallas kernels, hid_grad_call(): pl.pallas_call(hid_grad_kernel, grid=(width // N_BLK,), in_specs=[fixed(r...  34.7 us
    ppermute x29, starting transfers between devices, flip(): return lax.ppermute(values, 'sp', [(dev, dev ^ bit) for dev in range(n_sp)])  26.3 us
  transfers between devices with their start and end apart: 32, of which 9 were waited for; matrix products, arithmetic and copies ran while one was open for 1% of the time, Pallas kernels for 45%

profile of v1, /device:TPU:0, one launch (start us, length us, event | category | flops | bytes accessed | tf_op | source)
XLA Modules:
  0.0 703.7 jit_solution(3968233903998518240)
XLA Ops:
  0.6 10.0 %all_to_all.29 = s32[8,1,128]{2,1,0:T(1,128)S(1)} all-to-all(s32[8,1,128]{2,1,0:T(1,128)} %bitcast.15), channel_id=1, replica_groups=mesh['dp'=2,'sp'=8] {'sp'}, dimensions={0} | all-to-all | bytes 8192 | tf_op jit(solution)/shard_map/all_to_all | solution.py:423
  10.7 53.5 %all_to_all.30 = bf16[8,128,2048]{2,1,0:T(8,128)(2,1)} all-to-all(bf16[8,128,2048]{2,1,0:T(8,128)(2,1)} %param.11), channel_id=1, replica_groups=mesh['dp'=2,'sp'=8] {'sp'}, dimensions={0} | all-to-all | bytes 8388608 | tf_op jit(solution)/shard_map/all_to_all | solution.py:424
  64.2 4.7 all-to-all-start.3
  74.0 36.6 %qkv.1 = (bf16[1024,2048]{1,0:T(8,128)(2,1)}, f32[1024,2048]{1,0:T(8,128)}, f32[1024,2048]{1,0:T(8,128)}, bf16[1024,2048]{1,0:T(8,128)(2,1)}, f32[1024,1]{1,0:T(8,128)}, /*index=5*/f32[1024,1]{1,0:T(8,128)}) custom-call(bf16[1024,2048]{1,0:T(8,128)(2,1)} %bitcast.10, bf16[1,2048]{1,0:T(2,128)(2,1)} %reshape.59.gain_ref, bf16[2048,2048]{1,0:T(8,128)(2,1)} %wq_ref.3, ...), custom_call_target="tpu_custom_call" | custom-call | flops 25769803776 | bytes 54525952 | tf_op jit(solution)/shard_map/qkv/pallas_call | solution.py:101
  110.5 38.2 %attention_fwd.1 = (bf16[1024,2048]{1,0:T(8,128)(2,1)}, bf16[1024,2048]{1,0:T(8,128)(2,1)}, bf16[1024,2048]{1,0:T(8,128)(2,1)}, f32[16,1,1024]{2,1,0:T(1,128)}) custom-call(f32[1024,2048]{1,0:T(8,128)} %get-tuple-element.60.q1_ref.raw_ref, f32[1024,2048]{1,0:T(8,128)} %get-tuple-element.61.k1_ref.raw_ref, bf16[1024,2048]{1,0:T(8,128)(2,1)} %get-tuple-element.62.v_ref, ...), custom_call_target="tpu_custom_call" | custom-call | flops 8589934592 | bytes 33554432 | tf_op jit(solution)/shard_map/attention_fwd/pallas_call | solution.py:182
  150.2 14.7 %project_out.1.dep_ref = bf16[1024,2048]{1,0:T(8,128)(2,1)} custom-call(bf16[1024,2048]{1,0:T(8,128)(2,1)} %get-tuple-element.65.a_ref.dep_ref.la_ref, bf16[2048,2048]{1,0:T(8,128)(2,1)} %w_ref.3, bf16[1024,2048]{1,0:T(8,128)(2,1)} %bitcast.11, bf16[1024,2048]{1,0:T(8,128)(2,1)} %get-tuple-element.65.a_ref.dep_ref.la_ref), custom_call_target="tpu_custom_call" | custom-call | flops 8589934592 | bytes 20971520 | tf_op jit(solution)/shard_map/project_out/pallas_call | solution.py:213
  164.9 18.6 %weight_grad.4 = (f32[2,256,1024]{2,1,0:T(8,128)}, f32[2,256,1024]{2,1,0:T(8,128)}, f32[2,256,1024]{2,1,0:T(8,128)}, f32[2,256,1024]{2,1,0:T(8,128)}) custom-call(s32[4]{0:T(128)} %multiply_xor_fusion.idx_ref, bf16[1024,2048]{1,0:T(8,128)(2,1)} %get-tuple-element.65.a_ref.dep_ref.la_ref, bf16[1024,2048]{1,0:T(8,128)(2,1)} %collective-permute-done.1.lb_ref, ...), custom_call_target="tpu_custom_call" | custom-call | flops 8589934592 | bytes 33554432 | tf_op jit(solution)/shard_map/weight_grad/pallas_call | solution.py:316
  183.5 14.2 %head_grad.1.do_ref = bf16[1024,2048]{1,0:T(8,128)(2,1)} custom-call(bf16[1024,2048]{1,0:T(8,128)(2,1)} %bitcast.4.ra_ref.gy_ref, bf16[2048,2048]{1,0:T(8,128)(2,1)} %w_ref.3, f32[2,256,1024]{2,1,0:T(8,128)} %get-tuple-element.69.dep_ref.kl_ref), custom_call_target="tpu_custom_call" | custom-call | flops 8589934592 | bytes 16777216 | tf_op jit(solution)/shard_map/head_grad/pallas_call | solution.py:228
  197.7 47.9 %attention_bwd.1 = (bf16[1024,2048]{1,0:T(8,128)(2,1)}, bf16[1024,2048]{1,0:T(8,128)(2,1)}, bf16[1024,2048]{1,0:T(8,128)(2,1)}) custom-call(bf16[1024,2048]{1,0:T(8,128)(2,1)} %get-tuple-element.67.q_ref, bf16[1024,2048]{1,0:T(8,128)(2,1)} %get-tuple-element.68.k_ref, bf16[1024,2048]{1,0:T(8,128)(2,1)} %get-tuple-element.62.v_ref, ...), custom_call_target="tpu_custom_call" | custom-call | flops 21474836480 | bytes 29360128 | tf_op jit(solution)/shard_map/attention_bwd/pallas_call | solution.py:196
  249.1 44.9 %collective-permute-done.4.rl_ref = f32[2,256,1024]{2,1,0:T(8,128)} collective-permute-done((f32[2,256,1024]{2,1,0:T(8,128)}, f32[2,256,1024]{2,1,0:T(8,128)}, u32[]{:S(2)}, u32[]{:S(2)}) %collective-permute-start.4) | collective-permute-done | bytes 2097184 | tf_op jit(solution)/shard_map/ppermute | solution.py:406
  295.3 5.7 merge.4
  301.0 18.6 %weight_grad.5 = (f32[2,256,1024]{2,1,0:T(8,128)}, f32[2,256,1024]{2,1,0:T(8,128)}, f32[2,256,1024]{2,1,0:T(8,128)}, f32[2,256,1024]{2,1,0:T(8,128)}) custom-call(s32[4]{0:T(128)} %multiply_xor_fusion.idx_ref, bf16[1024,2048]{1,0:T(8,128)(2,1)} %get-tuple-element.66.la_ref, bf16[1024,2048]{1,0:T(8,128)(2,1)} %collective-permute-done.lb_ref, ...), custom_call_target="tpu_custom_call" | custom-call | flops 8589934592 | bytes 33554432 | tf_op jit(solution)/shard_map/weight_grad/pallas_call | solution.py:316
  319.6 11.1 %unnorm.2 = (bf16[1024,2048]{1,0:T(8,128)(2,1)}, f32[1,2048]{1,0:T(1,128)}) custom-call(bf16[1024,2048]{1,0:T(8,128)(2,1)} %get-tuple-element.71.dq_ref, f32[1024,2048]{1,0:T(8,128)} %get-tuple-element.60.q1_ref.raw_ref, f32[1024,1]{1,0:T(8,128)} %get-tuple-element.63.qinv_ref.inv_ref, bf16[1,2048]{1,0:T(2,128)(2,1)} %reshape.60.gq_ref.gain_ref, ...), custom_call_target="tpu_custom_call" | custom-call | flops 25165824 | bytes 16777216 | tf_op jit(solution)/shard_map/unnorm/pallas_call | solution.py:390
  330.7 11.1 %unnorm.3 = (bf16[1024,2048]{1,0:T(8,128)(2,1)}, f32[1,2048]{1,0:T(1,128)}) custom-call(bf16[1024,2048]{1,0:T(8,128)(2,1)} %get-tuple-element.79.dq_ref, f32[1024,2048]{1,0:T(8,128)} %get-tuple-element.61.k1_ref.raw_ref, f32[1024,1]{1,0:T(8,128)} %get-tuple-element.64.kinv_ref.inv_ref, bf16[1,2048]{1,0:T(2,128)(2,1)} %reshape.61.gk_ref.gain_ref, ...), custom_call_target="tpu_custom_call" | custom-call | flops 25165824 | bytes 16777216 | tf_op jit(solution)/shard_map/unnorm/pallas_call | solution.py:390
  342.3 4.8 all-to-all-start.2
  351.2 18.6 %weight_grad.6 = (f32[2,256,1024]{2,1,0:T(8,128)}, f32[2,256,1024]{2,1,0:T(8,128)}, f32[2,256,1024]{2,1,0:T(8,128)}, f32[2,256,1024]{2,1,0:T(8,128)}) custom-call(s32[4]{0:T(128)} %multiply_xor_fusion.idx_ref, bf16[1024,2048]{1,0:T(8,128)(2,1)} %get-tuple-element.66.la_ref, bf16[1024,2048]{1,0:T(8,128)(2,1)} %collective-permute-done.lb_ref, ...), custom_call_target="tpu_custom_call" | custom-call | flops 8589934592 | bytes 33554432 | tf_op jit(solution)/shard_map/weight_grad/pallas_call | solution.py:316
  369.8 18.6 %weight_grad.7 = (f32[2,256,1024]{2,1,0:T(8,128)}, f32[2,256,1024]{2,1,0:T(8,128)}, f32[2,256,1024]{2,1,0:T(8,128)}, f32[2,256,1024]{2,1,0:T(8,128)}) custom-call(s32[4]{0:T(128)} %multiply_xor_fusion.idx_ref, bf16[1024,2048]{1,0:T(8,128)(2,1)} %get-tuple-element.66.la_ref, bf16[1024,2048]{1,0:T(8,128)(2,1)} %collective-permute-done.lb_ref, ...), custom_call_target="tpu_custom_call" | custom-call | flops 8589934592 | bytes 33554432 | tf_op jit(solution)/shard_map/weight_grad/pallas_call | solution.py:316
  388.3 34.7 %hidden_grad.1.dh_ref = f32[1024,2048]{1,0:T(8,128)} custom-call(bf16[1024,2048]{1,0:T(8,128)(2,1)} %get-tuple-element.78.dep_ref.ra_ref.dq_ref, bf16[1024,2048]{1,0:T(8,128)(2,1)} %get-tuple-element.80.dep_ref.ra_ref.dk_ref, bf16[1024,2048]{1,0:T(8,128)(2,1)} %get-tuple-element.72.dep_ref.ra_ref.dv_ref, bf16[2048,2048]{1,0:T(8,128)(2,1)} %wq_ref.3, ...), custom_call_target="tpu_custom_call" | custom-call | flops 25769803776 | bytes 46137344 | tf_op jit(solution)/shard_map/hidden_grad/pallas_call | solution.py:257
  423.0 12.5 %input_grad.1 = (bf16[1024,2048]{1,0:T(8,128)(2,1)}, f32[1,2048]{1,0:T(1,128)}) custom-call(f32[1024,2048]{1,0:T(8,128)} %hidden_grad.1.dh_ref, bf16[1024,2048]{1,0:T(8,128)(2,1)} %bitcast.12, bf16[1024,2048]{1,0:T(8,128)(2,1)} %bitcast.4.ra_ref.gy_ref, bf16[1,2048]{1,0:T(2,128)(2,1)} %reshape.59.gain_ref), custom_call_target="tpu_custom_call" | custom-call | flops 25165824 | bytes 20971520 | tf_op jit(solution)/shard_map/input_grad/pallas_call | solution.py:286
  435.6 4.7 all-to-all-start.4
  444.2 18.8 %collective-permute-done.10.rr_ref = f32[2,256,1024]{2,1,0:T(8,128)} collective-permute-done((f32[2,256,1024]{2,1,0:T(8,128)}, f32[2,256,1024]{2,1,0:T(8,128)}, u32[]{:S(2)}, u32[]{:S(2)}) %collective-permute-start.10) | collective-permute-done | bytes 2097184 | tf_op jit(solution)/shard_map/ppermute | solution.py:406
  466.0 131.5 %collective-permute-done.17 = f32[3,256]{1,0:T(4,128)S(1)} collective-permute-done((f32[3,256]{1,0:T(4,128)S(1)}, f32[3,256]{1,0:T(4,128)S(1)}, u32[]{:S(2)}, u32[]{:S(2)}) %collective-permute-start.17) | collective-permute-done | bytes 3104 | tf_op jit(solution)/shard_map/ppermute | solution.py:406
  597.4 5.7 merge.5
  609.1 5.7 merge.6
  614.8 6.6 store_rows.2.dep_ref
  621.4 5.7 merge.7
  639.7 6.6 store_rows.3.dep_ref
  646.3 9.4 %collective-permute-done.26.rr_ref = f32[256,1024]{1,0:T(8,128)} collective-permute-done((f32[256,1024]{1,0:T(8,128)}, f32[256,1024]{1,0:T(8,128)}, u32[]{:S(2)}, u32[]{:S(2)}) %collective-permute-start.26) | collective-permute-done | bytes 1048608 | tf_op jit(solution)/shard_map/ppermute | solution.py:406
  655.7 4.1 final_add.5.dep_ref
  659.8 18.3 %collective-permute-done.24.rr_ref = f32[256,1024]{1,0:T(8,128)} collective-permute-done((f32[256,1024]{1,0:T(8,128)}, f32[256,1024]{1,0:T(8,128)}, u32[]{:S(2)}, u32[]{:S(2)}) %collective-permute-start.24) | collective-permute-done | bytes 1048608 | tf_op jit(solution)/shard_map/ppermute | solution.py:406
  678.1 4.1 final_add.6.dep_ref
  682.3 17.3 %collective-permute-done.28.rr_ref = f32[256,1024]{1,0:T(8,128)} collective-permute-done((f32[256,1024]{1,0:T(8,128)}, f32[256,1024]{1,0:T(8,128)}, u32[]{:S(2)}, u32[]{:S(2)}) %collective-permute-start.28) | collective-permute-done | bytes 1048608 | tf_op jit(solution)/shard_map/ppermute | solution.py:406
  (81 shorter events, 45.6 us)
Async XLA Ops:
  64.2 85.0 %all-to-all-start.3 = ((bf16[8,128,2048]{2,1,0:T(8,128)(2,1)}), bf16[8,128,2048]{2,1,0:T(8,128)(2,1)}, u32[]{:S(2)}, u32[]{:S(2)}) async-start(bf16[8,128,2048]{2,1,0:T(8,128)(2,1)} %param.12), calls=%async_computation.3 | async-start | bytes 8388608 | tf_op jit(solution)/shard_map/all_to_all | solution.py:425
  148.7 16.2 %collective-permute-start.1 = (bf16[1024,2048]{1,0:T(8,128)(2,1)}, bf16[1024,2048]{1,0:T(8,128)(2,1)}, u32[]{:S(2)}, u32[]{:S(2)}) collective-permute-start(bf16[1024,2048]{1,0:T(8,128)(2,1)} %get-tuple-element.65.a_ref.dep_ref.la_ref), channel_id=1, source_target_pairs={{0,1},{1,0},{2,3},{3,2},{4,5},{5,4},{6,7},{7,6},{8,9},{9,8},{10,11... | collective-permute-start | bytes 12582920 | tf_op jit(solution)/shard_map/ppermute | solution.py:406
  149.2 15.8 %collective-permute-start.2 = (bf16[1024,2048]{1,0:T(8,128)(2,1)}, bf16[1024,2048]{1,0:T(8,128)(2,1)}, u32[]{:S(2)}, u32[]{:S(2)}) collective-permute-start(bf16[1024,2048]{1,0:T(8,128)(2,1)} %bitcast.4.ra_ref.gy_ref), channel_id=1, source_target_pairs={{0,1},{1,0},{2,3},{3,2},{4,5},{5,4},{6,7},{7,6},{8,9},{9,8},{10,11... | collective-permute-start | bytes 12582920 | tf_op jit(solution)/shard_map/ppermute | solution.py:406
  149.8 151.2 %collective-permute-start = (bf16[1024,2048]{1,0:T(8,128)(2,1)}, bf16[1024,2048]{1,0:T(8,128)(2,1)}, u32[]{:S(2)}, u32[]{:S(2)}) collective-permute-start(bf16[1024,2048]{1,0:T(8,128)(2,1)} %get-tuple-element.66.la_ref), channel_id=1, source_target_pairs={{0,1},{1,0},{2,3},{3,2},{4,5},{5,4},{6,7},{7,6},{8,9},{9,8},{10,11... | collective-permute-start | bytes 12582920 | tf_op jit(solution)/shard_map/ppermute | solution.py:406
  245.5 55.4 %collective-permute-start.3 = (bf16[1024,2048]{1,0:T(8,128)(2,1)}, bf16[1024,2048]{1,0:T(8,128)(2,1)}, u32[]{:S(2)}, u32[]{:S(2)}) collective-permute-start(bf16[1024,2048]{1,0:T(8,128)(2,1)} %get-tuple-element.72.dep_ref.ra_ref.dv_ref), channel_id=1, source_target_pairs={{0,1},{1,0},{2,3},{3,2},{4,5},{5,4},{6,7},{7,6},{8,9},{9,8},{10,11... | collective-permute-start | bytes 12582920 | tf_op jit(solution)/shard_map/ppermute | solution.py:406
  245.7 48.2 %collective-permute-start.4 = (f32[2,256,1024]{2,1,0:T(8,128)}, f32[2,256,1024]{2,1,0:T(8,128)}, u32[]{:S(2)}, u32[]{:S(2)}) collective-permute-start(f32[2,256,1024]{2,1,0:T(8,128)} %get-tuple-element.73), channel_id=1, source_target_pairs={{0,2},{1,3},{2,0},{3,1},{4,6},{5,7},{6,4},{7,5},{8,10},{9,11},{10,... | collective-permute-start | bytes 6291464 | tf_op jit(solution)/shard_map/ppermute | solution.py:406
  247.6 47.7 %collective-permute-start.5 = (f32[2,256,1024]{2,1,0:T(8,128)}, f32[2,256,1024]{2,1,0:T(8,128)}, u32[]{:S(2)}, u32[]{:S(2)}) collective-permute-start(f32[2,256,1024]{2,1,0:T(8,128)} %get-tuple-element.75), channel_id=1, source_target_pairs={{0,4},{1,5},{2,6},{3,7},{4,0},{5,1},{6,2},{7,3},{8,12},{9,13},{10,... | collective-permute-start | bytes 6291464 | tf_op jit(solution)/shard_map/ppermute | solution.py:406
  330.7 20.1 %collective-permute-start.6 = (bf16[1024,2048]{1,0:T(8,128)(2,1)}, bf16[1024,2048]{1,0:T(8,128)(2,1)}, u32[]{:S(2)}, u32[]{:S(2)}) collective-permute-start(bf16[1024,2048]{1,0:T(8,128)(2,1)} %get-tuple-element.78.dep_ref.ra_ref.dq_ref), channel_id=1, source_target_pairs={{0,1},{1,0},{2,3},{3,2},{4,5},{5,4},{6,7},{7,6},{8,9},{9,8},{10,11... | collective-permute-start | bytes 12582920 | tf_op jit(solution)/shard_map/ppermute | solution.py:406
  341.8 28.0 %collective-permute-start.11 = (bf16[1024,2048]{1,0:T(8,128)(2,1)}, bf16[1024,2048]{1,0:T(8,128)(2,1)}, u32[]{:S(2)}, u32[]{:S(2)}) collective-permute-start(bf16[1024,2048]{1,0:T(8,128)(2,1)} %get-tuple-element.80.dep_ref.ra_ref.dk_ref), channel_id=1, source_target_pairs={{0,1},{1,0},{2,3},{3,2},{4,5},{5,4},{6,7},{7,6},{8,9},{9,8},{10,11... | collective-permute-start | bytes 12582920 | tf_op jit(solution)/shard_map/ppermute | solution.py:406
  342.3 93.2 %all-to-all-start.2 = ((bf16[8,128,2048]{2,1,0:T(8,128)(2,1)}), bf16[8,128,2048]{2,1,0:T(8,128)(2,1)}, u32[]{:S(2)}, u32[]{:S(2)}) async-start(bf16[8,128,2048]{2,1,0:T(8,128)(2,1)} %bitcast.13), calls=%async_computation.2 | async-start | bytes 8388608 | tf_op jit(solution)/shard_map/all_to_all | solution.py:432
  347.1 95.1 %collective-permute-start.12 = (f32[256,1024]{1,0:T(8,128)}, f32[256,1024]{1,0:T(8,128)}, u32[]{:S(2)}, u32[]{:S(2)}) collective-permute-start(f32[256,1024]{1,0:T(8,128)} %get-tuple-element.92), channel_id=1, source_target_pairs={{0,4},{1,5},{2,6},{3,7},{4,0},{5,1},{6,2},{7,3},{8,12},{9,13},{10,... | collective-permute-start | bytes 3145736 | tf_op jit(solution)/shard_map/ppermute | solution.py:406
  348.8 94.9 %collective-permute-start.13 = (f32[256,1024]{1,0:T(8,128)}, f32[256,1024]{1,0:T(8,128)}, u32[]{:S(2)}, u32[]{:S(2)}) collective-permute-start(f32[256,1024]{1,0:T(8,128)} %get-tuple-element.94), channel_id=1, source_target_pairs={{0,2},{1,3},{2,0},{3,1},{4,6},{5,7},{6,4},{7,5},{8,10},{9,11},{10,... | collective-permute-start | bytes 3145736 | tf_op jit(solution)/shard_map/ppermute | solution.py:406
  350.2 112.7 %collective-permute-start.10 = (f32[2,256,1024]{2,1,0:T(8,128)}, f32[2,256,1024]{2,1,0:T(8,128)}, u32[]{:S(2)}, u32[]{:S(2)}) collective-permute-start(f32[2,256,1024]{2,1,0:T(8,128)} %get-tuple-element.87), channel_id=1, source_target_pairs={{0,4},{1,5},{2,6},{3,7},{4,0},{5,1},{6,2},{7,3},{8,12},{9,13},{10,... | collective-permute-start | bytes 6291464 | tf_op jit(solution)/shard_map/ppermute | solution.py:406
  350.8 112.6 %collective-permute-start.9 = (f32[2,256,1024]{2,1,0:T(8,128)}, f32[2,256,1024]{2,1,0:T(8,128)}, u32[]{:S(2)}, u32[]{:S(2)}) collective-permute-start(f32[2,256,1024]{2,1,0:T(8,128)} %get-tuple-element.85), channel_id=1, source_target_pairs={{0,2},{1,3},{2,0},{3,1},{4,6},{5,7},{6,4},{7,5},{8,10},{9,11},{10,... | collective-permute-start | bytes 6291464 | tf_op jit(solution)/shard_map/ppermute | solution.py:406
  435.6 204.2 %all-to-all-start.4 = ((bf16[8,128,2048]{2,1,0:T(8,128)(2,1)}), bf16[8,128,2048]{2,1,0:T(8,128)(2,1)}, u32[]{:S(2)}, u32[]{:S(2)}) async-start(bf16[8,128,2048]{2,1,0:T(8,128)(2,1)} %bitcast.9), calls=%async_computation.4 | async-start | bytes 8388608 | tf_op jit(solution)/shard_map/all_to_all | solution.py:452
  440.3 164.4 %collective-permute-start.7 = (f32[2,256,1024]{2,1,0:T(8,128)}, f32[2,256,1024]{2,1,0:T(8,128)}, u32[]{:S(2)}, u32[]{:S(2)}) collective-permute-start(f32[2,256,1024]{2,1,0:T(8,128)} %get-tuple-element.82), channel_id=1, source_target_pairs={{0,2},{1,3},{2,0},{3,1},{4,6},{5,7},{6,4},{7,5},{8,10},{9,11},{10,... | collective-permute-start | bytes 6291464 | tf_op jit(solution)/shard_map/ppermute | solution.py:406
  442.2 163.1 %collective-permute-start.8 = (f32[2,256,1024]{2,1,0:T(8,128)}, f32[2,256,1024]{2,1,0:T(8,128)}, u32[]{:S(2)}, u32[]{:S(2)}) collective-permute-start(f32[2,256,1024]{2,1,0:T(8,128)} %get-tuple-element.84), channel_id=1, source_target_pairs={{0,4},{1,5},{2,6},{3,7},{4,0},{5,1},{6,2},{7,3},{8,12},{9,13},{10,... | collective-permute-start | bytes 6291464 | tf_op jit(solution)/shard_map/ppermute | solution.py:406
  443.7 162.7 %collective-permute-start.14 = (f32[2,256,1024]{2,1,0:T(8,128)}, f32[2,256,1024]{2,1,0:T(8,128)}, u32[]{:S(2)}, u32[]{:S(2)}) collective-permute-start(f32[2,256,1024]{2,1,0:T(8,128)} %get-tuple-element.95), channel_id=1, source_target_pairs={{0,2},{1,3},{2,0},{3,1},{4,6},{5,7},{6,4},{7,5},{8,10},{9,11},{10,... | collective-permute-start | bytes 6291464 | tf_op jit(solution)/shard_map/ppermute | solution.py:406
  463.0 144.9 %collective-permute-start.15 = (f32[2,256,1024]{2,1,0:T(8,128)}, f32[2,256,1024]{2,1,0:T(8,128)}, u32[]{:S(2)}, u32[]{:S(2)}) collective-permute-start(f32[2,256,1024]{2,1,0:T(8,128)} %get-tuple-element.97), channel_id=1, source_target_pairs={{0,4},{1,5},{2,6},{3,7},{4,0},{5,1},{6,2},{7,3},{8,12},{9,13},{10,... | collective-permute-start | bytes 6291464 | tf_op jit(solution)/shard_map/ppermute | solution.py:406
  463.3 1.2 collective-permute-start.16
  464.5 132.9 %collective-permute-start.17 = (f32[3,256]{1,0:T(4,128)S(1)}, f32[3,256]{1,0:T(4,128)S(1)}, u32[]{:S(2)}, u32[]{:S(2)}) collective-permute-start(f32[3,256]{1,0:T(4,128)S(1)} %get-tuple-element.117), channel_id=1, source_target_pairs={{0,2},{1,3},{2,0},{3,1},{4,6},{5,7},{6,4},{7,5},{8,10},{9,11},{10,... | collective-permute-start | bytes 9224 | tf_op jit(solution)/shard_map/ppermute | solution.py:406
  597.4 5.7 collective-permute-start.18
  603.2 30.2 %collective-permute-start.25 = (f32[256,1024]{1,0:T(8,128)}, f32[256,1024]{1,0:T(8,128)}, u32[]{:S(2)}, u32[]{:S(2)}) collective-permute-start(f32[256,1024]{1,0:T(8,128)} %get-tuple-element.105), channel_id=1, source_target_pairs={{0,4},{1,5},{2,6},{3,7},{4,0},{5,1},{6,2},{7,3},{8,12},{9,13},{10,... | collective-permute-start | bytes 3145736 | tf_op jit(solution)/shard_map/ppermute | solution.py:406
  604.7 24.6 %collective-permute-start.19 = (f32[3,256]{1,0:T(4,128)S(1)}, f32[3,256]{1,0:T(4,128)S(1)}, u32[]{:S(2)}, u32[]{:S(2)}) collective-permute-start(f32[3,256]{1,0:T(4,128)S(1)} %get-tuple-element.115), channel_id=1, source_target_pairs={{0,4},{1,5},{2,6},{3,7},{4,0},{5,1},{6,2},{7,3},{8,12},{9,13},{10,... | collective-permute-start | bytes 9224 | tf_op jit(solution)/shard_map/ppermute | solution.py:406
  605.2 25.7 %collective-permute-start.20 = (f32[3,256]{1,0:T(4,128)S(1)}, f32[3,256]{1,0:T(4,128)S(1)}, u32[]{:S(2)}, u32[]{:S(2)}) collective-permute-start(f32[3,256]{1,0:T(4,128)S(1)} %get-tuple-element.114), channel_id=1, source_target_pairs={{0,5},{1,4},{2,7},{3,6},{4,1},{5,0},{6,3},{7,2},{8,13},{9,12},{10,... | collective-permute-start | bytes 9224 | tf_op jit(solution)/shard_map/ppermute | solution.py:406
  606.4 26.0 %collective-permute-start.21 = (f32[3,256]{1,0:T(4,128)S(1)}, f32[3,256]{1,0:T(4,128)S(1)}, u32[]{:S(2)}, u32[]{:S(2)}) collective-permute-start(f32[3,256]{1,0:T(4,128)S(1)} %get-tuple-element.113), channel_id=1, source_target_pairs={{0,6},{1,7},{2,4},{3,5},{4,2},{5,3},{6,0},{7,1},{8,14},{9,15},{10,... | collective-permute-start | bytes 9224 | tf_op jit(solution)/shard_map/ppermute | solution.py:406
  607.9 25.1 %collective-permute-start.22 = (f32[3,256]{1,0:T(4,128)S(1)}, f32[3,256]{1,0:T(4,128)S(1)}, u32[]{:S(2)}, u32[]{:S(2)}) collective-permute-start(f32[3,256]{1,0:T(4,128)S(1)} %get-tuple-element.112), channel_id=1, source_target_pairs={{0,7},{1,6},{2,5},{3,4},{4,3},{5,2},{6,1},{7,0},{8,15},{9,14},{10,... | collective-permute-start | bytes 9224 | tf_op jit(solution)/shard_map/ppermute | solution.py:406
  629.3 26.3 %collective-permute-start.26 = (f32[256,1024]{1,0:T(8,128)}, f32[256,1024]{1,0:T(8,128)}, u32[]{:S(2)}, u32[]{:S(2)}) collective-permute-start(f32[256,1024]{1,0:T(8,128)} %get-tuple-element.107), channel_id=1, source_target_pairs={{0,2},{1,3},{2,0},{3,1},{4,6},{5,7},{6,4},{7,5},{8,10},{9,11},{10,... | collective-permute-start | bytes 3145736 | tf_op jit(solution)/shard_map/ppermute | solution.py:406
  630.9 28.9 %collective-permute-start.23 = (f32[256,1024]{1,0:T(8,128)}, f32[256,1024]{1,0:T(8,128)}, u32[]{:S(2)}, u32[]{:S(2)}) collective-permute-start(f32[256,1024]{1,0:T(8,128)} %get-tuple-element.102), channel_id=1, source_target_pairs={{0,4},{1,5},{2,6},{3,7},{4,0},{5,1},{6,2},{7,3},{8,12},{9,13},{10,... | collective-permute-start | bytes 3145736 | tf_op jit(solution)/shard_map/ppermute | solution.py:406
  632.4 45.7 %collective-permute-start.24 = (f32[256,1024]{1,0:T(8,128)}, f32[256,1024]{1,0:T(8,128)}, u32[]{:S(2)}, u32[]{:S(2)}) collective-permute-start(f32[256,1024]{1,0:T(8,128)} %get-tuple-element.104), channel_id=1, source_target_pairs={{0,2},{1,3},{2,0},{3,1},{4,6},{5,7},{6,4},{7,5},{8,10},{9,11},{10,... | collective-permute-start | bytes 3145736 | tf_op jit(solution)/shard_map/ppermute | solution.py:406
  633.0 49.3 %collective-permute-start.27 = (f32[256,1024]{1,0:T(8,128)}, f32[256,1024]{1,0:T(8,128)}, u32[]{:S(2)}, u32[]{:S(2)}) collective-permute-start(f32[256,1024]{1,0:T(8,128)} %get-tuple-element.108), channel_id=1, source_target_pairs={{0,4},{1,5},{2,6},{3,7},{4,0},{5,1},{6,2},{7,3},{8,12},{9,13},{10,... | collective-permute-start | bytes 3145736 | tf_op jit(solution)/shard_map/ppermute | solution.py:406
  633.4 66.2 %collective-permute-start.28 = (f32[256,1024]{1,0:T(8,128)}, f32[256,1024]{1,0:T(8,128)}, u32[]{:S(2)}, u32[]{:S(2)}) collective-permute-start(f32[256,1024]{1,0:T(8,128)} %get-tuple-element.110), channel_id=1, source_target_pairs={{0,2},{1,3},{2,0},{3,1},{4,6},{5,7},{6,4},{7,5},{8,10},{9,11},{10,... | collective-permute-start | bytes 3145736 | tf_op jit(solution)/shard_map/ppermute | solution.py:406
  (6 other events, 99.1 us)

commit v2 on v1

--- a/solution.py
+++ b/solution.py
@@ -42,6 +42,8 @@
 N_BLK = 256
 MIB = 1024 * 1024
 VMEM_MIB = 63
+HEADS = 2
+WIDE = 512
 
 
 def bf_shape(*dims):
@@ -64,55 +66,125 @@
     return pl.BlockSpec(dims, lambda i: (0,) * len(dims), pipeline_mode=pl.Buffered(1))
 
 
-def qkv_kernel(x_ref, gain_ref, wq_ref, wk_ref, wv_ref, hid_ref, q_ref, k_ref, v_ref, qinv_ref, kinv_ref, qsum, ksum):
-    step = pl.program_id(0)
-    rows, width = x_ref.shape
-
-    @pl.when(step == 0)
-    def _():
-        @pl.loop(0, rows // 128)
-        def _(blk):
-            span = pl.ds(pl.multiple_of(blk * 128, 128), 128)
-            x_f = x_ref[span, :].astype(jnp.float32)
+def partner_of(me, off):
+    flipped = me
+    for bit in (1, 2, 4):
+        if off & bit:
+            flipped = flipped + bit - 2 * bit * ((me // bit) % 2)
+    return flipped
+
+
+def gather_qkv_kernel(x_ref, pos_ref, gain_ref, wq_ref, wk_ref, wv_ref, xs_ref, hid_ref, q_ref, k_ref, v_ref, qinv_ref, kinv_ref, pos_out,
+                      x_s, pos_s, wq_s, wk_s, wv_s, hid_s, q_s, k_s, v_s, send_sem, recv_sem, psend_sem, precv_sem, w_sem, own_sem, x_out_sem, out_sem):
+    n_sp, tok, width = x_ref.shape
+    me = lax.axis_index('sp')
+    pair = 2 * tok
+    barrier = pltpu.get_barrier_semaphore()
+    for off in range(1, n_sp):
+        pl.semaphore_signal(barrier, inc=1, device_id={'sp': partner_of(me, off)}, device_id_type=pl.DeviceIdType.MESH)
+    pl.semaphore_wait(barrier, n_sp - 1)
+
+    copies, pos_copies = [], []
+    for off in range(n_sp):
+        peer = partner_of(me, off)
+        if off == 0:
+            copies.append(pltpu.make_async_copy(x_ref.at[me], x_s.at[me], own_sem.at[0]))
+            pos_copies.append(pltpu.make_async_copy(pos_ref.at[me], pos_s.at[me], own_sem.at[1]))
+        else:
+            pos_copies.append(pltpu.make_async_remote_copy(
+                src_ref=pos_ref.at[peer], dst_ref=pos_s.at[me], send_sem=psend_sem.at[off], recv_sem=precv_sem.at[off],
+                device_id={'sp': peer}, device_id_type=pl.DeviceIdType.MESH))
+            copies.append(pltpu.make_async_remote_copy(
+                src_ref=x_ref.at[peer], dst_ref=x_s.at[me], send_sem=send_sem.at[off], recv_sem=recv_sem.at[off],
+                device_id={'sp': peer}, device_id_type=pl.DeviceIdType.MESH))
+        pos_copies[-1].start()
+        copies[-1].start()
+    loads = [pltpu.make_async_copy(src, dst, w_sem.at[i]) for i, (src, dst) in enumerate(((wq_ref, wq_s), (wk_ref, wk_s), (wv_ref, wv_s)))]
+    for load in loads:
+        load.start()
+
+    outs = []
+    for step in range(n_sp // 2):
+        slot = step % 2
+        chip = partner_of(me, 2 * step) // 2
+        if step == 0:
+            copies[0].wait()
+        else:
+            copies[2 * step].wait_recv()
+        copies[2 * step + 1].wait_recv()
+        rows = pl.ds(pl.multiple_of(chip * pair, pair), pair)
+        if step >= 2:
+            for out in outs[step - 2]:
+                out.wait()
+        for part in range(2):
+            x_f = x_s[2 * chip + part].astype(jnp.float32)
             inv_rms = lax.rsqrt(jnp.mean(x_f * x_f, axis=-1, keepdims=True) + NORM_EPS)
-            hid_ref[span, :] = (x_f * inv_rms * gain_ref[...].astype(jnp.float32)).astype(jnp.bfloat16)
-
-        qsum[...] = jnp.zeros_like(qsum)
-        ksum[...] = jnp.zeros_like(ksum)
-
-    for w_ref, out_ref, acc in ((wq_ref, q_ref, qsum), (wk_ref, k_ref, ksum)):
-        raw = mm(hid_ref[...], w_ref[...])
-        out_ref[...] = raw
-        for part in range(N_BLK // 128):
-            piece = raw[:, part * 128:(part + 1) * 128]
-            acc[...] += piece * piece
-    v_ref[...] = mm(hid_ref[...], wv_ref[...]).astype(jnp.bfloat16)
-
-    @pl.when(step == pl.num_programs(0) - 1)
-    def _():
-        for acc, inv_ref in ((qsum, qinv_ref), (ksum, kinv_ref)):
-            inv_ref[...] = lax.rsqrt(jnp.sum(acc[...], axis=-1, keepdims=True) * (1.0 / width) + NORM_EPS)
-
-
-def qkv_call(x_seq, gain, w_query, w_key, w_value):
-    rows, width = x_seq.shape
-    w_col = pl.BlockSpec((width, N_BLK), lambda i: (0, i))
-    o_col = pl.BlockSpec((rows, N_BLK), lambda i: (0, i))
-    return pl.pallas_call(
-        qkv_kernel, grid=(width // N_BLK,),
-        in_specs=[fixed(rows, width), fixed(1, width), w_col, w_col, w_col],
-        out_specs=[pl.BlockSpec((rows, width), lambda i: (0, 0)), o_col, o_col, o_col] + [pl.BlockSpec((rows, 1), lambda i: (0, 0))] * 2,
-        out_shape=[bf_shape(rows, width), f32_shape(rows, width), f32_shape(rows, width), bf_shape(rows, width), f32_shape(rows, 1), f32_shape(rows, 1)],
-        scratch_shapes=[pltpu.VMEM((rows, 128), jnp.float32)] * 2,
+            hid_s[slot, part * tok:(part + 1) * tok, :] = (x_f * inv_rms * gain_ref[...].astype(jnp.float32)).astype(jnp.bfloat16)
+        if step == 0:
+            for load in loads:
+                load.wait()
+
+        def columns(blk, sums):
+            cols = pl.ds(pl.multiple_of(blk * N_BLK, N_BLK), N_BLK)
+            hid = hid_s[slot]
+            new_sums = []
+            for w_s, dst, total in ((wq_s, q_s, sums[0]), (wk_s, k_s, sums[1])):
+                raw = mm(hid, w_s[:, cols])
+                dst[slot, :, cols] = raw
+                for lo in range(0, N_BLK, 128):
+                    total = total + raw[:, lo:lo + 128] * raw[:, lo:lo + 128]
+                new_sums.append(total)
+            v_s[slot, :, cols] = mm(hid, wv_s[:, cols]).astype(jnp.bfloat16)
+            return tuple(new_sums)
+
+        zero = jnp.zeros((pair, 128), jnp.float32)
+        sums = lax.fori_loop(0, width // N_BLK, columns, (zero, zero))
+        for total, inv_ref in zip(sums, (qinv_ref, kinv_ref)):
+            inv_ref[rows, :] = lax.rsqrt(jnp.sum(total, axis=-1, keepdims=True) * (1.0 / width) + NORM_EPS)
+        group = [pltpu.make_async_copy(src.at[slot], dst.at[rows], out_sem.at[slot, i])
+                 for i, (src, dst) in enumerate(((hid_s, hid_ref), (q_s, q_ref), (k_s, k_ref), (v_s, v_ref)))]
+        for part in range(2):
+            group.append(pltpu.make_async_copy(x_s.at[2 * chip + part], xs_ref.at[2 * chip + part], x_out_sem.at[2 * step + part]))
+        for out in group:
+            out.start()
+        outs.append(group)
+    for group in outs[-2:]:
+        for out in group:
+            out.wait()
+    pos_copies[0].wait()
+    for off in range(1, n_sp):
+        pos_copies[off].wait()
+        copies[off].wait_send()
+    pos_out[...] = pos_s[...]
+
+
+def gather_qkv_call(x_loc, positions, gain, w_query, w_key, w_value):
+    n_sp, tok, width = x_loc.shape
+    rows, pair = n_sp * tok, 2 * tok
+    hbm = pl.BlockSpec(memory_space=pltpu.HBM)
+    vmem = pl.BlockSpec(memory_space=pltpu.VMEM)
+    dma = pltpu.SemaphoreType.DMA
+    return pl.pallas_call(
+        gather_qkv_kernel,
+        in_specs=[hbm, hbm, vmem, hbm, hbm, hbm],
+        out_specs=[hbm] * 5 + [vmem] * 3,
+        out_shape=[bf_shape(n_sp, tok, width), bf_shape(rows, width), f32_shape(rows, width), f32_shape(rows, width), bf_shape(rows, width),
+                   f32_shape(rows, 1), f32_shape(rows, 1), jax.ShapeDtypeStruct((n_sp, 1, tok), jnp.int32)],
+        scratch_shapes=[
+            pltpu.VMEM((n_sp, tok, width), jnp.bfloat16), pltpu.VMEM((n_sp, 1, tok), jnp.int32)]
+        + [pltpu.VMEM((width, width), jnp.bfloat16)] * 3
+        + [pltpu.VMEM((2, pair, width), jnp.bfloat16), pltpu.VMEM((2, pair, width), jnp.float32), pltpu.VMEM((2, pair, width), jnp.float32), pltpu.VMEM((2, pair, width), jnp.bfloat16)]
+        + [dma((n_sp,)), dma((n_sp,)), dma((n_sp,)), dma((n_sp,)), dma((3,)), dma((2,)), dma((n_sp,)), dma((2, 4))],
         cost_estimate=cost(6 * rows * width * width, 6 * width * width + 14 * rows * width),
-        compiler_params=limit(48), name="qkv",
-    )(x_seq, gain.reshape(1, width), w_query, w_key, w_value)
-
-
-def rope_heads(q1_ref, k1_ref, qinv_ref, kinv_ref, gq_ref, gk_ref, cos_ref, sin_ref, q_s, k_s):
+        compiler_params=pltpu.CompilerParams(vmem_limit_bytes=VMEM_MIB * MIB, collective_id=0, has_side_effects=True),
+        name="gather_qkv",
+    )(x_loc, positions.reshape(n_sp, 1, tok), gain.reshape(1, width), w_query, w_key, w_value)
+
+
+def rope_heads(q1_ref, k1_ref, qinv_ref, kinv_ref, gq_ref, gk_ref, cos_ref, sin_ref, q_s, k_s, cols):
     cos_t, sin_t = cos_ref[...], sin_ref[...]
-    q_s[...] = rotate(q1_ref[...] * qinv_ref[...] * gq_ref[...].astype(jnp.float32), cos_t, sin_t).astype(jnp.bfloat16)
-    k_s[...] = rotate(k1_ref[...] * kinv_ref[...] * gk_ref[...].astype(jnp.float32), cos_t, sin_t).astype(jnp.bfloat16)
+    q_s[:, cols] = rotate(q1_ref[:, cols] * qinv_ref[...] * gq_ref[:, cols].astype(jnp.float32), cos_t, sin_t).astype(jnp.bfloat16)
+    k_s[:, cols] = rotate(k1_ref[:, cols] * kinv_ref[...] * gk_ref[:, cols].astype(jnp.float32), cos_t, sin_t).astype(jnp.bfloat16)
 
 
 def masked_scores(keys, q_blk, q_lo):
@@ -124,63 +196,71 @@
     return edge if q_lo == 0 else jnp.concatenate([scores[:q_lo, :], edge], axis=0)
 
 
+def head_cols(head):
+    return slice(head * HEAD_DIM, (head + 1) * HEAD_DIM)
+
+
 def attn_fwd_kernel(q1_ref, k1_ref, v_ref, qinv_ref, kinv_ref, gq_ref, gk_ref, cos_ref, sin_ref, a_ref, q_s, k_s, lse_ref):
     seq = q1_ref.shape[0]
-    rope_heads(q1_ref, k1_ref, qinv_ref, kinv_ref, gq_ref, gk_ref, cos_ref, sin_ref, q_s, k_s)
     to_log2 = HEAD_DIM ** -0.5 * LOG2E
-    v_t = v_ref[...].T
+    for head in range(HEADS):
+        rope_heads(q1_ref, k1_ref, qinv_ref, kinv_ref, gq_ref, gk_ref, cos_ref, sin_ref, q_s, k_s, head_cols(head))
+    v_t = [v_ref[:, head_cols(head)].T for head in range(HEADS)]
     for blk in range(seq // Q_BLK):
         q_lo, k_len = blk * Q_BLK, (blk + 1) * Q_BLK
-        scores = masked_scores(k_s[:k_len, :], q_s[q_lo:k_len, :], q_lo)
-        top = jnp.max(scores, axis=0, keepdims=True)
-        prob = jnp.exp2((scores - top) * to_log2)
-        total = jnp.sum(prob, axis=0, keepdims=True)
-        out_t = mm(v_t[:, :k_len], prob.astype(jnp.bfloat16)) * (1.0 / total)
-        a_ref[q_lo:k_len, :] = out_t.T.astype(jnp.bfloat16)
-        lse_ref[0, :, q_lo:k_len] = top * to_log2 + jnp.log2(total)
+        scores = [masked_scores(k_s[:k_len, head_cols(h)], q_s[q_lo:k_len, head_cols(h)], q_lo) for h in range(HEADS)]
+        for head in range(HEADS):
+            top = jnp.max(scores[head], axis=0, keepdims=True)
+            prob = jnp.exp2((scores[head] - top) * to_log2)
+            total = jnp.sum(prob, axis=0, keepdims=True)
+            out_t = mm(v_t[head][:, :k_len], prob.astype(jnp.bfloat16)) * (1.0 / total)
+            a_ref[q_lo:k_len, head_cols(head)] = out_t.T.astype(jnp.bfloat16)
+            lse_ref[head, :, q_lo:k_len] = top * to_log2 + jnp.log2(total)
 
 
 def attn_bwd_kernel(q_ref, k_ref, v_ref, do_ref, lse_ref, dep_ref, dq_ref, dk_ref, dv_ref, dk_s, dv_s):
     seq = q_ref.shape[0]
     scale = HEAD_DIM ** -0.5
-    k_t = k_ref[...].T
+    k_t = [k_ref[:, head_cols(head)].T for head in range(1)]
     n_blk = seq // Q_BLK
     for blk in reversed(range(n_blk)):
         q_lo, k_len = blk * Q_BLK, (blk + 1) * Q_BLK
-        q_blk = q_ref[q_lo:k_len, :]
-        do_blk = do_ref[q_lo:k_len, :]
-        scores = masked_scores(k_ref[:k_len, :], q_blk, q_lo)
-        prob = jnp.exp2(scores * (scale * LOG2E) - lse_ref[0, :, q_lo:k_len])
-        d_prob = mm_nt(v_ref[:k_len, :], do_blk)
-        row_dot = jnp.sum(prob * d_prob, axis=0, keepdims=True)
-        ds_bf = (prob * ((d_prob - row_dot) * scale)).astype(jnp.bfloat16)
-        dq_t = mm(k_t[:, :k_len], ds_bf)
-        dq_ref[q_lo:k_len, :] = dq_t.T.astype(jnp.bfloat16)
-        dv_part = mm(prob.astype(jnp.bfloat16), do_blk)
-        dk_part = mm(ds_bf, q_blk)
-        if blk == n_blk - 1:
-            dv_s[...] = dv_part
-            dk_s[...] = dk_part
-        else:
-            dv_s[:k_len, :] += dv_part
-            dk_s[:k_len, :] += dk_part
+        for head in range(1):
+            cols = head_cols(head)
+            q_blk = q_ref[q_lo:k_len, cols]
+            do_blk = do_ref[q_lo:k_len, cols]
+            scores = masked_scores(k_ref[:k_len, cols], q_blk, q_lo)
+            prob = jnp.exp2(scores * (scale * LOG2E) - lse_ref[head, :, q_lo:k_len])
+            d_prob = mm_nt(v_ref[:k_len, cols], do_blk)
+            row_dot = jnp.sum(prob * d_prob, axis=0, keepdims=True)
+            ds_bf = (prob * ((d_prob - row_dot) * scale)).astype(jnp.bfloat16)
+            dq_t = mm(k_t[head][:, :k_len], ds_bf)
+            dq_ref[q_lo:k_len, cols] = dq_t.T.astype(jnp.bfloat16)
+            dv_part = mm(prob.astype(jnp.bfloat16), do_blk)
+            dk_part = mm(ds_bf, q_blk)
+            if blk == n_blk - 1:
+                dv_s[:, cols] = dv_part
+                dk_s[:, cols] = dk_part
+            else:
+                dv_s[:k_len, cols] += dv_part
+                dk_s[:k_len, cols] += dk_part
     dv_ref[...] = dv_s[...].astype(jnp.bfloat16)
     dk_ref[...] = dk_s[...].astype(jnp.bfloat16)
 
 
-def attn_specs(seq):
-    head = pl.BlockSpec((seq, HEAD_DIM), lambda h: (0, h))
-    lse = pl.BlockSpec((1, 1, seq), lambda h: (h, 0, 0))
+def attn_specs(seq, heads):
+    head = pl.BlockSpec((seq, heads * HEAD_DIM), lambda h: (0, h))
+    lse = pl.BlockSpec((heads, 1, seq), lambda h: (h, 0, 0))
     return head, lse
 
 
 def attn_fwd_call(q_raw, k_raw, v_val, q_inv, k_inv, g_query, g_key, cos_t, sin_t):
     seq, width = q_raw.shape
     n_heads = width // HEAD_DIM
-    head, lse = attn_specs(seq)
-    gain = pl.BlockSpec((1, HEAD_DIM), lambda h: (0, h))
-    return pl.pallas_call(
-        attn_fwd_kernel, grid=(n_heads,),
+    head, lse = attn_specs(seq, HEADS)
+    gain = pl.BlockSpec((1, HEADS * HEAD_DIM), lambda h: (0, h))
+    return pl.pallas_call(
+        attn_fwd_kernel, grid=(n_heads // HEADS,),
         in_specs=[head, head, head, fixed(seq, 1), fixed(seq, 1), gain, gain, fixed(seq, HEAD_DIM), fixed(seq, HEAD_DIM)],
         out_specs=[head, head, head, lse],
         out_shape=[bf_shape(seq, width)] * 3 + [f32_shape(n_heads, 1, seq)],
@@ -192,7 +272,7 @@
 def attn_bwd_call(q_bf, k_bf, v_val, d_attn, lse_all, dep):
     seq, width = q_bf.shape
     n_heads = width // HEAD_DIM
-    head, lse = attn_specs(seq)
+    head, lse = attn_specs(seq, 1)
     return pl.pallas_call(
         attn_bwd_kernel, grid=(n_heads,),
         in_specs=[head, head, head, head, lse, ANY_SPEC],
@@ -209,10 +289,10 @@
 
 def out_call(attended, w_out, x_seq, dep):
     rows, width = x_seq.shape
-    o_col = pl.BlockSpec((rows, N_BLK), lambda i: (0, i))
-    return pl.pallas_call(
-        out_kernel, grid=(width // N_BLK,),
-        in_specs=[fixed(rows, width), pl.BlockSpec((width, N_BLK), lambda i: (0, i)), o_col, ANY_SPEC],
+    o_col = pl.BlockSpec((rows, WIDE), lambda i: (0, i))
+    return pl.pallas_call(
+        out_kernel, grid=(width // WIDE,),
+        in_specs=[fixed(rows, width), pl.BlockSpec((width, WIDE), lambda i: (0, i)), o_col, ANY_SPEC],
         out_specs=o_col, out_shape=bf_shape(rows, width),
         cost_estimate=cost(2 * rows * width * width, 2 * width * width + 6 * rows * width),
         compiler_params=limit(32), name="project_out",
@@ -226,9 +306,9 @@
 def head_grad_call(gy_seq, w_out, dep):
     rows, width = gy_seq.shape
     return pl.pallas_call(
-        head_grad_kernel, grid=(width // N_BLK,),
-        in_specs=[fixed(rows, width), pl.BlockSpec((N_BLK, width), lambda i: (i, 0)), ANY_SPEC],
-        out_specs=pl.BlockSpec((rows, N_BLK), lambda i: (0, i)), out_shape=bf_shape(rows, width),
+        head_grad_kernel, grid=(width // WIDE,),
+        in_specs=[fixed(rows, width), pl.BlockSpec((WIDE, width), lambda i: (i, 0)), ANY_SPEC],
+        out_specs=pl.BlockSpec((rows, WIDE), lambda i: (0, i)), out_shape=bf_shape(rows, width),
         cost_estimate=cost(2 * rows * width * width, 2 * width * width + 4 * rows * width),
         compiler_params=limit(32), name="head_grad",
     )(gy_seq, w_out, dep)
@@ -420,20 +500,21 @@
             stay_l, away_l, stay_r, away_r = parts
             return stay_l, flip(away_l, 4), stay_r, flip(away_r, 2)
 
-        cos_t, sin_t = rope_tables(swap(positions).reshape(seq))
-        x_seq = swap(x_loc).reshape(seq, width)
+        x_swap, hidden, q_raw, k_raw, v_val, q_inv, k_inv, pos_seq = gather_qkv_call(x_loc, positions, g_norm, w_query, w_key, w_value)
+        cos_t, sin_t = rope_tables(pos_seq.reshape(seq))
+        x_seq = x_swap.reshape(seq, width)
+        grad_y, _ = lax.optimization_barrier((grad_y, q_inv))
         gy_seq = swap(grad_y).reshape(seq, width)
-        hidden, q_raw, k_raw, v_val, q_inv, k_inv = qkv_call(x_seq, g_norm, w_query, w_key, w_value)
         attended, q_bf, k_bf, lse_all = attn_fwd_call(q_raw, k_raw, v_val, q_inv, k_inv, g_query, g_key, cos_t, sin_t)
         a_peer = flip(attended, 1)
         gy_peer = flip(gy_seq, 1)
         hid_peer = flip(hidden, 1)
         y_seq = out_call(attended, w_out, x_seq, attended)
         y_swap = swap(y_seq.reshape(n_batch, loc_len, width))
-        part_o = weight_call(idx, attended, a_peer, gy_seq, gy_peer, y_seq)
+        d_attn = head_grad_call(gy_seq, w_out, y_seq)
+        part_o = weight_call(idx, attended, a_peer, gy_seq, gy_peer, d_attn)
         hop_o = first_hop(part_o)
-        d_attn = head_grad_call(gy_seq, w_out, part_o[2])
-        dq_bf, dk_bf, dv_bf = attn_bwd_call(q_bf, k_bf, v_val, d_attn, lse_all, y_seq)
+        dq_bf, dk_bf, dv_bf = attn_bwd_call(q_bf, k_bf, v_val, d_attn, lse_all, part_o[2])
         dv_peer = flip(dv_bf, 1)
         mrg_o = merge_call(*hop_o, dv_bf)
         fin_o = second_hop(mrg_o)

time: 706 us -> 672 us (0.952)
  blocking collectives: 63.6 us -> 0 us
  waiting for transfers between devices: 245 us -> 262 us
  Pallas kernels: 348 us -> 363 us
    all_to_all x2 -> x0, blocking collectives: 63.6 us -> none  [the longest x1 53.5 us: block_step(): x_seq = swap(x_loc).reshape(seq, width)]
    all_to_all x1, waiting for transfers between devices: 0.01 us -> 15.5 us  [block_step(): gy_seq = swap(grad_y).reshape(seq, width)]
    pallas_call x4, Pallas kernels: 104 us -> 119 us  [the longest x1 63.2 us: gather_qkv_call(): pl.pallas_call(gather_qkv_kernel, in_specs=[hbm, hbm, vmem, hbm, hbm, hbm...]
  transfers between devices with their start and end apart: 32 -> 32, of which waited for: 9 -> 10; matrix products, arithmetic and copies ran while one was open for 1% -> 1% of each run, Pallas kernels for 45% -> 40%
where the time goes in v2:
time: 672 us; the launch traced here: 671 us
  Pallas kernels  363 us (54%)
  waiting for transfers between devices  262 us (39%)
  starting transfers between devices  38.3 us (6%)
    ppermute x29, waiting for transfers between devices, flip(): return lax.ppermute(values, 'sp', [(dev, dev ^ bit) for dev in range(n_sp)])  246 us
    pallas_call x4, Pallas kernels, weight_call(): pl.pallas_call(weight_kernel, grid_spec=pltpu.PrefetchScalarGridSpec(num_...  74.1 us
    pallas_call x1, Pallas kernels, gather_qkv_call(): pl.pallas_call(gather_qkv_kernel, in_specs=[hbm, hbm, vmem, hbm, hbm, hbm...  63.2 us
    pallas_call x1, Pallas kernels, attn_bwd_call(): pl.pallas_call(attn_bwd_kernel, grid=(n_heads,), in_specs=[head, head, he...  48 us
    pallas_call x1, Pallas kernels, hid_grad_call(): pl.pallas_call(hid_grad_kernel, grid=(width // N_BLK,), in_specs=[fixed(r...  34.7 us
    pallas_call x1, Pallas kernels, attn_fwd_call(): pl.pallas_call(attn_fwd_kernel, grid=(n_heads // HEADS,), in_specs=[head,...  28.6 us
    ppermute x29, starting transfers between devices, flip(): return lax.ppermute(values, 'sp', [(dev, dev ^ bit) for dev in range(n_sp)])  24 us
    pallas_call x4, Pallas kernels, merge_call(): pl.pallas_call(merge_kernel, grid=(rows // 64,), in_specs=[inp] * 4 + [AN...  22.9 us
  transfers between devices with their start and end apart: 32, of which 10 were waited for; matrix products, arithmetic and copies ran while one was open for 1% of the time, Pallas kernels for 40%

profile of v2, /device:TPU:0, one launch (start us, length us, event | category | flops | bytes accessed | tf_op | source)
XLA Modules:
  0.0 670.5 jit_solution(5328005147930417299)
XLA Ops:
  1.9 63.2 %gather_qkv.1 = (bf16[8,128,2048]{2,1,0:T(8,128)(2,1)}, bf16[1024,2048]{1,0:T(8,128)(2,1)}, f32[1024,2048]{1,0:T(8,128)}, f32[1024,2048]{1,0:T(8,128)}, bf16[102...) custom-call(bf16[8,128,2048]{2,1,0:T(8,128)(2,1)} %x_ref.1, ...), custom_call_target="tpu_custom_call" | custom-call | flops 25769803776 | bytes 54525952 | tf_op jit(solution)/shard_map/gather_qkv/pallas_call | solution.py:167
  65.2 4.8 all-to-all-start.1
  74.5 28.6 %attention_fwd.1 = (bf16[1024,2048]{1,0:T(8,128)(2,1)}, bf16[1024,2048]{1,0:T(8,128)(2,1)}, bf16[1024,2048]{1,0:T(8,128)(2,1)}, f32[16,1,1024]{2,1,0:T(1,128)}) custom-call(f32[1024,2048]{1,0:T(8,128)} %get-tuple-element.63.q1_ref.raw_ref, f32[1024,2048]{1,0:T(8,128)} %get-tuple-element.64.k1_ref.raw_ref, bf16[1024,2048]{1,0:T(8,128)(2,1)} %get-tuple-element.65.v_ref, ...), custom_call_target="tpu_custom_call" | custom-call | flops 8589934592 | bytes 33554432 | tf_op jit(solution)/shard_map/attention_fwd/pallas_call | solution.py:262
  103.4 15.5 %all-to-all-done.1 = bf16[8,128,2048]{2,1,0:T(8,128)(2,1)} async-done(((bf16[8,128,2048]{2,1,0:T(8,128)(2,1)}), bf16[8,128,2048]{2,1,0:T(8,128)(2,1)}, u32[]{:S(2)}, u32[]{:S(2)}) %all-to-all-start.1) | async-done | bytes 4194336 | tf_op jit(solution)/shard_map/all_to_all | solution.py:507
  119.9 13.6 %project_out.1.dep_ref = bf16[1024,2048]{1,0:T(8,128)(2,1)} custom-call(bf16[1024,2048]{1,0:T(8,128)(2,1)} %get-tuple-element.69.a_ref.dep_ref.la_ref, bf16[2048,2048]{1,0:T(8,128)(2,1)} %w_ref.3, bf16[1024,2048]{1,0:T(8,128)(2,1)} %bitcast.11, bf16[1024,2048]{1,0:T(8,128)(2,1)} %get-tuple-element.69.a_ref.dep_ref.la_ref), custom_call_target="tpu_custom_call" | custom-call | flops 8589934592 | bytes 20971520 | tf_op jit(solution)/shard_map/project_out/pallas_call | solution.py:293
  133.5 13.3 %head_grad.1.dep_ref.do_ref = bf16[1024,2048]{1,0:T(8,128)(2,1)} custom-call(bf16[1024,2048]{1,0:T(8,128)(2,1)} %bitcast.4.gy_ref.ra_ref, bf16[2048,2048]{1,0:T(8,128)(2,1)} %w_ref.3, bf16[1024,2048]{1,0:T(8,128)(2,1)} %project_out.1.dep_ref), custom_call_target="tpu_custom_call" | custom-call | flops 8589934592 | bytes 16777216 | tf_op jit(solution)/shard_map/head_grad/pallas_call | solution.py:308
  146.9 18.6 %weight_grad.4 = (f32[2,256,1024]{2,1,0:T(8,128)}, f32[2,256,1024]{2,1,0:T(8,128)}, f32[2,256,1024]{2,1,0:T(8,128)}, f32[2,256,1024]{2,1,0:T(8,128)}) custom-call(s32[4]{0:T(128)} %multiply_xor_fusion.idx_ref, bf16[1024,2048]{1,0:T(8,128)(2,1)} %get-tuple-element.69.a_ref.dep_ref.la_ref, bf16[1024,2048]{1,0:T(8,128)(2,1)} %collective-permute-done.1.lb_ref, ...), custom_call_target="tpu_custom_call" | custom-call | flops 8589934592 | bytes 33554432 | tf_op jit(solution)/shard_map/weight_grad/pallas_call | solution.py:396
  165.5 48.0 %attention_bwd.1 = (bf16[1024,2048]{1,0:T(8,128)(2,1)}, bf16[1024,2048]{1,0:T(8,128)(2,1)}, bf16[1024,2048]{1,0:T(8,128)(2,1)}) custom-call(bf16[1024,2048]{1,0:T(8,128)(2,1)} %get-tuple-element.72.q_ref, bf16[1024,2048]{1,0:T(8,128)(2,1)} %get-tuple-element.73.k_ref, bf16[1024,2048]{1,0:T(8,128)(2,1)} %get-tuple-element.65.v_ref, ...), custom_call_target="tpu_custom_call" | custom-call | flops 21474836480 | bytes 29360128 | tf_op jit(solution)/shard_map/attention_bwd/pallas_call | solution.py:276
  214.7 47.2 %collective-permute-done.4.rl_ref = f32[2,256,1024]{2,1,0:T(8,128)} collective-permute-done((f32[2,256,1024]{2,1,0:T(8,128)}, f32[2,256,1024]{2,1,0:T(8,128)}, u32[]{:S(2)}, u32[]{:S(2)}) %collective-permute-start.4) | collective-permute-done | bytes 2097184 | tf_op jit(solution)/shard_map/ppermute | solution.py:486
  262.1 5.7 merge.4
  267.8 18.6 %weight_grad.5 = (f32[2,256,1024]{2,1,0:T(8,128)}, f32[2,256,1024]{2,1,0:T(8,128)}, f32[2,256,1024]{2,1,0:T(8,128)}, f32[2,256,1024]{2,1,0:T(8,128)}) custom-call(s32[4]{0:T(128)} %multiply_xor_fusion.idx_ref, bf16[1024,2048]{1,0:T(8,128)(2,1)} %get-tuple-element.71.la_ref, bf16[1024,2048]{1,0:T(8,128)(2,1)} %collective-permute-done.lb_ref, ...), custom_call_target="tpu_custom_call" | custom-call | flops 8589934592 | bytes 33554432 | tf_op jit(solution)/shard_map/weight_grad/pallas_call | solution.py:396
  286.4 11.1 %unnorm.2 = (bf16[1024,2048]{1,0:T(8,128)(2,1)}, f32[1,2048]{1,0:T(1,128)}) custom-call(bf16[1024,2048]{1,0:T(8,128)(2,1)} %get-tuple-element.77.dq_ref, f32[1024,2048]{1,0:T(8,128)} %get-tuple-element.63.q1_ref.raw_ref, f32[1024,1]{1,0:T(8,128)} %get-tuple-element.66.qinv_ref.inv_ref, bf16[1,2048]{1,0:T(2,128)(2,1)} %reshape.60.gq_ref.gain_ref, ...), custom_call_target="tpu_custom_call" | custom-call | flops 25165824 | bytes 16777216 | tf_op jit(solution)/shard_map/unnorm/pallas_call | solution.py:470
  297.5 11.1 %unnorm.3 = (bf16[1024,2048]{1,0:T(8,128)(2,1)}, f32[1,2048]{1,0:T(1,128)}) custom-call(bf16[1024,2048]{1,0:T(8,128)(2,1)} %get-tuple-element.85.dq_ref, f32[1024,2048]{1,0:T(8,128)} %get-tuple-element.64.k1_ref.raw_ref, f32[1024,1]{1,0:T(8,128)} %get-tuple-element.67.kinv_ref.inv_ref, bf16[1,2048]{1,0:T(2,128)(2,1)} %reshape.61.gk_ref.gain_ref, ...), custom_call_target="tpu_custom_call" | custom-call | flops 25165824 | bytes 16777216 | tf_op jit(solution)/shard_map/unnorm/pallas_call | solution.py:470
  309.1 4.8 all-to-all-start
  318.0 18.5 %weight_grad.6 = (f32[2,256,1024]{2,1,0:T(8,128)}, f32[2,256,1024]{2,1,0:T(8,128)}, f32[2,256,1024]{2,1,0:T(8,128)}, f32[2,256,1024]{2,1,0:T(8,128)}) custom-call(s32[4]{0:T(128)} %multiply_xor_fusion.idx_ref, bf16[1024,2048]{1,0:T(8,128)(2,1)} %get-tuple-element.71.la_ref, bf16[1024,2048]{1,0:T(8,128)(2,1)} %collective-permute-done.lb_ref, ...), custom_call_target="tpu_custom_call" | custom-call | flops 8589934592 | bytes 33554432 | tf_op jit(solution)/shard_map/weight_grad/pallas_call | solution.py:396
  336.5 18.5 %weight_grad.7 = (f32[2,256,1024]{2,1,0:T(8,128)}, f32[2,256,1024]{2,1,0:T(8,128)}, f32[2,256,1024]{2,1,0:T(8,128)}, f32[2,256,1024]{2,1,0:T(8,128)}) custom-call(s32[4]{0:T(128)} %multiply_xor_fusion.idx_ref, bf16[1024,2048]{1,0:T(8,128)(2,1)} %get-tuple-element.71.la_ref, bf16[1024,2048]{1,0:T(8,128)(2,1)} %collective-permute-done.lb_ref, ...), custom_call_target="tpu_custom_call" | custom-call | flops 8589934592 | bytes 33554432 | tf_op jit(solution)/shard_map/weight_grad/pallas_call | solution.py:396
  355.0 34.7 %hidden_grad.1.dh_ref = f32[1024,2048]{1,0:T(8,128)} custom-call(bf16[1024,2048]{1,0:T(8,128)(2,1)} %get-tuple-element.84.dep_ref.ra_ref.dq_ref, bf16[1024,2048]{1,0:T(8,128)(2,1)} %get-tuple-element.86.dep_ref.ra_ref.dk_ref, bf16[1024,2048]{1,0:T(8,128)(2,1)} %get-tuple-element.78.dep_ref.ra_ref.dv_ref, bf16[2048,2048]{1,0:T(8,128)(2,1)} %wq_ref.3, ...), custom_call_target="tpu_custom_call" | custom-call | flops 25769803776 | bytes 46137344 | tf_op jit(solution)/shard_map/hidden_grad/pallas_call | solution.py:337
  389.6 12.5 %input_grad.1 = (bf16[1024,2048]{1,0:T(8,128)(2,1)}, f32[1,2048]{1,0:T(1,128)}) custom-call(f32[1024,2048]{1,0:T(8,128)} %hidden_grad.1.dh_ref, bf16[1024,2048]{1,0:T(8,128)(2,1)} %bitcast.12, bf16[1024,2048]{1,0:T(8,128)(2,1)} %bitcast.4.gy_ref.ra_ref, bf16[1,2048]{1,0:T(2,128)(2,1)} %reshape.59.gain_ref), custom_call_target="tpu_custom_call" | custom-call | flops 25165824 | bytes 20971520 | tf_op jit(solution)/shard_map/input_grad/pallas_call | solution.py:366
  402.2 4.7 all-to-all-start.2
  410.8 18.9 %collective-permute-done.10.rr_ref = f32[2,256,1024]{2,1,0:T(8,128)} collective-permute-done((f32[2,256,1024]{2,1,0:T(8,128)}, f32[2,256,1024]{2,1,0:T(8,128)}, u32[]{:S(2)}, u32[]{:S(2)}) %collective-permute-start.10) | collective-permute-done | bytes 2097184 | tf_op jit(solution)/shard_map/ppermute | solution.py:486
  432.8 131.4 %collective-permute-done.17 = f32[3,256]{1,0:T(4,128)S(1)} collective-permute-done((f32[3,256]{1,0:T(4,128)S(1)}, f32[3,256]{1,0:T(4,128)S(1)}, u32[]{:S(2)}, u32[]{:S(2)}) %collective-permute-start.17) | collective-permute-done | bytes 3104 | tf_op jit(solution)/shard_map/ppermute | solution.py:486
  564.2 5.7 merge.5
  575.9 5.8 merge.6
  581.6 6.6 store_rows.2.dep_ref
  588.2 5.7 merge.7
  606.5 6.6 store_rows.3.dep_ref
  613.1 9.4 %collective-permute-done.26.rr_ref = f32[256,1024]{1,0:T(8,128)} collective-permute-done((f32[256,1024]{1,0:T(8,128)}, f32[256,1024]{1,0:T(8,128)}, u32[]{:S(2)}, u32[]{:S(2)}) %collective-permute-start.26) | collective-permute-done | bytes 1048608 | tf_op jit(solution)/shard_map/ppermute | solution.py:486
  622.4 4.1 final_add.5.dep_ref
  626.6 18.3 %collective-permute-done.24.rr_ref = f32[256,1024]{1,0:T(8,128)} collective-permute-done((f32[256,1024]{1,0:T(8,128)}, f32[256,1024]{1,0:T(8,128)}, u32[]{:S(2)}, u32[]{:S(2)}) %collective-permute-start.24) | collective-permute-done | bytes 1048608 | tf_op jit(solution)/shard_map/ppermute | solution.py:486
  644.9 4.1 final_add.6.dep_ref
  649.1 17.3 %collective-permute-done.28.rr_ref = f32[256,1024]{1,0:T(8,128)} collective-permute-done((f32[256,1024]{1,0:T(8,128)}, f32[256,1024]{1,0:T(8,128)}, u32[]{:S(2)}, u32[]{:S(2)}) %collective-permute-start.28) | collective-permute-done | bytes 1048608 | tf_op jit(solution)/shard_map/ppermute | solution.py:486
  666.4 4.1 final_add.7
  (79 shorter events, 38.7 us)
Async XLA Ops:
  65.2 53.7 %all-to-all-start.1 = ((bf16[8,128,2048]{2,1,0:T(8,128)(2,1)}), bf16[8,128,2048]{2,1,0:T(8,128)(2,1)}, u32[]{:S(2)}, u32[]{:S(2)}) async-start(bf16[8,128,2048]{2,1,0:T(8,128)(2,1)} %param.12), calls=%async_computation.1 | async-start | bytes 8388608 | tf_op jit(solution)/shard_map/all_to_all | solution.py:507
  103.0 43.8 %collective-permute-start.1 = (bf16[1024,2048]{1,0:T(8,128)(2,1)}, bf16[1024,2048]{1,0:T(8,128)(2,1)}, u32[]{:S(2)}, u32[]{:S(2)}) collective-permute-start(bf16[1024,2048]{1,0:T(8,128)(2,1)} %get-tuple-element.69.a_ref.dep_ref.la_ref), channel_id=1, source_target_pairs={{0,1},{1,0},{2,3},{3,2},{4,5},{5,4},{6,7},{7,6},{8,9},{9,8},{10,11... | collective-permute-start | bytes 12582920 | tf_op jit(solution)/shard_map/ppermute | solution.py:486
  118.9 28.0 %collective-permute-start.2 = (bf16[1024,2048]{1,0:T(8,128)(2,1)}, bf16[1024,2048]{1,0:T(8,128)(2,1)}, u32[]{:S(2)}, u32[]{:S(2)}) collective-permute-start(bf16[1024,2048]{1,0:T(8,128)(2,1)} %bitcast.4.gy_ref.ra_ref), channel_id=1, source_target_pairs={{0,1},{1,0},{2,3},{3,2},{4,5},{5,4},{6,7},{7,6},{8,9},{9,8},{10,11... | collective-permute-start | bytes 12582920 | tf_op jit(solution)/shard_map/ppermute | solution.py:486
  118.9 148.9 %collective-permute-start = (bf16[1024,2048]{1,0:T(8,128)(2,1)}, bf16[1024,2048]{1,0:T(8,128)(2,1)}, u32[]{:S(2)}, u32[]{:S(2)}) collective-permute-start(bf16[1024,2048]{1,0:T(8,128)(2,1)} %get-tuple-element.71.la_ref), channel_id=1, source_target_pairs={{0,1},{1,0},{2,3},{3,2},{4,5},{5,4},{6,7},{7,6},{8,9},{9,8},{10,11... | collective-permute-start | bytes 12582920 | tf_op jit(solution)/shard_map/ppermute | solution.py:486
  213.5 54.3 %collective-permute-start.3 = (bf16[1024,2048]{1,0:T(8,128)(2,1)}, bf16[1024,2048]{1,0:T(8,128)(2,1)}, u32[]{:S(2)}, u32[]{:S(2)}) collective-permute-start(bf16[1024,2048]{1,0:T(8,128)(2,1)} %get-tuple-element.78.dep_ref.ra_ref.dv_ref), channel_id=1, source_target_pairs={{0,1},{1,0},{2,3},{3,2},{4,5},{5,4},{6,7},{7,6},{8,9},{9,8},{10,11... | collective-permute-start | bytes 12582920 | tf_op jit(solution)/shard_map/ppermute | solution.py:486
  213.5 48.4 %collective-permute-start.4 = (f32[2,256,1024]{2,1,0:T(8,128)}, f32[2,256,1024]{2,1,0:T(8,128)}, u32[]{:S(2)}, u32[]{:S(2)}) collective-permute-start(f32[2,256,1024]{2,1,0:T(8,128)} %get-tuple-element.79), channel_id=1, source_target_pairs={{0,2},{1,3},{2,0},{3,1},{4,6},{5,7},{6,4},{7,5},{8,10},{9,11},{10,... | collective-permute-start | bytes 6291464 | tf_op jit(solution)/shard_map/ppermute | solution.py:486
  214.1 48.0 %collective-permute-start.5 = (f32[2,256,1024]{2,1,0:T(8,128)}, f32[2,256,1024]{2,1,0:T(8,128)}, u32[]{:S(2)}, u32[]{:S(2)}) collective-permute-start(f32[2,256,1024]{2,1,0:T(8,128)} %get-tuple-element.81), channel_id=1, source_target_pairs={{0,4},{1,5},{2,6},{3,7},{4,0},{5,1},{6,2},{7,3},{8,12},{9,13},{10,... | collective-permute-start | bytes 6291464 | tf_op jit(solution)/shard_map/ppermute | solution.py:486
  297.5 20.1 %collective-permute-start.6 = (bf16[1024,2048]{1,0:T(8,128)(2,1)}, bf16[1024,2048]{1,0:T(8,128)(2,1)}, u32[]{:S(2)}, u32[]{:S(2)}) collective-permute-start(bf16[1024,2048]{1,0:T(8,128)(2,1)} %get-tuple-element.84.dep_ref.ra_ref.dq_ref), channel_id=1, source_target_pairs={{0,1},{1,0},{2,3},{3,2},{4,5},{5,4},{6,7},{7,6},{8,9},{9,8},{10,11... | collective-permute-start | bytes 12582920 | tf_op jit(solution)/shard_map/ppermute | solution.py:486
  308.6 27.9 %collective-permute-start.11 = (bf16[1024,2048]{1,0:T(8,128)(2,1)}, bf16[1024,2048]{1,0:T(8,128)(2,1)}, u32[]{:S(2)}, u32[]{:S(2)}) collective-permute-start(bf16[1024,2048]{1,0:T(8,128)(2,1)} %get-tuple-element.86.dep_ref.ra_ref.dk_ref), channel_id=1, source_target_pairs={{0,1},{1,0},{2,3},{3,2},{4,5},{5,4},{6,7},{7,6},{8,9},{9,8},{10,11... | collective-permute-start | bytes 12582920 | tf_op jit(solution)/shard_map/ppermute | solution.py:486
  309.1 93.0 %all-to-all-start = ((bf16[8,128,2048]{2,1,0:T(8,128)(2,1)}), bf16[8,128,2048]{2,1,0:T(8,128)(2,1)}, u32[]{:S(2)}, u32[]{:S(2)}) async-start(bf16[8,128,2048]{2,1,0:T(8,128)(2,1)} %bitcast.10), calls=%async_computation | async-start | bytes 8388608 | tf_op jit(solution)/shard_map/all_to_all | solution.py:513
  313.9 94.9 %collective-permute-start.12 = (f32[256,1024]{1,0:T(8,128)}, f32[256,1024]{1,0:T(8,128)}, u32[]{:S(2)}, u32[]{:S(2)}) collective-permute-start(f32[256,1024]{1,0:T(8,128)} %get-tuple-element.98), channel_id=1, source_target_pairs={{0,4},{1,5},{2,6},{3,7},{4,0},{5,1},{6,2},{7,3},{8,12},{9,13},{10,... | collective-permute-start | bytes 3145736 | tf_op jit(solution)/shard_map/ppermute | solution.py:486
  315.6 94.7 %collective-permute-start.13 = (f32[256,1024]{1,0:T(8,128)}, f32[256,1024]{1,0:T(8,128)}, u32[]{:S(2)}, u32[]{:S(2)}) collective-permute-start(f32[256,1024]{1,0:T(8,128)} %get-tuple-element.100), channel_id=1, source_target_pairs={{0,2},{1,3},{2,0},{3,1},{4,6},{5,7},{6,4},{7,5},{8,10},{9,11},{10,... | collective-permute-start | bytes 3145736 | tf_op jit(solution)/shard_map/ppermute | solution.py:486
  317.0 112.7 %collective-permute-start.10 = (f32[2,256,1024]{2,1,0:T(8,128)}, f32[2,256,1024]{2,1,0:T(8,128)}, u32[]{:S(2)}, u32[]{:S(2)}) collective-permute-start(f32[2,256,1024]{2,1,0:T(8,128)} %get-tuple-element.93), channel_id=1, source_target_pairs={{0,4},{1,5},{2,6},{3,7},{4,0},{5,1},{6,2},{7,3},{8,12},{9,13},{10,... | collective-permute-start | bytes 6291464 | tf_op jit(solution)/shard_map/ppermute | solution.py:486
  317.6 112.6 %collective-permute-start.9 = (f32[2,256,1024]{2,1,0:T(8,128)}, f32[2,256,1024]{2,1,0:T(8,128)}, u32[]{:S(2)}, u32[]{:S(2)}) collective-permute-start(f32[2,256,1024]{2,1,0:T(8,128)} %get-tuple-element.91), channel_id=1, source_target_pairs={{0,2},{1,3},{2,0},{3,1},{4,6},{5,7},{6,4},{7,5},{8,10},{9,11},{10,... | collective-permute-start | bytes 6291464 | tf_op jit(solution)/shard_map/ppermute | solution.py:486
  402.2 204.4 %all-to-all-start.2 = ((bf16[8,128,2048]{2,1,0:T(8,128)(2,1)}), bf16[8,128,2048]{2,1,0:T(8,128)(2,1)}, u32[]{:S(2)}, u32[]{:S(2)}) async-start(bf16[8,128,2048]{2,1,0:T(8,128)(2,1)} %bitcast.9), calls=%async_computation.2 | async-start | bytes 8388608 | tf_op jit(solution)/shard_map/all_to_all | solution.py:533
  406.9 164.6 %collective-permute-start.7 = (f32[2,256,1024]{2,1,0:T(8,128)}, f32[2,256,1024]{2,1,0:T(8,128)}, u32[]{:S(2)}, u32[]{:S(2)}) collective-permute-start(f32[2,256,1024]{2,1,0:T(8,128)} %get-tuple-element.88), channel_id=1, source_target_pairs={{0,2},{1,3},{2,0},{3,1},{4,6},{5,7},{6,4},{7,5},{8,10},{9,11},{10,... | collective-permute-start | bytes 6291464 | tf_op jit(solution)/shard_map/ppermute | solution.py:486
  408.8 163.2 %collective-permute-start.8 = (f32[2,256,1024]{2,1,0:T(8,128)}, f32[2,256,1024]{2,1,0:T(8,128)}, u32[]{:S(2)}, u32[]{:S(2)}) collective-permute-start(f32[2,256,1024]{2,1,0:T(8,128)} %get-tuple-element.90), channel_id=1, source_target_pairs={{0,4},{1,5},{2,6},{3,7},{4,0},{5,1},{6,2},{7,3},{8,12},{9,13},{10,... | collective-permute-start | bytes 6291464 | tf_op jit(solution)/shard_map/ppermute | solution.py:486
  410.3 162.9 %collective-permute-start.14 = (f32[2,256,1024]{2,1,0:T(8,128)}, f32[2,256,1024]{2,1,0:T(8,128)}, u32[]{:S(2)}, u32[]{:S(2)}) collective-permute-start(f32[2,256,1024]{2,1,0:T(8,128)} %get-tuple-element.101), channel_id=1, source_target_pairs={{0,2},{1,3},{2,0},{3,1},{4,6},{5,7},{6,4},{7,5},{8,10},{9,11},{10,... | collective-permute-start | bytes 6291464 | tf_op jit(solution)/shard_map/ppermute | solution.py:486
  429.8 144.9 %collective-permute-start.15 = (f32[2,256,1024]{2,1,0:T(8,128)}, f32[2,256,1024]{2,1,0:T(8,128)}, u32[]{:S(2)}, u32[]{:S(2)}) collective-permute-start(f32[2,256,1024]{2,1,0:T(8,128)} %get-tuple-element.103), channel_id=1, source_target_pairs={{0,4},{1,5},{2,6},{3,7},{4,0},{5,1},{6,2},{7,3},{8,12},{9,13},{10,... | collective-permute-start | bytes 6291464 | tf_op jit(solution)/shard_map/ppermute | solution.py:486
  430.2 1.2 collective-permute-start.16
  431.4 132.8 %collective-permute-start.17 = (f32[3,256]{1,0:T(4,128)S(1)}, f32[3,256]{1,0:T(4,128)S(1)}, u32[]{:S(2)}, u32[]{:S(2)}) collective-permute-start(f32[3,256]{1,0:T(4,128)S(1)} %get-tuple-element.123), channel_id=1, source_target_pairs={{0,2},{1,3},{2,0},{3,1},{4,6},{5,7},{6,4},{7,5},{8,10},{9,11},{10,... | collective-permute-start | bytes 9224 | tf_op jit(solution)/shard_map/ppermute | solution.py:486
  564.2 5.7 collective-permute-start.18
  569.9 30.2 %collective-permute-start.25 = (f32[256,1024]{1,0:T(8,128)}, f32[256,1024]{1,0:T(8,128)}, u32[]{:S(2)}, u32[]{:S(2)}) collective-permute-start(f32[256,1024]{1,0:T(8,128)} %get-tuple-element.111), channel_id=1, source_target_pairs={{0,4},{1,5},{2,6},{3,7},{4,0},{5,1},{6,2},{7,3},{8,12},{9,13},{10,... | collective-permute-start | bytes 3145736 | tf_op jit(solution)/shard_map/ppermute | solution.py:486
  571.5 24.6 %collective-permute-start.19 = (f32[3,256]{1,0:T(4,128)S(1)}, f32[3,256]{1,0:T(4,128)S(1)}, u32[]{:S(2)}, u32[]{:S(2)}) collective-permute-start(f32[3,256]{1,0:T(4,128)S(1)} %get-tuple-element.121), channel_id=1, source_target_pairs={{0,4},{1,5},{2,6},{3,7},{4,0},{5,1},{6,2},{7,3},{8,12},{9,13},{10,... | collective-permute-start | bytes 9224 | tf_op jit(solution)/shard_map/ppermute | solution.py:486
  572.0 25.7 %collective-permute-start.20 = (f32[3,256]{1,0:T(4,128)S(1)}, f32[3,256]{1,0:T(4,128)S(1)}, u32[]{:S(2)}, u32[]{:S(2)}) collective-permute-start(f32[3,256]{1,0:T(4,128)S(1)} %get-tuple-element.120), channel_id=1, source_target_pairs={{0,5},{1,4},{2,7},{3,6},{4,1},{5,0},{6,3},{7,2},{8,13},{9,12},{10,... | collective-permute-start | bytes 9224 | tf_op jit(solution)/shard_map/ppermute | solution.py:486
  573.2 26.0 %collective-permute-start.21 = (f32[3,256]{1,0:T(4,128)S(1)}, f32[3,256]{1,0:T(4,128)S(1)}, u32[]{:S(2)}, u32[]{:S(2)}) collective-permute-start(f32[3,256]{1,0:T(4,128)S(1)} %get-tuple-element.119), channel_id=1, source_target_pairs={{0,6},{1,7},{2,4},{3,5},{4,2},{5,3},{6,0},{7,1},{8,14},{9,15},{10,... | collective-permute-start | bytes 9224 | tf_op jit(solution)/shard_map/ppermute | solution.py:486
  574.7 25.1 %collective-permute-start.22 = (f32[3,256]{1,0:T(4,128)S(1)}, f32[3,256]{1,0:T(4,128)S(1)}, u32[]{:S(2)}, u32[]{:S(2)}) collective-permute-start(f32[3,256]{1,0:T(4,128)S(1)} %get-tuple-element.118), channel_id=1, source_target_pairs={{0,7},{1,6},{2,5},{3,4},{4,3},{5,2},{6,1},{7,0},{8,15},{9,14},{10,... | collective-permute-start | bytes 9224 | tf_op jit(solution)/shard_map/ppermute | solution.py:486
  596.1 26.3 %collective-permute-start.26 = (f32[256,1024]{1,0:T(8,128)}, f32[256,1024]{1,0:T(8,128)}, u32[]{:S(2)}, u32[]{:S(2)}) collective-permute-start(f32[256,1024]{1,0:T(8,128)} %get-tuple-element.113), channel_id=1, source_target_pairs={{0,2},{1,3},{2,0},{3,1},{4,6},{5,7},{6,4},{7,5},{8,10},{9,11},{10,... | collective-permute-start | bytes 3145736 | tf_op jit(solution)/shard_map/ppermute | solution.py:486
  597.7 28.9 %collective-permute-start.23 = (f32[256,1024]{1,0:T(8,128)}, f32[256,1024]{1,0:T(8,128)}, u32[]{:S(2)}, u32[]{:S(2)}) collective-permute-start(f32[256,1024]{1,0:T(8,128)} %get-tuple-element.108), channel_id=1, source_target_pairs={{0,4},{1,5},{2,6},{3,7},{4,0},{5,1},{6,2},{7,3},{8,12},{9,13},{10,... | collective-permute-start | bytes 3145736 | tf_op jit(solution)/shard_map/ppermute | solution.py:486
  599.2 45.7 %collective-permute-start.24 = (f32[256,1024]{1,0:T(8,128)}, f32[256,1024]{1,0:T(8,128)}, u32[]{:S(2)}, u32[]{:S(2)}) collective-permute-start(f32[256,1024]{1,0:T(8,128)} %get-tuple-element.110), channel_id=1, source_target_pairs={{0,2},{1,3},{2,0},{3,1},{4,6},{5,7},{6,4},{7,5},{8,10},{9,11},{10,... | collective-permute-start | bytes 3145736 | tf_op jit(solution)/shard_map/ppermute | solution.py:486
  599.8 49.3 %collective-permute-start.27 = (f32[256,1024]{1,0:T(8,128)}, f32[256,1024]{1,0:T(8,128)}, u32[]{:S(2)}, u32[]{:S(2)}) collective-permute-start(f32[256,1024]{1,0:T(8,128)} %get-tuple-element.114), channel_id=1, source_target_pairs={{0,4},{1,5},{2,6},{3,7},{4,0},{5,1},{6,2},{7,3},{8,12},{9,13},{10,... | collective-permute-start | bytes 3145736 | tf_op jit(solution)/shard_map/ppermute | solution.py:486
  600.2 66.2 %collective-permute-start.28 = (f32[256,1024]{1,0:T(8,128)}, f32[256,1024]{1,0:T(8,128)}, u32[]{:S(2)}, u32[]{:S(2)}) collective-permute-start(f32[256,1024]{1,0:T(8,128)} %get-tuple-element.116), channel_id=1, source_target_pairs={{0,2},{1,3},{2,0},{3,1},{4,6},{5,7},{6,4},{7,5},{8,10},{9,11},{10,... | collective-permute-start | bytes 3145736 | tf_op jit(solution)/shard_map/ppermute | solution.py:486
  (6 other events, 98.9 us)

commit v3 on v2

--- a/solution.py
+++ b/solution.py
@@ -124,30 +124,34 @@
             for load in loads:
                 load.wait()
 
+        early = [pltpu.make_async_copy(hid_s.at[slot], hid_ref.at[rows], out_sem.at[slot, 3])]
+        for part in range(2):
+            early.append(pltpu.make_async_copy(x_s.at[2 * chip + part], xs_ref.at[2 * chip + part], x_out_sem.at[2 * step + part]))
+        for out in early:
+            out.start()
+
         def columns(blk, sums):
-            cols = pl.ds(pl.multiple_of(blk * N_BLK, N_BLK), N_BLK)
+            cols = pl.ds(pl.multiple_of(blk * WIDE, WIDE), WIDE)
             hid = hid_s[slot]
             new_sums = []
             for w_s, dst, total in ((wq_s, q_s, sums[0]), (wk_s, k_s, sums[1])):
                 raw = mm(hid, w_s[:, cols])
                 dst[slot, :, cols] = raw
-                for lo in range(0, N_BLK, 128):
+                for lo in range(0, WIDE, 128):
                     total = total + raw[:, lo:lo + 128] * raw[:, lo:lo + 128]
                 new_sums.append(total)
             v_s[slot, :, cols] = mm(hid, wv_s[:, cols]).astype(jnp.bfloat16)
             return tuple(new_sums)
 
         zero = jnp.zeros((pair, 128), jnp.float32)
-        sums = lax.fori_loop(0, width // N_BLK, columns, (zero, zero))
+        sums = lax.fori_loop(0, width // WIDE, columns, (zero, zero))
         for total, inv_ref in zip(sums, (qinv_ref, kinv_ref)):
             inv_ref[rows, :] = lax.rsqrt(jnp.sum(total, axis=-1, keepdims=True) * (1.0 / width) + NORM_EPS)
-        group = [pltpu.make_async_copy(src.at[slot], dst.at[rows], out_sem.at[slot, i])
-                 for i, (src, dst) in enumerate(((hid_s, hid_ref), (q_s, q_ref), (k_s, k_ref), (v_s, v_ref)))]
-        for part in range(2):
-            group.append(pltpu.make_async_copy(x_s.at[2 * chip + part], xs_ref.at[2 * chip + part], x_out_sem.at[2 * step + part]))
-        for out in group:
+        late = [pltpu.make_async_copy(src.at[slot], dst.at[rows], out_sem.at[slot, i])
+                for i, (src, dst) in enumerate(((q_s, q_ref), (k_s, k_ref), (v_s, v_ref)))]
+        for out in late:
             out.start()
-        outs.append(group)
+        outs.append(early + late)
     for group in outs[-2:]:
         for out in group:
             out.wait()
@@ -306,9 +310,9 @@
 def head_grad_call(gy_seq, w_out, dep):
     rows, width = gy_seq.shape
     return pl.pallas_call(
-        head_grad_kernel, grid=(width // WIDE,),
-        in_specs=[fixed(rows, width), pl.BlockSpec((WIDE, width), lambda i: (i, 0)), ANY_SPEC],
-        out_specs=pl.BlockSpec((rows, WIDE), lambda i: (0, i)), out_shape=bf_shape(rows, width),
+        head_grad_kernel, grid=(width // N_BLK,),
+        in_specs=[fixed(rows, width), pl.BlockSpec((N_BLK, width), lambda i: (i, 0)), ANY_SPEC],
+        out_specs=pl.BlockSpec((rows, N_BLK), lambda i: (0, i)), out_shape=bf_shape(rows, width),
         cost_estimate=cost(2 * rows * width * width, 2 * width * width + 4 * rows * width),
         compiler_params=limit(32), name="head_grad",
     )(gy_seq, w_out, dep)

time: 672 us -> 672 us (level)
  no operation moved by 1% of the time
where the time goes in v3:
time: 672 us; the launch traced here: 670 us
  Pallas kernels  362 us (54%)
  waiting for transfers between devices  262 us (39%)
  starting transfers between devices  38.3 us (6%)
    ppermute x29, waiting for transfers between devices, flip(): return lax.ppermute(values, 'sp', [(dev, dev ^ bit) for dev in range(n_sp)])  246 us
    pallas_call x4, Pallas kernels, weight_call(): pl.pallas_call(weight_kernel, grid_spec=pltpu.PrefetchScalarGridSpec(num_...  74.1 us
    pallas_call x1, Pallas kernels, gather_qkv_call(): pl.pallas_call(gather_qkv_kernel, in_specs=[hbm, hbm, vmem, hbm, hbm, hbm...  61.5 us
    pallas_call x1, Pallas kernels, attn_bwd_call(): pl.pallas_call(attn_bwd_kernel, grid=(n_heads,), in_specs=[head, head, he...  48 us
    pallas_call x1, Pallas kernels, hid_grad_call(): pl.pallas_call(hid_grad_kernel, grid=(width // N_BLK,), in_specs=[fixed(r...  34.7 us
    pallas_call x1, Pallas kernels, attn_fwd_call(): pl.pallas_call(attn_fwd_kernel, grid=(n_heads // HEADS,), in_specs=[head,...  28.6 us
    ppermute x29, starting transfers between devices, flip(): return lax.ppermute(values, 'sp', [(dev, dev ^ bit) for dev in range(n_sp)])  24 us
    pallas_call x4, Pallas kernels, merge_call(): pl.pallas_call(merge_kernel, grid=(rows // 64,), in_specs=[inp] * 4 + [AN...  22.9 us
  transfers between devices with their start and end apart: 32, of which 10 were waited for; matrix products, arithmetic and copies ran while one was open for 1% of the time, Pallas kernels for 40%

profile of v3, /device:TPU:0, one launch (start us, length us, event | category | flops | bytes accessed | tf_op | source)
XLA Modules:
  0.0 669.6 jit_solution(10427285573125990129)
XLA Ops:
  1.9 61.5 %gather_qkv.1 = (bf16[8,128,2048]{2,1,0:T(8,128)(2,1)}, bf16[1024,2048]{1,0:T(8,128)(2,1)}, f32[1024,2048]{1,0:T(8,128)}, f32[1024,2048]{1,0:T(8,128)}, bf16[102...) custom-call(bf16[8,128,2048]{2,1,0:T(8,128)(2,1)} %x_ref.1, ...), custom_call_target="tpu_custom_call" | custom-call | flops 25769803776 | bytes 54525952 | tf_op jit(solution)/shard_map/gather_qkv/pallas_call | solution.py:171
  63.4 4.8 all-to-all-start.1
  72.7 28.6 %attention_fwd.1 = (bf16[1024,2048]{1,0:T(8,128)(2,1)}, bf16[1024,2048]{1,0:T(8,128)(2,1)}, bf16[1024,2048]{1,0:T(8,128)(2,1)}, f32[16,1,1024]{2,1,0:T(1,128)}) custom-call(f32[1024,2048]{1,0:T(8,128)} %get-tuple-element.63.q1_ref.raw_ref, f32[1024,2048]{1,0:T(8,128)} %get-tuple-element.64.k1_ref.raw_ref, bf16[1024,2048]{1,0:T(8,128)(2,1)} %get-tuple-element.65.v_ref, ...), custom_call_target="tpu_custom_call" | custom-call | flops 8589934592 | bytes 33554432 | tf_op jit(solution)/shard_map/attention_fwd/pallas_call | solution.py:266
  101.7 15.5 %all-to-all-done.1 = bf16[8,128,2048]{2,1,0:T(8,128)(2,1)} async-done(((bf16[8,128,2048]{2,1,0:T(8,128)(2,1)}), bf16[8,128,2048]{2,1,0:T(8,128)(2,1)}, u32[]{:S(2)}, u32[]{:S(2)}) %all-to-all-start.1) | async-done | bytes 4194336 | tf_op jit(solution)/shard_map/all_to_all | solution.py:511
  118.1 13.6 %project_out.1.dep_ref = bf16[1024,2048]{1,0:T(8,128)(2,1)} custom-call(bf16[1024,2048]{1,0:T(8,128)(2,1)} %get-tuple-element.69.a_ref.dep_ref.la_ref, bf16[2048,2048]{1,0:T(8,128)(2,1)} %w_ref.3, bf16[1024,2048]{1,0:T(8,128)(2,1)} %bitcast.11, bf16[1024,2048]{1,0:T(8,128)(2,1)} %get-tuple-element.69.a_ref.dep_ref.la_ref), custom_call_target="tpu_custom_call" | custom-call | flops 8589934592 | bytes 20971520 | tf_op jit(solution)/shard_map/project_out/pallas_call | solution.py:297
  131.8 14.2 %head_grad.1.dep_ref.do_ref = bf16[1024,2048]{1,0:T(8,128)(2,1)} custom-call(bf16[1024,2048]{1,0:T(8,128)(2,1)} %bitcast.4.gy_ref.ra_ref, bf16[2048,2048]{1,0:T(8,128)(2,1)} %w_ref.3, bf16[1024,2048]{1,0:T(8,128)(2,1)} %project_out.1.dep_ref), custom_call_target="tpu_custom_call" | custom-call | flops 8589934592 | bytes 16777216 | tf_op jit(solution)/shard_map/head_grad/pallas_call | solution.py:312
  145.9 18.6 %weight_grad.4 = (f32[2,256,1024]{2,1,0:T(8,128)}, f32[2,256,1024]{2,1,0:T(8,128)}, f32[2,256,1024]{2,1,0:T(8,128)}, f32[2,256,1024]{2,1,0:T(8,128)}) custom-call(s32[4]{0:T(128)} %multiply_xor_fusion.idx_ref, bf16[1024,2048]{1,0:T(8,128)(2,1)} %get-tuple-element.69.a_ref.dep_ref.la_ref, bf16[1024,2048]{1,0:T(8,128)(2,1)} %collective-permute-done.1.lb_ref, ...), custom_call_target="tpu_custom_call" | custom-call | flops 8589934592 | bytes 33554432 | tf_op jit(solution)/shard_map/weight_grad/pallas_call | solution.py:400
  164.5 48.0 %attention_bwd.1 = (bf16[1024,2048]{1,0:T(8,128)(2,1)}, bf16[1024,2048]{1,0:T(8,128)(2,1)}, bf16[1024,2048]{1,0:T(8,128)(2,1)}) custom-call(bf16[1024,2048]{1,0:T(8,128)(2,1)} %get-tuple-element.72.q_ref, bf16[1024,2048]{1,0:T(8,128)(2,1)} %get-tuple-element.73.k_ref, bf16[1024,2048]{1,0:T(8,128)(2,1)} %get-tuple-element.65.v_ref, ...), custom_call_target="tpu_custom_call" | custom-call | flops 21474836480 | bytes 29360128 | tf_op jit(solution)/shard_map/attention_bwd/pallas_call | solution.py:280
  213.7 47.2 %collective-permute-done.4.rl_ref = f32[2,256,1024]{2,1,0:T(8,128)} collective-permute-done((f32[2,256,1024]{2,1,0:T(8,128)}, f32[2,256,1024]{2,1,0:T(8,128)}, u32[]{:S(2)}, u32[]{:S(2)}) %collective-permute-start.4) | collective-permute-done | bytes 2097184 | tf_op jit(solution)/shard_map/ppermute | solution.py:490
  261.1 5.7 merge.4
  266.8 18.6 %weight_grad.5 = (f32[2,256,1024]{2,1,0:T(8,128)}, f32[2,256,1024]{2,1,0:T(8,128)}, f32[2,256,1024]{2,1,0:T(8,128)}, f32[2,256,1024]{2,1,0:T(8,128)}) custom-call(s32[4]{0:T(128)} %multiply_xor_fusion.idx_ref, bf16[1024,2048]{1,0:T(8,128)(2,1)} %get-tuple-element.71.la_ref, bf16[1024,2048]{1,0:T(8,128)(2,1)} %collective-permute-done.lb_ref, ...), custom_call_target="tpu_custom_call" | custom-call | flops 8589934592 | bytes 33554432 | tf_op jit(solution)/shard_map/weight_grad/pallas_call | solution.py:400
  285.4 11.1 %unnorm.2 = (bf16[1024,2048]{1,0:T(8,128)(2,1)}, f32[1,2048]{1,0:T(1,128)}) custom-call(bf16[1024,2048]{1,0:T(8,128)(2,1)} %get-tuple-element.77.dq_ref, f32[1024,2048]{1,0:T(8,128)} %get-tuple-element.63.q1_ref.raw_ref, f32[1024,1]{1,0:T(8,128)} %get-tuple-element.66.qinv_ref.inv_ref, bf16[1,2048]{1,0:T(2,128)(2,1)} %reshape.60.gq_ref.gain_ref, ...), custom_call_target="tpu_custom_call" | custom-call | flops 25165824 | bytes 16777216 | tf_op jit(solution)/shard_map/unnorm/pallas_call | solution.py:474
  296.5 11.1 %unnorm.3 = (bf16[1024,2048]{1,0:T(8,128)(2,1)}, f32[1,2048]{1,0:T(1,128)}) custom-call(bf16[1024,2048]{1,0:T(8,128)(2,1)} %get-tuple-element.85.dq_ref, f32[1024,2048]{1,0:T(8,128)} %get-tuple-element.64.k1_ref.raw_ref, f32[1024,1]{1,0:T(8,128)} %get-tuple-element.67.kinv_ref.inv_ref, bf16[1,2048]{1,0:T(2,128)(2,1)} %reshape.61.gk_ref.gain_ref, ...), custom_call_target="tpu_custom_call" | custom-call | flops 25165824 | bytes 16777216 | tf_op jit(solution)/shard_map/unnorm/pallas_call | solution.py:474
  308.1 4.8 all-to-all-start
  317.0 18.5 %weight_grad.6 = (f32[2,256,1024]{2,1,0:T(8,128)}, f32[2,256,1024]{2,1,0:T(8,128)}, f32[2,256,1024]{2,1,0:T(8,128)}, f32[2,256,1024]{2,1,0:T(8,128)}) custom-call(s32[4]{0:T(128)} %multiply_xor_fusion.idx_ref, bf16[1024,2048]{1,0:T(8,128)(2,1)} %get-tuple-element.71.la_ref, bf16[1024,2048]{1,0:T(8,128)(2,1)} %collective-permute-done.lb_ref, ...), custom_call_target="tpu_custom_call" | custom-call | flops 8589934592 | bytes 33554432 | tf_op jit(solution)/shard_map/weight_grad/pallas_call | solution.py:400
  335.6 18.5 %weight_grad.7 = (f32[2,256,1024]{2,1,0:T(8,128)}, f32[2,256,1024]{2,1,0:T(8,128)}, f32[2,256,1024]{2,1,0:T(8,128)}, f32[2,256,1024]{2,1,0:T(8,128)}) custom-call(s32[4]{0:T(128)} %multiply_xor_fusion.idx_ref, bf16[1024,2048]{1,0:T(8,128)(2,1)} %get-tuple-element.71.la_ref, bf16[1024,2048]{1,0:T(8,128)(2,1)} %collective-permute-done.lb_ref, ...), custom_call_target="tpu_custom_call" | custom-call | flops 8589934592 | bytes 33554432 | tf_op jit(solution)/shard_map/weight_grad/pallas_call | solution.py:400
  354.0 34.7 %hidden_grad.1.dh_ref = f32[1024,2048]{1,0:T(8,128)} custom-call(bf16[1024,2048]{1,0:T(8,128)(2,1)} %get-tuple-element.84.dep_ref.ra_ref.dq_ref, bf16[1024,2048]{1,0:T(8,128)(2,1)} %get-tuple-element.86.dep_ref.ra_ref.dk_ref, bf16[1024,2048]{1,0:T(8,128)(2,1)} %get-tuple-element.78.dep_ref.ra_ref.dv_ref, bf16[2048,2048]{1,0:T(8,128)(2,1)} %wq_ref.3, ...), custom_call_target="tpu_custom_call" | custom-call | flops 25769803776 | bytes 46137344 | tf_op jit(solution)/shard_map/hidden_grad/pallas_call | solution.py:341
  388.7 12.5 %input_grad.1 = (bf16[1024,2048]{1,0:T(8,128)(2,1)}, f32[1,2048]{1,0:T(1,128)}) custom-call(f32[1024,2048]{1,0:T(8,128)} %hidden_grad.1.dh_ref, bf16[1024,2048]{1,0:T(8,128)(2,1)} %bitcast.12, bf16[1024,2048]{1,0:T(8,128)(2,1)} %bitcast.4.gy_ref.ra_ref, bf16[1,2048]{1,0:T(2,128)(2,1)} %reshape.59.gain_ref), custom_call_target="tpu_custom_call" | custom-call | flops 25165824 | bytes 20971520 | tf_op jit(solution)/shard_map/input_grad/pallas_call | solution.py:370
  401.2 4.7 all-to-all-start.2
  409.9 18.9 %collective-permute-done.10.rr_ref = f32[2,256,1024]{2,1,0:T(8,128)} collective-permute-done((f32[2,256,1024]{2,1,0:T(8,128)}, f32[2,256,1024]{2,1,0:T(8,128)}, u32[]{:S(2)}, u32[]{:S(2)}) %collective-permute-start.10) | collective-permute-done | bytes 2097184 | tf_op jit(solution)/shard_map/ppermute | solution.py:490
  431.9 131.4 %collective-permute-done.17 = f32[3,256]{1,0:T(4,128)S(1)} collective-permute-done((f32[3,256]{1,0:T(4,128)S(1)}, f32[3,256]{1,0:T(4,128)S(1)}, u32[]{:S(2)}, u32[]{:S(2)}) %collective-permute-start.17) | collective-permute-done | bytes 3104 | tf_op jit(solution)/shard_map/ppermute | solution.py:490
  563.3 5.7 merge.5
  574.9 5.8 merge.6
  580.7 6.6 store_rows.2.dep_ref
  587.2 5.7 merge.7
  605.5 6.6 store_rows.3.dep_ref
  612.1 9.4 %collective-permute-done.26.rr_ref = f32[256,1024]{1,0:T(8,128)} collective-permute-done((f32[256,1024]{1,0:T(8,128)}, f32[256,1024]{1,0:T(8,128)}, u32[]{:S(2)}, u32[]{:S(2)}) %collective-permute-start.26) | collective-permute-done | bytes 1048608 | tf_op jit(solution)/shard_map/ppermute | solution.py:490
  621.5 4.1 final_add.5.dep_ref
  625.6 18.3 %collective-permute-done.24.rr_ref = f32[256,1024]{1,0:T(8,128)} collective-permute-done((f32[256,1024]{1,0:T(8,128)}, f32[256,1024]{1,0:T(8,128)}, u32[]{:S(2)}, u32[]{:S(2)}) %collective-permute-start.24) | collective-permute-done | bytes 1048608 | tf_op jit(solution)/shard_map/ppermute | solution.py:490
  644.0 4.1 final_add.6.dep_ref
  648.1 17.3 %collective-permute-done.28.rr_ref = f32[256,1024]{1,0:T(8,128)} collective-permute-done((f32[256,1024]{1,0:T(8,128)}, f32[256,1024]{1,0:T(8,128)}, u32[]{:S(2)}, u32[]{:S(2)}) %collective-permute-start.28) | collective-permute-done | bytes 1048608 | tf_op jit(solution)/shard_map/ppermute | solution.py:490
  665.4 4.1 final_add.7
  (79 shorter events, 38.7 us)
Async XLA Ops:
  63.4 53.7 %all-to-all-start.1 = ((bf16[8,128,2048]{2,1,0:T(8,128)(2,1)}), bf16[8,128,2048]{2,1,0:T(8,128)(2,1)}, u32[]{:S(2)}, u32[]{:S(2)}) async-start(bf16[8,128,2048]{2,1,0:T(8,128)(2,1)} %param.12), calls=%async_computation.1 | async-start | bytes 8388608 | tf_op jit(solution)/shard_map/all_to_all | solution.py:511
  101.3 44.7 %collective-permute-start.1 = (bf16[1024,2048]{1,0:T(8,128)(2,1)}, bf16[1024,2048]{1,0:T(8,128)(2,1)}, u32[]{:S(2)}, u32[]{:S(2)}) collective-permute-start(bf16[1024,2048]{1,0:T(8,128)(2,1)} %get-tuple-element.69.a_ref.dep_ref.la_ref), channel_id=1, source_target_pairs={{0,1},{1,0},{2,3},{3,2},{4,5},{5,4},{6,7},{7,6},{8,9},{9,8},{10,11... | collective-permute-start | bytes 12582920 | tf_op jit(solution)/shard_map/ppermute | solution.py:490
  117.1 28.8 %collective-permute-start.2 = (bf16[1024,2048]{1,0:T(8,128)(2,1)}, bf16[1024,2048]{1,0:T(8,128)(2,1)}, u32[]{:S(2)}, u32[]{:S(2)}) collective-permute-start(bf16[1024,2048]{1,0:T(8,128)(2,1)} %bitcast.4.gy_ref.ra_ref), channel_id=1, source_target_pairs={{0,1},{1,0},{2,3},{3,2},{4,5},{5,4},{6,7},{7,6},{8,9},{9,8},{10,11... | collective-permute-start | bytes 12582920 | tf_op jit(solution)/shard_map/ppermute | solution.py:490
  117.1 149.7 %collective-permute-start = (bf16[1024,2048]{1,0:T(8,128)(2,1)}, bf16[1024,2048]{1,0:T(8,128)(2,1)}, u32[]{:S(2)}, u32[]{:S(2)}) collective-permute-start(bf16[1024,2048]{1,0:T(8,128)(2,1)} %get-tuple-element.71.la_ref), channel_id=1, source_target_pairs={{0,1},{1,0},{2,3},{3,2},{4,5},{5,4},{6,7},{7,6},{8,9},{9,8},{10,11... | collective-permute-start | bytes 12582920 | tf_op jit(solution)/shard_map/ppermute | solution.py:490
  212.5 54.3 %collective-permute-start.3 = (bf16[1024,2048]{1,0:T(8,128)(2,1)}, bf16[1024,2048]{1,0:T(8,128)(2,1)}, u32[]{:S(2)}, u32[]{:S(2)}) collective-permute-start(bf16[1024,2048]{1,0:T(8,128)(2,1)} %get-tuple-element.78.dep_ref.ra_ref.dv_ref), channel_id=1, source_target_pairs={{0,1},{1,0},{2,3},{3,2},{4,5},{5,4},{6,7},{7,6},{8,9},{9,8},{10,11... | collective-permute-start | bytes 12582920 | tf_op jit(solution)/shard_map/ppermute | solution.py:490
  212.5 48.4 %collective-permute-start.4 = (f32[2,256,1024]{2,1,0:T(8,128)}, f32[2,256,1024]{2,1,0:T(8,128)}, u32[]{:S(2)}, u32[]{:S(2)}) collective-permute-start(f32[2,256,1024]{2,1,0:T(8,128)} %get-tuple-element.79), channel_id=1, source_target_pairs={{0,2},{1,3},{2,0},{3,1},{4,6},{5,7},{6,4},{7,5},{8,10},{9,11},{10,... | collective-permute-start | bytes 6291464 | tf_op jit(solution)/shard_map/ppermute | solution.py:490
  213.1 48.0 %collective-permute-start.5 = (f32[2,256,1024]{2,1,0:T(8,128)}, f32[2,256,1024]{2,1,0:T(8,128)}, u32[]{:S(2)}, u32[]{:S(2)}) collective-permute-start(f32[2,256,1024]{2,1,0:T(8,128)} %get-tuple-element.81), channel_id=1, source_target_pairs={{0,4},{1,5},{2,6},{3,7},{4,0},{5,1},{6,2},{7,3},{8,12},{9,13},{10,... | collective-permute-start | bytes 6291464 | tf_op jit(solution)/shard_map/ppermute | solution.py:490
  296.5 20.1 %collective-permute-start.6 = (bf16[1024,2048]{1,0:T(8,128)(2,1)}, bf16[1024,2048]{1,0:T(8,128)(2,1)}, u32[]{:S(2)}, u32[]{:S(2)}) collective-permute-start(bf16[1024,2048]{1,0:T(8,128)(2,1)} %get-tuple-element.84.dep_ref.ra_ref.dq_ref), channel_id=1, source_target_pairs={{0,1},{1,0},{2,3},{3,2},{4,5},{5,4},{6,7},{7,6},{8,9},{9,8},{10,11... | collective-permute-start | bytes 12582920 | tf_op jit(solution)/shard_map/ppermute | solution.py:490
  307.6 27.9 %collective-permute-start.11 = (bf16[1024,2048]{1,0:T(8,128)(2,1)}, bf16[1024,2048]{1,0:T(8,128)(2,1)}, u32[]{:S(2)}, u32[]{:S(2)}) collective-permute-start(bf16[1024,2048]{1,0:T(8,128)(2,1)} %get-tuple-element.86.dep_ref.ra_ref.dk_ref), channel_id=1, source_target_pairs={{0,1},{1,0},{2,3},{3,2},{4,5},{5,4},{6,7},{7,6},{8,9},{9,8},{10,11... | collective-permute-start | bytes 12582920 | tf_op jit(solution)/shard_map/ppermute | solution.py:490
  308.1 93.0 %all-to-all-start = ((bf16[8,128,2048]{2,1,0:T(8,128)(2,1)}), bf16[8,128,2048]{2,1,0:T(8,128)(2,1)}, u32[]{:S(2)}, u32[]{:S(2)}) async-start(bf16[8,128,2048]{2,1,0:T(8,128)(2,1)} %bitcast.10), calls=%async_computation | async-start | bytes 8388608 | tf_op jit(solution)/shard_map/all_to_all | solution.py:517
  312.9 94.9 %collective-permute-start.12 = (f32[256,1024]{1,0:T(8,128)}, f32[256,1024]{1,0:T(8,128)}, u32[]{:S(2)}, u32[]{:S(2)}) collective-permute-start(f32[256,1024]{1,0:T(8,128)} %get-tuple-element.98), channel_id=1, source_target_pairs={{0,4},{1,5},{2,6},{3,7},{4,0},{5,1},{6,2},{7,3},{8,12},{9,13},{10,... | collective-permute-start | bytes 3145736 | tf_op jit(solution)/shard_map/ppermute | solution.py:490
  314.6 94.7 %collective-permute-start.13 = (f32[256,1024]{1,0:T(8,128)}, f32[256,1024]{1,0:T(8,128)}, u32[]{:S(2)}, u32[]{:S(2)}) collective-permute-start(f32[256,1024]{1,0:T(8,128)} %get-tuple-element.100), channel_id=1, source_target_pairs={{0,2},{1,3},{2,0},{3,1},{4,6},{5,7},{6,4},{7,5},{8,10},{9,11},{10,... | collective-permute-start | bytes 3145736 | tf_op jit(solution)/shard_map/ppermute | solution.py:490
  316.1 112.7 %collective-permute-start.10 = (f32[2,256,1024]{2,1,0:T(8,128)}, f32[2,256,1024]{2,1,0:T(8,128)}, u32[]{:S(2)}, u32[]{:S(2)}) collective-permute-start(f32[2,256,1024]{2,1,0:T(8,128)} %get-tuple-element.93), channel_id=1, source_target_pairs={{0,4},{1,5},{2,6},{3,7},{4,0},{5,1},{6,2},{7,3},{8,12},{9,13},{10,... | collective-permute-start | bytes 6291464 | tf_op jit(solution)/shard_map/ppermute | solution.py:490
  316.6 112.6 %collective-permute-start.9 = (f32[2,256,1024]{2,1,0:T(8,128)}, f32[2,256,1024]{2,1,0:T(8,128)}, u32[]{:S(2)}, u32[]{:S(2)}) collective-permute-start(f32[2,256,1024]{2,1,0:T(8,128)} %get-tuple-element.91), channel_id=1, source_target_pairs={{0,2},{1,3},{2,0},{3,1},{4,6},{5,7},{6,4},{7,5},{8,10},{9,11},{10,... | collective-permute-start | bytes 6291464 | tf_op jit(solution)/shard_map/ppermute | solution.py:490
  401.2 204.4 %all-to-all-start.2 = ((bf16[8,128,2048]{2,1,0:T(8,128)(2,1)}), bf16[8,128,2048]{2,1,0:T(8,128)(2,1)}, u32[]{:S(2)}, u32[]{:S(2)}) async-start(bf16[8,128,2048]{2,1,0:T(8,128)(2,1)} %bitcast.9), calls=%async_computation.2 | async-start | bytes 8388608 | tf_op jit(solution)/shard_map/all_to_all | solution.py:537
  405.9 164.6 %collective-permute-start.7 = (f32[2,256,1024]{2,1,0:T(8,128)}, f32[2,256,1024]{2,1,0:T(8,128)}, u32[]{:S(2)}, u32[]{:S(2)}) collective-permute-start(f32[2,256,1024]{2,1,0:T(8,128)} %get-tuple-element.88), channel_id=1, source_target_pairs={{0,2},{1,3},{2,0},{3,1},{4,6},{5,7},{6,4},{7,5},{8,10},{9,11},{10,... | collective-permute-start | bytes 6291464 | tf_op jit(solution)/shard_map/ppermute | solution.py:490
  407.8 163.2 %collective-permute-start.8 = (f32[2,256,1024]{2,1,0:T(8,128)}, f32[2,256,1024]{2,1,0:T(8,128)}, u32[]{:S(2)}, u32[]{:S(2)}) collective-permute-start(f32[2,256,1024]{2,1,0:T(8,128)} %get-tuple-element.90), channel_id=1, source_target_pairs={{0,4},{1,5},{2,6},{3,7},{4,0},{5,1},{6,2},{7,3},{8,12},{9,13},{10,... | collective-permute-start | bytes 6291464 | tf_op jit(solution)/shard_map/ppermute | solution.py:490
  409.3 162.9 %collective-permute-start.14 = (f32[2,256,1024]{2,1,0:T(8,128)}, f32[2,256,1024]{2,1,0:T(8,128)}, u32[]{:S(2)}, u32[]{:S(2)}) collective-permute-start(f32[2,256,1024]{2,1,0:T(8,128)} %get-tuple-element.101), channel_id=1, source_target_pairs={{0,2},{1,3},{2,0},{3,1},{4,6},{5,7},{6,4},{7,5},{8,10},{9,11},{10,... | collective-permute-start | bytes 6291464 | tf_op jit(solution)/shard_map/ppermute | solution.py:490
  428.8 144.9 %collective-permute-start.15 = (f32[2,256,1024]{2,1,0:T(8,128)}, f32[2,256,1024]{2,1,0:T(8,128)}, u32[]{:S(2)}, u32[]{:S(2)}) collective-permute-start(f32[2,256,1024]{2,1,0:T(8,128)} %get-tuple-element.103), channel_id=1, source_target_pairs={{0,4},{1,5},{2,6},{3,7},{4,0},{5,1},{6,2},{7,3},{8,12},{9,13},{10,... | collective-permute-start | bytes 6291464 | tf_op jit(solution)/shard_map/ppermute | solution.py:490
  429.2 1.2 collective-permute-start.16
  430.4 132.8 %collective-permute-start.17 = (f32[3,256]{1,0:T(4,128)S(1)}, f32[3,256]{1,0:T(4,128)S(1)}, u32[]{:S(2)}, u32[]{:S(2)}) collective-permute-start(f32[3,256]{1,0:T(4,128)S(1)} %get-tuple-element.123), channel_id=1, source_target_pairs={{0,2},{1,3},{2,0},{3,1},{4,6},{5,7},{6,4},{7,5},{8,10},{9,11},{10,... | collective-permute-start | bytes 9224 | tf_op jit(solution)/shard_map/ppermute | solution.py:490
  563.3 5.7 collective-permute-start.18
  569.0 30.2 %collective-permute-start.25 = (f32[256,1024]{1,0:T(8,128)}, f32[256,1024]{1,0:T(8,128)}, u32[]{:S(2)}, u32[]{:S(2)}) collective-permute-start(f32[256,1024]{1,0:T(8,128)} %get-tuple-element.111), channel_id=1, source_target_pairs={{0,4},{1,5},{2,6},{3,7},{4,0},{5,1},{6,2},{7,3},{8,12},{9,13},{10,... | collective-permute-start | bytes 3145736 | tf_op jit(solution)/shard_map/ppermute | solution.py:490
  570.5 24.6 %collective-permute-start.19 = (f32[3,256]{1,0:T(4,128)S(1)}, f32[3,256]{1,0:T(4,128)S(1)}, u32[]{:S(2)}, u32[]{:S(2)}) collective-permute-start(f32[3,256]{1,0:T(4,128)S(1)} %get-tuple-element.121), channel_id=1, source_target_pairs={{0,4},{1,5},{2,6},{3,7},{4,0},{5,1},{6,2},{7,3},{8,12},{9,13},{10,... | collective-permute-start | bytes 9224 | tf_op jit(solution)/shard_map/ppermute | solution.py:490
  571.1 25.7 %collective-permute-start.20 = (f32[3,256]{1,0:T(4,128)S(1)}, f32[3,256]{1,0:T(4,128)S(1)}, u32[]{:S(2)}, u32[]{:S(2)}) collective-permute-start(f32[3,256]{1,0:T(4,128)S(1)} %get-tuple-element.120), channel_id=1, source_target_pairs={{0,5},{1,4},{2,7},{3,6},{4,1},{5,0},{6,3},{7,2},{8,13},{9,12},{10,... | collective-permute-start | bytes 9224 | tf_op jit(solution)/shard_map/ppermute | solution.py:490
  572.2 26.0 %collective-permute-start.21 = (f32[3,256]{1,0:T(4,128)S(1)}, f32[3,256]{1,0:T(4,128)S(1)}, u32[]{:S(2)}, u32[]{:S(2)}) collective-permute-start(f32[3,256]{1,0:T(4,128)S(1)} %get-tuple-element.119), channel_id=1, source_target_pairs={{0,6},{1,7},{2,4},{3,5},{4,2},{5,3},{6,0},{7,1},{8,14},{9,15},{10,... | collective-permute-start | bytes 9224 | tf_op jit(solution)/shard_map/ppermute | solution.py:490
  573.7 25.1 %collective-permute-start.22 = (f32[3,256]{1,0:T(4,128)S(1)}, f32[3,256]{1,0:T(4,128)S(1)}, u32[]{:S(2)}, u32[]{:S(2)}) collective-permute-start(f32[3,256]{1,0:T(4,128)S(1)} %get-tuple-element.118), channel_id=1, source_target_pairs={{0,7},{1,6},{2,5},{3,4},{4,3},{5,2},{6,1},{7,0},{8,15},{9,14},{10,... | collective-permute-start | bytes 9224 | tf_op jit(solution)/shard_map/ppermute | solution.py:490
  595.1 26.3 %collective-permute-start.26 = (f32[256,1024]{1,0:T(8,128)}, f32[256,1024]{1,0:T(8,128)}, u32[]{:S(2)}, u32[]{:S(2)}) collective-permute-start(f32[256,1024]{1,0:T(8,128)} %get-tuple-element.113), channel_id=1, source_target_pairs={{0,2},{1,3},{2,0},{3,1},{4,6},{5,7},{6,4},{7,5},{8,10},{9,11},{10,... | collective-permute-start | bytes 3145736 | tf_op jit(solution)/shard_map/ppermute | solution.py:490
  596.7 28.9 %collective-permute-start.23 = (f32[256,1024]{1,0:T(8,128)}, f32[256,1024]{1,0:T(8,128)}, u32[]{:S(2)}, u32[]{:S(2)}) collective-permute-start(f32[256,1024]{1,0:T(8,128)} %get-tuple-element.108), channel_id=1, source_target_pairs={{0,4},{1,5},{2,6},{3,7},{4,0},{5,1},{6,2},{7,3},{8,12},{9,13},{10,... | collective-permute-start | bytes 3145736 | tf_op jit(solution)/shard_map/ppermute | solution.py:490
  598.2 45.7 %collective-permute-start.24 = (f32[256,1024]{1,0:T(8,128)}, f32[256,1024]{1,0:T(8,128)}, u32[]{:S(2)}, u32[]{:S(2)}) collective-permute-start(f32[256,1024]{1,0:T(8,128)} %get-tuple-element.110), channel_id=1, source_target_pairs={{0,2},{1,3},{2,0},{3,1},{4,6},{5,7},{6,4},{7,5},{8,10},{9,11},{10,... | collective-permute-start | bytes 3145736 | tf_op jit(solution)/shard_map/ppermute | solution.py:490
  598.8 49.3 %collective-permute-start.27 = (f32[256,1024]{1,0:T(8,128)}, f32[256,1024]{1,0:T(8,128)}, u32[]{:S(2)}, u32[]{:S(2)}) collective-permute-start(f32[256,1024]{1,0:T(8,128)} %get-tuple-element.114), channel_id=1, source_target_pairs={{0,4},{1,5},{2,6},{3,7},{4,0},{5,1},{6,2},{7,3},{8,12},{9,13},{10,... | collective-permute-start | bytes 3145736 | tf_op jit(solution)/shard_map/ppermute | solution.py:490
  599.2 66.2 %collective-permute-start.28 = (f32[256,1024]{1,0:T(8,128)}, f32[256,1024]{1,0:T(8,128)}, u32[]{:S(2)}, u32[]{:S(2)}) collective-permute-start(f32[256,1024]{1,0:T(8,128)} %get-tuple-element.116), channel_id=1, source_target_pairs={{0,2},{1,3},{2,0},{3,1},{4,6},{5,7},{6,4},{7,5},{8,10},{9,11},{10,... | collective-permute-start | bytes 3145736 | tf_op jit(solution)/shard_map/ppermute | solution.py:490
  (6 other events, 98.9 us)
